TPU v7x, 32 devices: a whole 2x2x4 slice. The times are simulated.
32 devices in a mesh: dp: 8 (over z, x), mp: 4 (over y, core).
Axes of the slice: x: 2, y: 2, z: 4, core: 2. Of those that a mesh axis runs over, the one named last changes fastest.
Arguments:
- tokens: bfloat16 [8, 196, 1280], P('dp'), may hold values from -6 to 6
- pad_mask: int32 [8, 196], P('dp'), may hold values from 0 to 1, as said below
- cotangent: bfloat16 [8, 196, 1280], P('dp'), may hold values from -6 to 6
- norm_gains: float32 [2, 1280], replicated, may hold values from 0.5 to 1.5
- norm_biases: float32 [2, 1280], replicated, may hold values from -2 to 2
- out_biases: float32 [2, 1280], replicated, may hold values from -2 to 2
- qkv_bias: float32 [3840], P('mp'), may hold values from -2 to 2
- up_bias: float32 [5120], P('mp'), may hold values from -2 to 2
- rel_pos: float32 [2, 27, 80], replicated, may hold values from -0.6 to 0.6
- attn_owner: int32 [4, 64], P('mp'), may hold values from 0 to 63, as said below
- mlp_owner: int32 [4, 128], P('mp'), may hold values from 0 to 127, as said below
- attn_master: float32 [4, 64, 25600], P('mp', 'dp')
- mlp_master: float32 [4, 128, 25600], P('mp', 'dp')
- attn_left: float32 [4, 64, 25600], P('mp', 'dp'), may hold values from -0.5 to 0.5
- attn_right: float32 [4, 64, 25600], P('mp', 'dp'), may hold values from -0.5 to 0.5
- mlp_left: float32 [4, 128, 25600], P('mp', 'dp'), may hold values from -0.5 to 0.5
- mlp_right: float32 [4, 128, 25600], P('mp', 'dp'), may hold values from -0.5 to 0.5
- attn_first: float32 [4, 64, 25600], P('mp', 'dp')
- attn_second: float32 [4, 64, 25600], P('mp', 'dp'), as said below
- mlp_first: float32 [4, 128, 25600], P('mp', 'dp')
- mlp_second: float32 [4, 128, 25600], P('mp', 'dp'), as said below
Outputs:
- block_output: bfloat16 [8, 196, 1280], P('dp')
- tokens_grad: float32 [8, 196, 1280], P('dp')
- gains_grad: float32 [2, 1280], replicated
- biases_grad: float32 [2, 1280], replicated
- out_biases_grad: float32 [2, 1280], replicated
- qkv_bias_grad: float32 [3840], P('mp')
- up_bias_grad: float32 [5120], P('mp')
- rel_pos_grad: float32 [2, 27, 80], replicated
- attn_grad: float32 [4, 64, 25600], P('mp', 'dp')
- mlp_grad: float32 [4, 128, 25600], P('mp', 'dp')
- attn_new: float32 [4, 64, 25600], P('mp', 'dp')
- mlp_new: float32 [4, 128, 25600], P('mp', 'dp')
- attn_copy: bfloat16 [4, 64, 25600], P('mp', 'dp')
- mlp_copy: bfloat16 [4, 128, 25600], P('mp', 'dp')
- attn_first_new: float32 [4, 64, 25600], P('mp', 'dp')
- attn_second_new: float32 [4, 64, 25600], P('mp', 'dp')
- mlp_first_new: float32 [4, 128, 25600], P('mp', 'dp')
- mlp_second_new: float32 [4, 128, 25600], P('mp', 'dp')
Inputs may be any that keep to these rules, and one draw needn't show every extreme that they name: `pad_mask`: slot s holds window s mod (25) of image s // 25, windows row-major in a 5 x 5 grid of 14 x 14 tokens, tokens row-major; slots of images from 1 on are all 0; in each image the 1 entries form a 64 x 64 square at an offset of 0 to 6 rows and columns. `attn_owner`: each row is a permutation of 0 to 63. `mlp_owner`: each row is a permutation of 0 to 127. `attn_second`: every entry is positive. `mlp_second`: every entry is positive.
All inputs are finite; a program needn't handle non-finite values.
Results may differ from a plain program's by a relative error of at most 0.017.
Values may be sent and summed in bfloat16 or wider, within the bound.
A program may use at most 192 MiB of HBM per device.

v0:
```python
import math

import jax
import jax.numpy as jnp
from jax import lax
from jax.sharding import PartitionSpec as P

highest = lax.Precision.HIGHEST
norm_eps = 1e-06
beta_one = 0.9
beta_two = 0.95
adam_eps = 1e-08
learn_rate = 0.02


def untile(tile_rows, row_count, col_count, tile_side):
    shaped = tile_rows.reshape(row_count // tile_side, col_count // tile_side, tile_side, tile_side)
    return shaped.transpose(0, 2, 1, 3).reshape(row_count, col_count)


def retile(matrix, tile_side):
    row_count, col_count = matrix.shape
    shaped = matrix.reshape(row_count // tile_side, tile_side, col_count // tile_side, tile_side)
    return shaped.transpose(0, 2, 1, 3).reshape(-1, tile_side * tile_side)


def rel_onehot(win_side):
    positions = jnp.arange(win_side, dtype=jnp.int32)
    offset = positions[:, None] - positions[None, :] + (win_side - 1)
    entries = jnp.arange(2 * win_side - 1, dtype=jnp.int32)
    return (offset[:, :, None] == entries[None, None, :]).astype(jnp.float32)


def norm_forward(values, norm_gain, norm_shift):
    centre = values - jnp.mean(values, axis=-1, keepdims=True)
    inverse = lax.rsqrt(jnp.mean(centre * centre, axis=-1, keepdims=True) + norm_eps)
    unit_rows = centre * inverse
    return (unit_rows * norm_gain + norm_shift, unit_rows, inverse)


def norm_backward(grad_in, unit_rows, inverse, norm_gain):
    grad_unit = grad_in * norm_gain
    centred = grad_unit - jnp.mean(grad_unit, axis=-1, keepdims=True)
    return inverse * (centred - unit_rows * jnp.mean(grad_unit * unit_rows, axis=-1, keepdims=True))


def gelu_pair(values):
    normal_cdf = 0.5 * (1.0 + lax.erf(values * 0.5**0.5))
    density = jnp.exp(-0.5 * values * values) * (2.0 * math.pi) ** (-0.5)
    return (values * normal_cdf, normal_cdf + values * density)


def soap_step(grad_tiles, master, left_basis, right_basis, first_moment, second_moment):
    tile_side = math.isqrt(grad_tiles.shape[2])
    square = (grad_tiles.shape[0], grad_tiles.shape[1], tile_side, tile_side)
    left_square = left_basis.reshape(square)
    right_square = right_basis.reshape(square)
    half_turn = jnp.einsum(
        "mtji,mtjk->mtik", left_square, grad_tiles.reshape(square), precision=highest
    )
    rotated = jnp.einsum("mtik,mtkl->mtil", half_turn, right_square, precision=highest).reshape(
        grad_tiles.shape
    )
    first_new = beta_one * first_moment + (1.0 - beta_one) * rotated
    second_new = beta_two * second_moment + (1.0 - beta_two) * rotated * rotated
    direction = (first_new / (jnp.sqrt(second_new) + adam_eps)).reshape(square)
    back_half = jnp.einsum("mtij,mtjk->mtik", left_square, direction, precision=highest)
    update = jnp.einsum("mtik,mtlk->mtil", back_half, right_square, precision=highest).reshape(
        grad_tiles.shape
    )
    master_new = master - learn_rate * update
    return (master_new, master_new.astype(jnp.bfloat16), first_new, second_new)


def local(
    tokens,
    pad_mask,
    cotangent,
    norm_gains,
    norm_biases,
    out_biases,
    qkv_bias,
    up_bias,
    rel_pos,
    attn_owner,
    mlp_owner,
    attn_master,
    mlp_master,
    attn_left,
    attn_right,
    mlp_left,
    mlp_right,
    attn_first,
    attn_second,
    mlp_first,
    mlp_second,
):
    windows, win_tokens, model_width = tokens.shape
    row_count = windows * win_tokens
    qkv_cols = qkv_bias.shape[0]
    head_cols = qkv_cols // 3
    unit_cols = up_bias.shape[0]
    head_dim = rel_pos.shape[2]
    heads_here = head_cols // head_dim
    win_side = (rel_pos.shape[1] + 1) // 2
    tile_side = math.isqrt(attn_master.shape[2])
    qkv_count = model_width // tile_side * (qkv_cols // tile_side)
    up_count = model_width // tile_side * (unit_cols // tile_side)
    score_scale = head_dim ** (-0.5)
    attn_stored, mlp_stored = (
        lax.all_gather(attn_master.astype(jnp.bfloat16), "dp", axis=1, tiled=True),
        lax.all_gather(mlp_master.astype(jnp.bfloat16), "dp", axis=1, tiled=True),
    )
    attn_order = jnp.argsort(attn_owner[0])
    mlp_order = jnp.argsort(mlp_owner[0])
    attn_sorted = attn_stored[0][attn_order]
    mlp_sorted = mlp_stored[0][mlp_order]
    w_qkv = untile(attn_sorted[:qkv_count], model_width, qkv_cols, tile_side)
    w_proj = untile(attn_sorted[qkv_count:], head_cols, model_width, tile_side)
    w_up = untile(mlp_sorted[:up_count], model_width, unit_cols, tile_side)
    w_down = untile(mlp_sorted[up_count:], unit_cols, model_width, tile_side)
    onehot = rel_onehot(win_side)
    table_h = jnp.einsum("ijr,rc->ijc", onehot, rel_pos[0], precision=highest)
    table_w = jnp.einsum("ijr,rc->ijc", onehot, rel_pos[1], precision=highest)
    flat_rows = tokens.reshape(row_count, model_width).astype(jnp.float32)
    live_rows = pad_mask.reshape(row_count, 1).astype(jnp.float32)
    normed, unit_one, inverse_one = norm_forward(flat_rows, norm_gains[0], norm_biases[0])
    normed_low = (normed * live_rows).astype(jnp.bfloat16)
    mixed_rows = (jnp.dot(normed_low, w_qkv, preferred_element_type=jnp.float32) + qkv_bias).astype(
        jnp.bfloat16
    )
    head_parts = mixed_rows.reshape(windows, win_tokens, 3, heads_here, head_dim)
    queries = head_parts[:, :, 0]
    key_rows = head_parts[:, :, 1]
    value_rows = head_parts[:, :, 2]
    query_grid = queries.astype(jnp.float32).reshape(
        windows, win_side, win_side, heads_here, head_dim
    )

    def score_rows():
        direct = (
            jnp.einsum("wqhc,wkhc->whqk", queries, key_rows, preferred_element_type=jnp.float32)
            * score_scale
        )
        along_h = jnp.einsum("wabhc,akc->whabk", query_grid, table_h, precision=highest)
        along_w = jnp.einsum("wabhc,blc->whabl", query_grid, table_w, precision=highest)
        return direct + (along_h[..., :, None] + along_w[..., None, :]).reshape(
            windows, heads_here, win_tokens, win_tokens
        )

    scores = score_rows()
    row_top = jnp.max(scores, axis=-1, keepdims=True)
    exponent = jnp.exp(scores - row_top)
    row_total = jnp.sum(exponent, axis=-1, keepdims=True)
    log_total = row_top + jnp.log(row_total)
    probs_low = (exponent / row_total).astype(jnp.bfloat16)
    attended = jnp.einsum(
        "whqk,wkhc->wqhc", probs_low, value_rows, preferred_element_type=jnp.float32
    )
    attended_low = attended.reshape(row_count, head_cols).astype(jnp.bfloat16)
    branch = lax.psum(
        jnp.dot(attended_low, w_proj, preferred_element_type=jnp.float32).astype(jnp.bfloat16), "mp"
    ).astype(jnp.float32)
    middle = flat_rows + branch + out_biases[0]
    second, unit_two, inverse_two = norm_forward(middle, norm_gains[1], norm_biases[1])
    second_low = second.astype(jnp.bfloat16)
    hidden = jnp.dot(second_low, w_up, preferred_element_type=jnp.float32) + up_bias
    active, gelu_slope = gelu_pair(hidden)
    active_low = active.astype(jnp.bfloat16)
    down_sum = lax.psum(
        jnp.dot(active_low, w_down, preferred_element_type=jnp.float32).astype(jnp.bfloat16), "mp"
    ).astype(jnp.float32)
    block_output = (
        ((middle + down_sum + out_biases[1]) * live_rows)
        .astype(jnp.bfloat16)
        .reshape(windows, win_tokens, model_width)
    )
    grad_out = cotangent.reshape(row_count, model_width).astype(jnp.float32) * live_rows
    grad_out_low = grad_out.astype(jnp.bfloat16)
    down_bias_grad = jnp.sum(grad_out, axis=0)
    w_down_grad = jnp.einsum(
        "nf,nd->fd", active_low, grad_out_low, preferred_element_type=jnp.float32
    )
    grad_active = jnp.einsum("nd,fd->nf", grad_out_low, w_down, preferred_element_type=jnp.float32)
    grad_hidden = (grad_active * gelu_slope).astype(jnp.bfloat16)
    up_bias_grad = jnp.sum(grad_hidden.astype(jnp.float32), axis=0)
    w_up_grad = jnp.einsum("nd,nf->df", second_low, grad_hidden, preferred_element_type=jnp.float32)
    mlp_stack = jnp.concatenate(
        [retile(w_up_grad, tile_side), retile(w_down_grad, tile_side)], axis=0
    )[mlp_owner[0]][None]
    grad_second = lax.psum(
        jnp.einsum("nf,df->nd", grad_hidden, w_up, preferred_element_type=jnp.float32).astype(
            jnp.bfloat16
        ),
        "mp",
    ).astype(jnp.float32)
    gain_two_grad = jnp.sum(grad_second * unit_two, axis=0)
    shift_two_grad = jnp.sum(grad_second, axis=0)
    grad_middle = grad_out + norm_backward(grad_second, unit_two, inverse_two, norm_gains[1])
    proj_bias_grad = jnp.sum(grad_middle, axis=0)
    grad_branch = grad_middle.astype(jnp.bfloat16)
    w_proj_grad = jnp.einsum(
        "nc,nd->cd", attended_low, grad_branch, preferred_element_type=jnp.float32
    )
    grad_attended = jnp.einsum("nd,cd->nc", grad_branch, w_proj, preferred_element_type=jnp.float32)
    grad_attended = grad_attended.astype(jnp.bfloat16).reshape(
        windows, win_tokens, heads_here, head_dim
    )
    probs_full = jnp.exp(score_rows() - log_total)
    probs_again = probs_full.astype(jnp.bfloat16)
    grad_probs = jnp.einsum(
        "wqhc,wkhc->whqk", grad_attended, value_rows, preferred_element_type=jnp.float32
    )
    grad_values = jnp.einsum(
        "whqk,wqhc->wkhc", probs_again, grad_attended, preferred_element_type=jnp.float32
    )
    grad_scores = (
        probs_full * (grad_probs - jnp.sum(probs_full * grad_probs, axis=-1, keepdims=True))
    ).astype(jnp.bfloat16)
    grad_queries = (
        jnp.einsum("whqk,wkhc->wqhc", grad_scores, key_rows, preferred_element_type=jnp.float32)
        * score_scale
    )
    grad_keys = (
        jnp.einsum("whqk,wqhc->wkhc", grad_scores, queries, preferred_element_type=jnp.float32)
        * score_scale
    )
    grad_grid = grad_scores.astype(jnp.float32).reshape(
        windows, heads_here, win_side, win_side, win_side, win_side
    )
    grad_h = jnp.sum(grad_grid, axis=5)
    grad_w = jnp.sum(grad_grid, axis=4)
    grad_rel_q = jnp.einsum("whabk,akc->wabhc", grad_h, table_h, precision=highest) + jnp.einsum(
        "whabl,blc->wabhc", grad_w, table_w, precision=highest
    )
    grad_queries = grad_queries + grad_rel_q.reshape(windows, win_tokens, heads_here, head_dim)
    table_h_grad = jnp.einsum("whabk,wabhc->akc", grad_h, query_grid, precision=highest)
    table_w_grad = jnp.einsum("whabl,wabhc->blc", grad_w, query_grid, precision=highest)
    rel_part = jnp.stack(
        [
            jnp.einsum("ijr,ijc->rc", onehot, table_h_grad, precision=highest),
            jnp.einsum("ijr,ijc->rc", onehot, table_w_grad, precision=highest),
        ]
    )
    grad_mixed = (
        jnp.stack([grad_queries, grad_keys, grad_values], axis=2)
        .reshape(row_count, qkv_cols)
        .astype(jnp.bfloat16)
    )
    qkv_bias_grad = jnp.sum(grad_mixed.astype(jnp.float32), axis=0)
    w_qkv_grad = jnp.einsum("nd,nc->dc", normed_low, grad_mixed, preferred_element_type=jnp.float32)
    grad_normed, rel_sum = (
        lax.psum(
            jnp.einsum("nc,dc->nd", grad_mixed, w_qkv, preferred_element_type=jnp.float32).astype(
                jnp.bfloat16
            ),
            "mp",
        ).astype(jnp.float32),
        lax.psum(rel_part.astype(jnp.bfloat16), "mp").astype(jnp.float32),
    )
    grad_normed = grad_normed * live_rows
    gain_one_grad = jnp.sum(grad_normed * unit_one, axis=0)
    shift_one_grad = jnp.sum(grad_normed, axis=0)
    tokens_grad = (
        grad_middle + norm_backward(grad_normed, unit_one, inverse_one, norm_gains[0])
    ).reshape(windows, win_tokens, model_width)
    attn_stack = jnp.concatenate(
        [retile(w_qkv_grad, tile_side), retile(w_proj_grad, tile_side)], axis=0
    )[attn_owner[0]][None]
    attn_grad, mlp_grad = (
        lax.psum_scatter(attn_stack, "dp", scatter_dimension=1, tiled=True),
        lax.psum_scatter(mlp_stack, "dp", scatter_dimension=1, tiled=True),
    )
    gains_grad, biases_grad, out_biases_grad, rel_pos_grad, qkv_bias_total, up_bias_total = (
        lax.psum(
            (
                jnp.stack([gain_one_grad, gain_two_grad]),
                jnp.stack([shift_one_grad, shift_two_grad]),
                jnp.stack([proj_bias_grad, down_bias_grad]),
                rel_sum,
                qkv_bias_grad,
                up_bias_grad,
            ),
            "dp",
        )
    )
    attn_new, attn_copy, attn_first_new, attn_second_new = soap_step(
        attn_grad, attn_master, attn_left, attn_right, attn_first, attn_second
    )
    mlp_new, mlp_copy, mlp_first_new, mlp_second_new = soap_step(
        mlp_grad, mlp_master, mlp_left, mlp_right, mlp_first, mlp_second
    )
    return (
        block_output,
        tokens_grad,
        gains_grad,
        biases_grad,
        out_biases_grad,
        qkv_bias_total,
        up_bias_total,
        rel_pos_grad,
        attn_grad,
        mlp_grad,
        attn_new,
        mlp_new,
        attn_copy,
        mlp_copy,
        attn_first_new,
        attn_second_new,
        mlp_first_new,
        mlp_second_new,
    )


def solution(mesh):
    placed = (
        P("dp", None, None),
        P("dp", None),
        P("dp", None, None),
        P(),
        P(),
        P(),
        P("mp"),
        P("mp"),
        P(),
        P("mp", None),
        P("mp", None),
        P("mp", "dp", None),
        P("mp", "dp", None),
        P("mp", "dp", None),
        P("mp", "dp", None),
        P("mp", "dp", None),
        P("mp", "dp", None),
        P("mp", "dp", None),
        P("mp", "dp", None),
        P("mp", "dp", None),
        P("mp", "dp", None),
    )
    return jax.shard_map(
        local,
        mesh=mesh,
        in_specs=placed,
        out_specs=(
            P("dp", None, None),
            P("dp", None, None),
            P(),
            P(),
            P(),
            P("mp"),
            P("mp"),
            P(),
            P("mp", "dp", None),
            P("mp", "dp", None),
            P("mp", "dp", None),
            P("mp", "dp", None),
            P("mp", "dp", None),
            P("mp", "dp", None),
            P("mp", "dp", None),
            P("mp", "dp", None),
            P("mp", "dp", None),
            P("mp", "dp", None),
        ),
        check_vma=False,
    )
```

profile of v0, /device:TPU:0, one launch (start us, length us, event | category | flops | bytes accessed | tf_op | source)
XLA Modules:
  0.0 885.5 jit_solution(16054658435756151305)
XLA Ops:
  17.7 57.3 %all-gather.3.cloned.1.call-done = bf16[1,64,25600]{2,1,0:T(8,128)(2,1)} async-done(((bf16[1,8,25600]{2,1,0:T(8,128)(2,1)}), bf16[1,64,25600]{2,1,0:T(8,128)(2,1)}) %all-gather.3.cloned.1.call-update) | async-done | bytes 3276816 | tf_op jit(solution)/shard_map/all_gather | solution.py:111
  75.0 9.5 %gather_fusion = bf16[64,25600]{1,0:T(8,128)(2,1)} fusion(bf16[64,25600]{1,0:T(8,128)(2,1)} %bitcast.343, s32[1024]{0:T(1024)S(1)} %pad_clamp_fusion.3), kind=kCustom, calls=%fused_computation | custom fusion | bytes 6553856 | tf_op jit(solution)/shard_map/gather | solution.py:116
  86.2 6.1 reshape.646
  92.3 7.0 copy.92
  99.3 6.1 reshape.647
  140.3 26.7 %all-reduce.6.cloned.1.call-done = bf16[196,1280]{1,0:T(8,128)(2,1)} async-done(((bf16[196,1280]{1,0:T(8,128)(2,1)}), bf16[196,1280]{1,0:T(8,128)(2,1)}) %all-reduce.6.cloned.1.call-update) | async-done | bytes 501776 | tf_op jit(solution)/shard_map/psum | solution.py:161
  169.7 102.3 %all-gather.5.cloned.1.call-done = bf16[1,128,25600]{2,1,0:T(8,128)(2,1)} async-done(((bf16[1,16,25600]{2,1,0:T(8,128)(2,1)}), bf16[1,128,25600]{2,1,0:T(8,128)(2,1)}) %all-gather.5.cloned.1.call-update) | async-done | bytes 6553616 | tf_op jit(solution)/shard_map/all_gather | solution.py:112
  272.0 16.9 %gather_fusion.1 = bf16[128,25600]{1,0:T(8,128)(2,1)} fusion(bf16[128,25600]{1,0:T(8,128)(2,1)} %bitcast.342, s32[1024]{0:T(1024)S(1)} %pad_clamp_fusion.2), kind=kCustom, calls=%fused_computation.1 | custom fusion | bytes 13107712 | tf_op jit(solution)/shard_map/gather | solution.py:117
  288.9 6.1 fusion.103
  295.0 9.7 %reshape.655 = bf16[8,8,160,160]{3,2,1,0:T(8,128)(2,1)} reshape(bf16[64,25600]{1,0:T(8,128)(2,1)} %get-tuple-element.115) | data formatting | bytes 6553600 | tf_op jit(solution)/shard_map/reshape | solution.py:17
  304.7 8.0 copy.177
  312.7 9.2 %reshape.656 = bf16[1280,1280]{1,0:T(8,128)(2,1)} reshape(bf16[8,160,8,160]{3,2,1,0:T(8,128)(2,1)} %bitcast.347) | data formatting | bytes 6553600 | tf_op jit(solution)/shard_map/reshape | solution.py:18
  321.8 9.7 %reshape.657 = bf16[8,8,160,160]{3,2,1,0:T(8,128)(2,1)} reshape(bf16[64,25600]{1,0:T(8,128)(2,1)} %get-tuple-element.116) | data formatting | bytes 6553600 | tf_op jit(solution)/shard_map/reshape | solution.py:17
  331.5 7.9 copy.176
  339.5 9.4 %reshape.658 = bf16[1280,1280]{1,0:T(8,128)(2,1)} reshape(bf16[8,160,8,160]{3,2,1,0:T(8,128)(2,1)} %bitcast.348) | data formatting | bytes 6553600 | tf_op jit(solution)/shard_map/reshape | solution.py:18
  361.7 27.6 %all-reduce.8.cloned.1.call-done = bf16[196,1280]{1,0:T(8,128)(2,1)} async-done(((bf16[196,1280]{1,0:T(8,128)(2,1)}), bf16[196,1280]{1,0:T(8,128)(2,1)}) %all-reduce.8.cloned.1.call-update) | async-done | bytes 501776 | tf_op jit(solution)/shard_map/psum | solution.py:191
  402.9 5.4 fusion.97
  430.5 26.9 %all-reduce.10.cloned.1.call-done = (bf16[196,1280]{1,0:T(8,128)(2,1)}, bf16[196,1280]{1,0:T(8,128)(2,1)}) async-done(((bf16[196,1280]{1,0:T(8,128)(2,1)}, bf16[196,1280]{1,0:T(8,128)(2,1)}), (bf16[196,1280]{1,0:T(8,128)(2,1)}, bf16[196,1280]{1,0:T(8,128)(2,1)})) %all-reduce.10.cloned.1.call-update) | async-done | bytes 1003536 | tf_op jit(solution)/shard_map/psum | solution.py:170
  467.8 9.4 %reshape.665 = f32[48,25600]{1,0:T(8,128)} reshape(f32[8,6,160,160]{3,2,1,0:T(8,128)} %convolution_bitcast_fusion.1) | data formatting | bytes 9830400 | tf_op jit(solution)/shard_map/reshape | solution.py:24
  477.2 5.6 pad_maximum_fusion.1
  482.8 10.7 %gather_fusion.2 = f32[64,25600]{1,0:T(8,128)} fusion(f32[64,25600]{1,0:T(8,128)} %pad_maximum_fusion.1, s32[1024]{0:T(1024)S(1)} %pad_clamp_fusion.1), kind=kCustom, calls=%fused_computation.2 | custom fusion | bytes 13107456 | tf_op jit(solution)/shard_map/gather | solution.py:267
  498.9 11.1 %reshape.667 = f32[8,160,8,160]{3,2,1,0:T(8,128)} reshape(f32[1280,1280]{1,0:T(8,128)} %fusion.96) | data formatting | bytes 13107200 | tf_op jit(solution)/shard_map/reshape | solution.py:23
  510.0 11.2 %copy.122 = f32[8,8,160,160]{3,2,1,0:T(8,128)} copy(f32[8,8,160,160]{3,1,2,0:T(8,128)} %bitcast.345) | data formatting | bytes 13107200 | tf_op jit(solution)/shard_map/transpose | solution.py:24
  521.2 12.2 %reshape.668 = f32[64,25600]{1,0:T(8,128)} reshape(f32[8,8,160,160]{3,2,1,0:T(8,128)} %copy.122) | data formatting | bytes 13107200 | tf_op jit(solution)/shard_map/reshape | solution.py:24
  539.0 12.0 %reshape.669 = f32[64,25600]{1,0:T(8,128)} reshape(f32[8,8,160,160]{3,2,1,0:T(8,128)} %convolution_bitcast_fusion) | data formatting | bytes 13107200 | tf_op jit(solution)/shard_map/reshape | solution.py:24
  551.0 10.8 %pad_maximum_fusion = f32[128,25600]{1,0:T(8,128)} fusion(f32[64,25600]{1,0:T(8,128)} %reshape.669, f32[64,25600]{1,0:T(8,128)} %reshape.668), kind=kLoop, calls=%fused_computation.4 | loop fusion | flops 3276800 | bytes 26214400 | tf_op jit(solution)/shard_map/concatenate | solution.py:188
  561.9 19.2 %gather_fusion.3 = f32[128,25600]{1,0:T(8,128)} fusion(f32[128,25600]{1,0:T(8,128)} %pad_maximum_fusion, s32[1024]{0:T(1024)S(1)} %pad_clamp_fusion), kind=kCustom, calls=%fused_computation.3 | custom fusion | bytes 26214912 | tf_op jit(solution)/shard_map/gather | solution.py:188
  594.4 11.3 %psum.86 = bf16[2,27,80]{2,1,0:T(8,128)(2,1)S(1)} all-reduce(bf16[2,27,80]{2,1,0:T(8,128)(2,1)S(1)} %pad_maximum_fusion.2), channel_id=1, replica_groups=mesh['dp'=8,'mp'=4] {'mp'}, use_global_device_ids=true, to_apply=%region_32.33 | all-reduce | flops 4320 | bytes 17280 | tf_op jit(solution)/shard_map/psum | solution.py:259
  609.1 40.7 %all-reduce = (f32[2,1280]{1,0:T(2,128)}, f32[2,1280]{1,0:T(2,128)}, f32[2,1280]{1,0:T(2,128)}, f32[960]{0:T(1024)}, f32[1280]{0:T(1024)}, /*index=5*/f32[2,27,80]{2,1,0:T(8,128)S(1)}) all-reduce(f32[2,1280]{1,0:T(2,128)S(1)} %pad_maximum_fusion.3, f32[2,1280]{1,0:T(2,128)S(1)} %pad_maximum_fusion.4, ...), channel_id=1, replica_groups=mesh['dp'=8,'mp'=4] {'dp'}, use_global_device_ids=true, to_apply=%region_21.22 | all-reduce | flops 14240 | bytes 105280 | tf_op jit(solution)/shard_map/psum | solution.py:275
  679.8 155.0 %reduce-scatter.5.cloned.1.call-done = f32[1,16,25600]{2,1,0:T(8,128)} async-done(((f32[1,128,25600]{2,1,0:T(8,128)}), f32[1,16,25600]{2,1,0:T(8,128)}) %reduce-scatter.5.cloned.1.call-update) | async-done | bytes 1638416 | tf_op jit(solution)/shard_map/reduce_scatter | solution.py:272
  838.6 8.1 fusion.111
  863.9 5.5 fusion.113
  (239 shorter events, 195.7 us)
Async XLA Ops:
  7.2 10.2 %copy-start = (bf16[1,196,1280]{2,1,0:T(8,128)(2,1)S(1)}, bf16[1,196,1280]{2,1,0:T(8,128)(2,1)}, u32[]{:S(2)}) copy-start(bf16[1,196,1280]{2,1,0:T(8,128)(2,1)} %param.21) | copy-start | bytes 1505284
  7.2 67.8 %all-gather.3.cloned.1.call-start = ((), (), s32[]{:S(2)}) async-start(), calls=%async_computation.2 | async-start | bytes 3686400 | tf_op jit(solution)/shard_map/all_gather | solution.py:111
  9.3 157.8 %all-reduce.6.cloned.1.call-start = ((), (), s32[]{:S(2)}) async-start(), calls=%async_computation.3 | async-start | bytes 1024000 | tf_op jit(solution)/shard_map/psum | solution.py:161
  10.0 381.0 %copy-start.37 = (f32[1,196]{1,0:T(1,128)}, f32[1,196]{1,0:T(1,128)S(1)}, u32[]{:S(2)}) copy-start(f32[1,196]{1,0:T(1,128)S(1)} %convert_element_type.176) | copy-start | bytes 2356
  17.4 88.0 %copy-start.35 = (f32[196]{0:T(256)}, f32[196]{0:T(256)S(1)}, u32[]{:S(2)}) copy-start(f32[196]{0:T(256)S(1)} %broadcast_multiply_fusion.5) | copy-start | bytes 2356
  17.7 87.8 %copy-start.40 = (f32[196]{0:T(256)}, f32[196]{0:T(256)S(1)}, u32[]{:S(2)}) copy-start(f32[196]{0:T(256)S(1)} %add_rsqrt_fusion.1) | copy-start | bytes 2356
  99.3 6.2 copy-start.44
  108.5 288.2 %copy-start.15 = (bf16[196,960]{0,1:T(8,128)(2,1)}, bf16[196,960]{0,1:T(8,128)(2,1)S(1)}, u32[]{:S(2)}) copy-start(bf16[196,960]{0,1:T(8,128)(2,1)S(1)} %copy.93) | copy-start | bytes 1128964
  108.7 10.2 %copy-start.11 = (bf16[1,196,1,4,80]{4,3,1,2,0:T(4,128)(2,1)}, bf16[1,196,1,4,80]{4,3,1,2,0:T(4,128)(2,1)S(1)}, u32[]{:S(2)}) copy-start(bf16[1,196,1,4,80]{4,3,1,2,0:T(4,128)(2,1)S(1)} %copy.95) | copy-start | bytes 376324
  125.4 8.1 copy-start.28
  133.5 6.8 copy-start.39
  134.8 137.2 %all-gather.5.cloned.1.call-start = ((), (), s32[]{:S(2)}) async-start(), calls=%async_computation.4 | async-start | bytes 7372800 | tf_op jit(solution)/shard_map/all_gather | solution.py:112
  137.3 252.1 %all-reduce.8.cloned.1.call-start = ((), (), s32[]{:S(2)}) async-start(), calls=%async_computation.5 | async-start | bytes 1024000 | tf_op jit(solution)/shard_map/psum | solution.py:191
  339.5 9.4 %copy-start.1 = (bf16[196,1280]{1,0:T(8,128)(2,1)S(1)}, bf16[196,1280]{1,0:T(8,128)(2,1)}, u32[]{:S(2)}) copy-start(bf16[196,1280]{1,0:T(8,128)(2,1)} %all-reduce.6.cloned.1.call-done) | copy-start | bytes 1505284
  339.5 9.4 %copy-start.43 = (f32[1280]{0:T(1024)S(1)}, f32[1280]{0:T(1024)}, u32[]{:S(2)}) copy-start(f32[1280]{0:T(1024)} %param.28) | copy-start | bytes 15364
  357.7 99.7 %all-reduce.10.cloned.1.call-start = ((), (), s32[]{:S(2)}) async-start(), calls=%async_computation.8 | async-start | bytes 2048000 | tf_op jit(solution)/shard_map/psum | solution.py:170
  396.7 6.2 copy-start.10
  402.9 6.7 copy-start.25
  410.5 8.8 copy-start.5
  420.9 229.6 %reduce-scatter.3.cloned.1.call-start = ((), (), s32[]{:S(2)}) async-start(), calls=%async_computation.6 | async-start | bytes 7372800 | tf_op jit(solution)/shard_map/reduce_scatter | solution.py:271
  425.8 31.6 %copy-start.23 = (bf16[1,196,1280]{2,1,0:T(8,128)(2,1)S(1)}, bf16[1,196,1280]{2,1,0:T(8,128)(2,1)}, u32[]{:S(2)}) copy-start(bf16[1,196,1280]{2,1,0:T(8,128)(2,1)} %param.23) | copy-start | bytes 1505284
  425.8 31.6 %copy-start.36 = (f32[196]{0:T(256)S(1)}, f32[196]{0:T(256)}, u32[]{:S(2)}) copy-start(f32[196]{0:T(256)} %copy-done.35) | copy-start | bytes 2356
  425.8 31.6 %copy-start.38 = (f32[1,196]{1,0:T(1,128)S(1)}, f32[1,196]{1,0:T(1,128)}, u32[]{:S(2)}) copy-start(f32[1,196]{1,0:T(1,128)} %copy-done.37) | copy-start | bytes 2356
  425.8 31.6 %copy-start.41 = (f32[196]{0:T(256)S(1)}, f32[196]{0:T(256)}, u32[]{:S(2)}) copy-start(f32[196]{0:T(256)} %copy-done.40) | copy-start | bytes 2356
  425.8 34.0 %copy-start.7 = (f32[196,1280]{1,0:T(8,128)S(1)}, f32[196,1280]{1,0:T(8,128)}, u32[]{:S(2)}) copy-start(f32[196,1280]{1,0:T(8,128)} %copy-done.6) | copy-start | bytes 3010564
  467.8 9.4 %copy-start.8 = (f32[16,25600]{1,0:T(8,128)S(1)}, f32[16,25600]{1,0:T(8,128)}, u32[]{:S(2)}) copy-start(f32[16,25600]{1,0:T(8,128)} %reshape.666) | copy-start | bytes 4915204
  493.5 341.2 %reduce-scatter.5.cloned.1.call-start = ((), (), s32[]{:S(2)}) async-start(), calls=%async_computation.7 | async-start | bytes 14745600 | tf_op jit(solution)/shard_map/reduce_scatter | solution.py:272
  521.2 12.2 %copy-start.21 = (bf16[1280,196]{0,1:T(8,128)(2,1)S(1)}, bf16[1280,196]{0,1:T(8,128)(2,1)}, u32[]{:S(2)}) copy-start(bf16[1280,196]{0,1:T(8,128)(2,1)} %get-tuple-element.121) | copy-start | bytes 1505284
  588.3 4.8 copy-start.33
  588.3 5.2 copy-start.16
  591.4 17.7 %copy-start.42 = (f32[1280]{0:T(1024)S(1)}, f32[1280]{0:T(1024)}, u32[]{:S(2)}) copy-start(f32[1280]{0:T(1024)} %get-tuple-element.128) | copy-start | bytes 15364
  672.0 5.5 copy-start.18
  (25 other events, 60.5 us)
Sparse Core Ops, SparseCore 0:
  10.8 64.1 all-gather.2
  134.9 32.0 all-reduce.5
  169.8 102.1 all-gather.4
  357.8 31.4 all-reduce.7
  421.0 36.3 all-reduce.9
  493.7 122.6 reduce-scatter.2
  620.5 214.1 reduce-scatter.4
where the time goes:
time: 895 us; the launch traced here: 886 us
  waiting for transfers between devices  396 us (44%)
  local copies, waits for them, and re-layouts  271 us (30%)
  matrix products  85.6 us (10%)
  other arithmetic  65.2 us (7%)
  blocking collectives  52.1 us (6%)
  between operations  15.1 us (2%)
    reduce_scatter x1, waiting for transfers between devices, local(): lax.psum_scatter(mlp_stack, 'dp', scatter_dimension=1, tiled=True)  155 us
    all_gather x1, waiting for transfers between devices, local(): lax.all_gather(mlp_master.astype(jnp.bfloat16), 'dp', axis=1, tiled=True)  102 us
    all_gather x1, waiting for transfers between devices, local(): lax.all_gather(attn_master.astype(jnp.bfloat16), 'dp', axis=1, tiled=True)  57.3 us
    reshape x8, local copies, waits for them, and re-layouts, untile(): tile_rows.reshape(row_count // tile_side, col_count // tile_side, tile_si...  54 us
    psum x1, blocking collectives, local(): lax.psum((jnp.stack([gain_one_grad, gain_two_grad]), jnp.stack([shift_one...  40.7 us
    reshape x4, local copies, waits for them, and re-layouts, retile(): return shaped.transpose(0, 2, 1, 3).reshape(-1, tile_side * tile_side)  38.3 us
    psum x1, waiting for transfers between devices, local(): lax.psum(jnp.einsum('nf,df->nd', grad_hidden, w_up, preferred_element_typ...  27.6 us
    reshape x4, local copies, waits for them, and re-layouts, untile(): return shaped.transpose(0, 2, 1, 3).reshape(row_count, col_count)  27.2 us
  transfers between devices with their start and end apart: 7, of which 6 were waited for; matrix products, arithmetic and copies ran while one was open for 18% of the time, Pallas kernels for 0%

commit v1 on v0

--- a/solution.py
+++ b/solution.py
@@ -2,7 +2,10 @@
 
 import jax
 import jax.numpy as jnp
+import numpy as np
 from jax import lax
+from jax.experimental import pallas as pl
+from jax.experimental.pallas import tpu as pltpu
 from jax.sharding import PartitionSpec as P
 
 highest = lax.Precision.HIGHEST
@@ -312,7 +315,433 @@
     )
 
 
-def solution(mesh):
+BF = jnp.bfloat16
+F32 = jnp.float32
+ROWS = 208
+SIDE = 160
+
+
+def dot(a, b):
+    return jnp.dot(a, b, preferred_element_type=F32)
+
+
+def dot_nt(a, b):
+    return lax.dot_general(a, b, (((1,), (1,)), ((), ())), preferred_element_type=F32)
+
+
+def dot_tn(a, b):
+    return lax.dot_general(a, b, (((0,), (0,)), ((), ())), preferred_element_type=F32)
+
+
+def lane_at(shape):
+    return lax.broadcasted_iota(jnp.int32, shape, len(shape) - 1)
+
+
+def low_parts(value):
+    high = value.astype(BF)
+    return high, (value - high.astype(F32)).astype(BF)
+
+
+def flat_to_square(read, square, count):
+    lane = lane_at((count, 128))
+
+    def body(group, carry):
+        base = pl.multiple_of(group * 640, 128)
+        x = [read(base + 128 * k) for k in range(5)]
+        r1 = pltpu.roll(x[1], 96, 1)
+        r2 = pltpu.roll(x[2], 96, 1)
+        h2 = pltpu.roll(x[2], 64, 1)
+        h3 = pltpu.roll(x[3], 64, 1)
+        r3 = pltpu.roll(x[3], 32, 1)
+        r4 = pltpu.roll(x[4], 32, 1)
+        pairs = (
+            (x[0], x[1]),
+            (jnp.where(lane < 96, r1, r2), r2),
+            (jnp.where(lane < 64, h2, h3), h3),
+            (jnp.where(lane < 32, r3, r4), r4),
+        )
+        for m, (wide, narrow) in enumerate(pairs):
+            square[0, pl.ds(4 * group + m, count, stride=SIDE), :] = wide
+            square[1, pl.ds(4 * group + m, count, stride=SIDE), :] = narrow
+        return carry
+
+    lax.fori_loop(0, 40, body, 0)
+
+
+def square_to_flat(square, write, count):
+    lane = lane_at((count, 128))
+
+    def body(group, carry):
+        base = pl.multiple_of(group * 640, 128)
+        a = [square[0, pl.ds(4 * group + m, count, stride=SIDE), :] for m in range(4)]
+        b = [square[1, pl.ds(4 * group + m, count, stride=SIDE), :] for m in range(4)]
+        a1 = pltpu.roll(a[1], 32, 1)
+        b1 = pltpu.roll(b[1], 32, 1)
+        a2 = pltpu.roll(a[2], 64, 1)
+        b2 = pltpu.roll(b[2], 64, 1)
+        a3 = pltpu.roll(a[3], 96, 1)
+        b3 = pltpu.roll(b[3], 96, 1)
+        write(base, a[0])
+        write(base + 128, jnp.where(lane < 32, b[0], a1))
+        write(base + 256, jnp.where(lane < 32, a1, jnp.where(lane < 64, b1, a2)))
+        write(base + 384, jnp.where(lane < 64, a2, jnp.where(lane < 96, b2, a3)))
+        write(base + 512, jnp.where(lane < 96, a3, b3))
+        return carry
+
+    lax.fori_loop(0, 40, body, 0)
+
+
+def pack_body(attn, mlp, wire_attn, wire_mlp, square):
+    lane = lane_at((SIDE, 128))
+    for source, first, target, slot in ((attn, 0, wire_attn, 0), (mlp, 0, wire_mlp, 0), (mlp, 8, wire_mlp, 2)):
+        flat_to_square(lambda at, s=source, f=first: s[f : f + 8, pl.ds(at, 128)], square, 8)
+        for half in range(2):
+            spare = None
+            for q in range(4):
+                row = (4 * half + q) * SIDE
+                target[5 * (slot + half) + q] = square[0, row : row + SIDE, :].astype(BF)
+                piece = square[1, row : row + SIDE, :]
+                if q == 0:
+                    spare = piece
+                else:
+                    spare = jnp.where(lane < 32 * q, spare, pltpu.roll(piece, 32 * q, 1))
+            target[5 * (slot + half) + 4] = spare.astype(BF)
+
+
+def unpack_narrow(wire, narrow, groups):
+    def body(g, carry):
+        last = wire[5 * g + 4]
+        for q in range(4):
+            narrow[4 * g + q] = last[:, 32 * q : 32 * q + 32]
+        return carry
+
+    lax.fori_loop(0, groups, body, 0)
+
+
+def unpack_sorted(wire, narrow, order, base, outs, rows, cols):
+    def body(t, carry):
+        row = t // cols
+        col = t - row * cols
+        stored = order[base + t]
+        where_at = pl.multiple_of(row * SIDE, 32)
+        outs[col, pl.ds(where_at, SIDE), 0:128] = wire[(stored // 4) * 5 + stored % 4]
+        outs[col, pl.ds(where_at, SIDE), 128:160] = narrow[stored]
+        return carry
+
+    lax.fori_loop(0, rows * cols, body, 0)
+
+
+def norm_parts(x):
+    mean = jnp.mean(x, axis=-1, keepdims=True)
+    centre = x - mean
+    inverse = lax.rsqrt(jnp.mean(centre * centre, axis=-1, keepdims=True) + norm_eps)
+    return centre * inverse, inverse
+
+
+def norm_back(grad_in, unit, inverse, gain):
+    w = grad_in * gain
+    return inverse * (
+        w - jnp.mean(w, axis=-1, keepdims=True) - unit * jnp.mean(w * unit, axis=-1, keepdims=True)
+    )
+
+
+def padded(ref, rows, kind=F32):
+    value = ref[...].astype(kind)
+    return jnp.concatenate([value, jnp.zeros((ROWS - rows, value.shape[1]), kind)], axis=0)
+
+
+def attn_forward(mixed, rel_hi, rel_lo, pick, spread, probs, att, scale, tokens_here):
+    lane = lane_at((ROWS, SIDE))
+    key_ok = lane_at((ROWS, ROWS)) < tokens_here
+    head = SIDE // 2
+    for p in range(2):
+        q, k, v = mixed[p], mixed[2 + p], mixed[4 + p]
+        parts = []
+        for h in range(2):
+            mine = (lane >= head) if h else (lane < head)
+            qm = jnp.where(mine, q, jnp.zeros_like(q))
+            s = dot_nt(qm, k) * scale
+            a_hi, a_lo = low_parts(dot_nt(qm, rel_hi[...]) + dot_nt(qm, rel_lo[...]))
+            for c in range(7):
+                mask = pick[:, 128 * c : 128 * c + 128]
+                table = spread[128 * c : 128 * c + 128, :]
+                s = s + dot(a_hi * mask, table) + dot(a_lo * mask, table)
+            s = jnp.where(key_ok, s, -1e30)
+            top = jnp.max(s, axis=-1, keepdims=True)
+            e = jnp.exp(s - top)
+            pr = e / jnp.sum(e, axis=-1, keepdims=True)
+            probs[2 * p + h] = pr
+            parts.append(dot(pr.astype(BF), v))
+        att[p] = jnp.where(lane < head, parts[0], parts[1]).astype(BF)
+
+
+def attn_backward(mixed, rel_hi, rel_lo, pick, spread, probs, gatt, gm, rel_out, scale):
+    lane = lane_at((ROWS, SIDE))
+    head = SIDE // 2
+    for p in range(2):
+        q, k, v = mixed[p], mixed[2 + p], mixed[4 + p]
+        ga = gatt[p]
+        dq, dk, dv, dr = [], [], [], []
+        for h in range(2):
+            mine = (lane >= head) if h else (lane < head)
+            pr = probs[2 * p + h]
+            gam = jnp.where(mine, ga, jnp.zeros_like(ga))
+            gp = dot_nt(gam, v)
+            dv.append(dot_tn(pr.astype(BF), ga))
+            ds = (pr * (gp - jnp.sum(pr * gp, axis=-1, keepdims=True))).astype(BF)
+            da = None
+            for c in range(7):
+                term = dot_nt(ds, spread[128 * c : 128 * c + 128, :]) * pick[:, 128 * c : 128 * c + 128].astype(F32)
+                da = term if da is None else da + term
+            da_hi, da_lo = low_parts(da)
+            relq = dot(da_hi, rel_hi[...]) + dot(da_lo, rel_hi[...]) + dot(da_hi, rel_lo[...])
+            dq.append(dot(ds, k) * scale + relq)
+            dk.append(dot_tn(ds, q) * scale)
+            dr.append(dot_tn(da_hi, q) + dot_tn(da_lo, q))
+        gm[p] = jnp.where(lane < head, dq[0], dq[1]).astype(BF)
+        gm[2 + p] = jnp.where(lane < head, dk[0], dk[1]).astype(BF)
+        gm[4 + p] = jnp.where(lane < head, dv[0], dv[1]).astype(BF)
+        rel = jnp.where(lane_at((128, SIDE)) < head, dr[0], dr[1])
+        if p == 0:
+            rel_out[...] = rel
+        else:
+            rel_out[...] += rel
+
+
+def attn_fwd_body(order, tokens, live, gains, biases, qkv_bias, rel_hi, rel_lo, pick, spread, wire,
+                  part, normed, mixed, probs, att, w_qkv, w_proj, narrow, block):
+    t = tokens.shape[0]
+    x = padded(tokens, t)
+    unit, _ = norm_parts(x)
+    normed[...] = ((unit * gains[0:1, :] + biases[0:1, :]) * live[...]).astype(BF)
+    unpack_narrow(wire, narrow, wire.shape[0] // 5)
+    unpack_sorted(wire, narrow, order, 0, w_qkv, 8, 6)
+    unpack_sorted(wire, narrow, order, 48, w_proj, 2, 8)
+
+    def mix(j, carry):
+        mixed[j] = (dot(normed[...], w_qkv[j]) + qkv_bias[pl.ds(j, 1), :]).astype(BF)
+        return carry
+
+    lax.fori_loop(0, 6, mix, 0)
+    attn_forward(mixed, rel_hi, rel_lo, pick, spread, probs, att, (SIDE // 2) ** -0.5, t)
+
+    def project(n, carry):
+        value = dot(att[0], w_proj[n, 0:SIDE, :]) + dot(att[1], w_proj[n, SIDE : 2 * SIDE, :])
+        block[n] = value
+        return carry
+
+    lax.fori_loop(0, 8, project, 0)
+    for n in range(8):
+        part[:, SIDE * n : SIDE * n + SIDE] = block[n][0:t, :].astype(BF)
+
+
+def mlp_body(order, tokens, live, cotangent, branch, gains, biases, out_biases, up_bias, wire,
+             part_down, part_second, sec_blocks, act_blocks, gh, go, bias_sums, w_up, w_down, narrow, block, second):
+    t = tokens.shape[0]
+    x = padded(tokens, t)
+    middle = x + padded(branch, t) + out_biases[0:1, :]
+    unit, _ = norm_parts(middle)
+    second[...] = (unit * gains[1:2, :] + biases[1:2, :]).astype(BF)
+    grad_out = padded(cotangent, t) * live[...]
+    for n in range(8):
+        sec_blocks[n] = second[:, SIDE * n : SIDE * n + SIDE]
+        go[n] = grad_out[:, SIDE * n : SIDE * n + SIDE].astype(BF)
+    unpack_narrow(wire, narrow, wire.shape[0] // 5)
+    unpack_sorted(wire, narrow, order, 0, w_up, 8, 8)
+    unpack_sorted(wire, narrow, order, 64, w_down, 8, 8)
+
+    def hidden_block(j, carry):
+        row = pl.multiple_of(j * SIDE, 32)
+        hid = dot(second[...], w_up[j]) + up_bias[pl.ds(j, 1), :]
+        cdf = 0.5 * (1.0 + lax.erf(hid * 0.5**0.5))
+        slope = cdf + hid * (jnp.exp(-0.5 * hid * hid) * (2.0 * math.pi) ** -0.5)
+        act_blocks[j] = (hid * cdf).astype(BF)
+        ga = dot_nt(go[0], w_down[0, pl.ds(row, SIDE), :])
+        for n in range(1, 8):
+            ga = ga + dot_nt(go[n], w_down[n, pl.ds(row, SIDE), :])
+        low = (ga * slope).astype(BF)
+        gh[j] = low
+        bias_sums[pl.ds(j, 1), :] = jnp.sum(low.astype(F32), axis=0, keepdims=True)
+        return carry
+
+    lax.fori_loop(0, 8, hidden_block, 0)
+
+    def second_back(i, carry):
+        row = pl.multiple_of(i * SIDE, 32)
+        value = dot_nt(gh[0], w_up[0, pl.ds(row, SIDE), :])
+        for j in range(1, 8):
+            value = value + dot_nt(gh[j], w_up[j, pl.ds(row, SIDE), :])
+        block[i] = value
+        return carry
+
+    lax.fori_loop(0, 8, second_back, 0)
+    for n in range(8):
+        part_second[:, SIDE * n : SIDE * n + SIDE] = block[n][0:t, :].astype(BF)
+
+    def down(n, carry):
+        value = dot(act_blocks[0], w_down[n, 0:SIDE, :])
+        for j in range(1, 8):
+            value = value + dot(act_blocks[j], w_down[n, j * SIDE : (j + 1) * SIDE, :])
+        block[n] = value
+        return carry
+
+    lax.fori_loop(0, 8, down, 0)
+    for n in range(8):
+        part_down[:, SIDE * n : SIDE * n + SIDE] = block[n][0:t, :].astype(BF)
+
+
+def grad_tiles_body(left_at, right_at, count, read_left, read_right, wire):
+    lane = lane_at((SIDE, 128))
+
+    def body(g, carry):
+        spare = None
+        for q in range(4):
+            s = 4 * g + q
+            tile = dot_tn(read_left(left_at[s]), read_right(right_at[s]))
+            wire[5 * g + q] = tile[:, 0:128].astype(BF)
+            piece = jnp.concatenate([tile[:, 128:160], jnp.zeros((SIDE, 96), F32)], axis=1)
+            spare = piece if q == 0 else jnp.where(lane < 32 * q, spare, pltpu.roll(piece, 32 * q, 1))
+        wire[5 * g + 4] = spare.astype(BF)
+        return carry
+
+    lax.fori_loop(0, count // 4, body, 0)
+
+
+def mid_back_body(order, tokens, live, cotangent, branch, down_sum, second_sum, gains, out_biases,
+                  wire, mixed, probs, normed, att, rel_hi, rel_lo, pick, spread,
+                  block_out, grad_middle_out, part_normed, rel_out, gm, gb, nb, sums, bias_sums,
+                  w_qkv, w_proj, narrow, block, gatt):
+    t = tokens.shape[0]
+    x = padded(tokens, t)
+    middle = x + padded(branch, t) + out_biases[0:1, :]
+    result = (middle + padded(down_sum, t) + out_biases[1:2, :]) * live[...]
+    block_out[...] = result[0:t, :].astype(BF)
+    grad_out = padded(cotangent, t) * live[...]
+    unit, inverse = norm_parts(middle)
+    grad_second = padded(second_sum, t)
+    sums[0:1, :] = jnp.sum(grad_second * unit, axis=0, keepdims=True)
+    sums[1:2, :] = jnp.sum(grad_second, axis=0, keepdims=True)
+    sums[2:3, :] = jnp.sum(grad_out, axis=0, keepdims=True)
+    grad_middle = grad_out + norm_back(grad_second, unit, inverse, gains[1:2, :])
+    sums[3:4, :] = jnp.sum(grad_middle, axis=0, keepdims=True)
+    grad_middle_out[...] = grad_middle[0:t, :]
+    for n in range(8):
+        gb[n] = grad_middle[:, SIDE * n : SIDE * n + SIDE].astype(BF)
+        nb[n] = normed[:, SIDE * n : SIDE * n + SIDE]
+    unpack_narrow(wire, narrow, wire.shape[0] // 5)
+    unpack_sorted(wire, narrow, order, 0, w_qkv, 8, 6)
+    unpack_sorted(wire, narrow, order, 48, w_proj, 2, 8)
+    for p in range(2):
+        value = dot_nt(gb[0], w_proj[0, p * SIDE : (p + 1) * SIDE, :])
+        for n in range(1, 8):
+            value = value + dot_nt(gb[n], w_proj[n, p * SIDE : (p + 1) * SIDE, :])
+        gatt[p] = value.astype(BF)
+    attn_backward(mixed, rel_hi, rel_lo, pick, spread, probs, gatt, gm, rel_out, (SIDE // 2) ** -0.5)
+    for j in range(6):
+        bias_sums[j : j + 1, :] = jnp.sum(gm[j].astype(F32), axis=0, keepdims=True)
+
+    def normed_back(i, carry):
+        row = pl.multiple_of(i * SIDE, 32)
+        value = dot_nt(gm[0], w_qkv[0, pl.ds(row, SIDE), :])
+        for j in range(1, 6):
+            value = value + dot_nt(gm[j], w_qkv[j, pl.ds(row, SIDE), :])
+        block[i] = value
+        return carry
+
+    lax.fori_loop(0, 8, normed_back, 0)
+    for n in range(8):
+        part_normed[:, SIDE * n : SIDE * n + SIDE] = block[n][0:t, :].astype(BF)
+
+
+def token_back_body(tokens, live, normed_sum, grad_middle, gains, tokens_grad, sums):
+    x = tokens[...].astype(F32)
+    unit, inverse = norm_parts(x)
+    grad_normed = normed_sum[...].astype(F32) * live[...]
+    sums[0:1, :] = jnp.sum(grad_normed * unit, axis=0, keepdims=True)
+    sums[1:2, :] = jnp.sum(grad_normed, axis=0, keepdims=True)
+    tokens_grad[...] = grad_middle[...] + norm_back(grad_normed, unit, inverse, gains[0:1, :])
+
+
+def square_tile(square, t):
+    row = pl.multiple_of(t * SIDE, 32)
+    return jnp.concatenate([square[0, pl.ds(row, SIDE), :], square[1, pl.ds(row, SIDE), 0:32]], axis=1)
+
+
+def put_tile(square, t, value):
+    row = pl.multiple_of(t * SIDE, 32)
+    square[0, pl.ds(row, SIDE), :] = value[:, 0:128]
+    square[1, pl.ds(row, SIDE), 0:32] = value[:, 128:160]
+
+
+def split_dot(kind, a, b):
+    a_hi, a_lo = low_parts(a)
+    b_hi, b_lo = low_parts(b)
+    return kind(a_hi, b_hi) + (kind(a_hi, b_lo) + kind(a_lo, b_hi))
+
+
+def soap_group(r0, grad_square, master, left, right, first, second,
+               grad_out, new_out, copy_out, first_out, second_out, sq_left, sq_right, sq_work):
+    rows = slice(r0, r0 + 8)
+
+    def writer(ref):
+        def write(at, value):
+            ref[rows, pl.ds(at, 128)] = value
+        return write
+
+    flat_to_square(lambda at: left[rows, pl.ds(at, 128)], sq_left, 8)
+    flat_to_square(lambda at: right[rows, pl.ds(at, 128)], sq_right, 8)
+    square_to_flat(grad_square, writer(grad_out), 8)
+
+    def rotate(t, carry):
+        l, r = square_tile(sq_left, t), square_tile(sq_right, t)
+        half = split_dot(dot_tn, l, square_tile(grad_square, t))
+        put_tile(sq_work, t, split_dot(dot, half, r))
+        return carry
+
+    lax.fori_loop(0, 8, rotate, 0)
+
+    def moments(at, rotated):
+        cols = pl.ds(at, 128)
+        f = beta_one * first[rows, cols] + (1.0 - beta_one) * rotated
+        s = beta_two * second[rows, cols] + (1.0 - beta_two) * rotated * rotated
+        first_out[rows, cols] = f
+        second_out[rows, cols] = s
+        new_out[rows, cols] = f / (jnp.sqrt(s) + adam_eps)
+
+    square_to_flat(sq_work, moments, 8)
+    flat_to_square(lambda at: new_out[rows, pl.ds(at, 128)], sq_work, 8)
+
+    def turn_back(t, carry):
+        l, r = square_tile(sq_left, t), square_tile(sq_right, t)
+        half = split_dot(dot, l, square_tile(sq_work, t))
+        put_tile(sq_work, t, split_dot(dot_nt, half, r))
+        return carry
+
+    lax.fori_loop(0, 8, turn_back, 0)
+
+    def finish(at, update):
+        cols = pl.ds(at, 128)
+        value = master[rows, cols] - learn_rate * update
+        new_out[rows, cols] = value
+        copy_out[rows, cols] = value.astype(BF)
+
+    square_to_flat(sq_work, finish, 8)
+
+
+def soap_body(wire, master, left, right, first, second,
+              grad_out, new_out, copy_out, first_out, second_out, sq_grad, sq_left, sq_right, sq_work):
+    for r in range(master.shape[0] // 8):
+        for half in range(2):
+            last = wire[5 * (2 * r + half) + 4].astype(F32)
+            for q in range(4):
+                row = (4 * half + q) * SIDE
+                sq_grad[0, row : row + SIDE, :] = wire[5 * (2 * r + half) + q].astype(F32)
+                sq_grad[1, row : row + SIDE, :] = last if q == 0 else pltpu.roll(last, 128 - 32 * q, 1)
+        soap_group(8 * r, sq_grad, master, left, right, first, second,
+                   grad_out, new_out, copy_out, first_out, second_out, sq_left, sq_right, sq_work)
+
+
+def build(mesh):
     placed = (
         P("dp", None, None),
         P("dp", None),
@@ -337,7 +766,7 @@
         P("mp", "dp", None),
     )
     return jax.shard_map(
-        local,
+        fast_local if dict(mesh.shape) == {"dp": 8, "mp": 4} else local,
         mesh=mesh,
         in_specs=placed,
         out_specs=(
@@ -362,3 +791,147 @@
         ),
         check_vma=False,
     )
+
+
+VM = pl.BlockSpec(memory_space=pltpu.VMEM)
+SM = pl.BlockSpec(memory_space=pltpu.SMEM)
+LIMIT = 60 * 1024 * 1024
+
+
+def call(body, tables, args, outs, scratch, name):
+    return pl.pallas_call(
+        body,
+        out_shape=[jax.ShapeDtypeStruct(shape, kind) for shape, kind in outs],
+        in_specs=[SM] * len(tables) + [VM] * len(args),
+        out_specs=[VM] * len(outs),
+        scratch_shapes=[pltpu.VMEM(shape, kind) for shape, kind in scratch],
+        compiler_params=pltpu.CompilerParams(vmem_limit_bytes=LIMIT),
+        name=name,
+    )(*tables, *args)
+
+
+def rel_constants(side):
+    rows = np.arange(ROWS)
+    lanes = np.arange(896)
+    within, along = lanes % 64, lanes // 64
+    high = np.where(rows < side * side, rows // side, -1)[:, None]
+    wide = np.where(rows < side * side, rows % side, -1)[:, None]
+    pick = np.where(within[None] < 32, high == along[None], wide == along[None])
+    keys = np.arange(ROWS)
+    key_h, key_w = keys // side, keys % side
+    offset = np.where(within[:, None] < 32, along[:, None] - key_h[None], along[:, None] - key_w[None]) + side - 1
+    spread = (offset == (within % 32)[:, None]) & (keys < side * side)[None]
+    return jnp.asarray(pick, BF), jnp.asarray(spread, BF)
+
+
+def inverse_order(owner):
+    count = owner.shape[0]
+    at = jnp.arange(count, dtype=jnp.int32)
+    return jnp.sum(jnp.where(owner[:, None] == at[None, :], at[:, None], 0), axis=0)
+
+
+def fast_local(
+    tokens, pad_mask, cotangent, norm_gains, norm_biases, out_biases, qkv_bias, up_bias, rel_pos,
+    attn_owner, mlp_owner, attn_master, mlp_master, attn_left, attn_right, mlp_left, mlp_right,
+    attn_first, attn_second, mlp_first, mlp_second,
+):
+    t, width = tokens.shape[1:]
+    tok, cot = tokens[0], cotangent[0]
+    live = jnp.pad(pad_mask[0].astype(F32), (0, ROWS - t))[:, None]
+    qb, ub = qkv_bias.reshape(6, SIDE), up_bias.reshape(8, SIDE)
+    rel = jnp.pad(rel_pos, ((0, 0), (0, 32 - rel_pos.shape[1]), (0, 0))).reshape(64, SIDE // 2)
+    rel_hi, rel_lo = low_parts(jnp.tile(rel, (2, 2)))
+    pick, spread = rel_constants((rel_pos.shape[1] + 1) // 2)
+    own_a, own_m = attn_owner[0], mlp_owner[0]
+    ord_a, ord_m = inverse_order(own_a), inverse_order(own_m)
+    xa = jnp.where(own_a < 48, own_a // 6, 8 + (own_a - 48) // 8)
+    ya = jnp.where(own_a < 48, own_a % 6, 6 + (own_a - 48) % 8)
+    xm, ym = own_m // 8, (own_m // 64) * 8 + own_m % 8
+
+    wire_a, wire_m = call(
+        pack_body, (), (attn_master[0], mlp_master[0]),
+        [((10, SIDE, 128), BF), ((20, SIDE, 128), BF)], [((2, 8 * SIDE, 128), F32)], "pack")
+    all_a = lax.all_gather(wire_a, "dp", axis=0, tiled=True)
+    all_m = lax.all_gather(wire_m, "dp", axis=0, tiled=True)
+
+    part, normed, mixed, probs, att = call(
+        attn_fwd_body, (ord_a,),
+        (tok, live, norm_gains, norm_biases, qb, rel_hi, rel_lo, pick, spread, all_a),
+        [((t, width), BF), ((ROWS, width), BF), ((6, ROWS, SIDE), BF), ((4, ROWS, ROWS), F32), ((2, ROWS, SIDE), BF)],
+        [((6, 8 * SIDE, SIDE), BF), ((8, 2 * SIDE, SIDE), BF), ((64, SIDE, 32), BF), ((8, ROWS, SIDE), F32)],
+        "attn_fwd")
+    branch = lax.psum(part, "mp")
+    part_down, part_second, sec_blocks, act_blocks, gh, go, up_sums = call(
+        mlp_body, (ord_m,),
+        (tok, live, cot, branch, norm_gains, norm_biases, out_biases, ub, all_m),
+        [((t, width), BF), ((t, width), BF)] + [((8, ROWS, SIDE), BF)] * 4 + [((8, SIDE), F32)],
+        [((8, 8 * SIDE, SIDE), BF), ((8, 8 * SIDE, SIDE), BF), ((128, SIDE, 32), BF), ((8, ROWS, SIDE), F32), ((ROWS, width), BF)],
+        "mlp")
+    second_sum = lax.psum(part_second, "mp")
+    down_sum = lax.psum(part_down, "mp")
+
+    def mlp_tiles(left_at, right_at, sec, act, gh_ref, go_ref, wire, lefts, rights):
+        lefts[0:8], lefts[8:16] = sec[...], act[...]
+        rights[0:8], rights[8:16] = gh_ref[...], go_ref[...]
+        grad_tiles_body(left_at, right_at, 128, lambda i: lefts[i], lambda i: rights[i], wire)
+
+    stack_m, = call(
+        mlp_tiles, (xm, ym), (sec_blocks, act_blocks, gh, go), [((160, SIDE, 128), BF)],
+        [((16, ROWS, SIDE), BF)] * 2, "mlp_tiles")
+    sum_m = lax.psum_scatter(stack_m, "dp", scatter_dimension=0, tiled=True)
+
+    block_out, grad_middle, part_normed, rel_part, gm, gb, nb, sums_two, qkv_sums = call(
+        mid_back_body, (ord_a,),
+        (tok, live, cot, branch, down_sum, second_sum, norm_gains, out_biases, all_a, mixed, probs, normed, att,
+         rel_hi, rel_lo, pick, spread),
+        [((t, width), BF), ((t, width), F32), ((t, width), BF), ((128, SIDE), F32), ((6, ROWS, SIDE), BF),
+         ((8, ROWS, SIDE), BF), ((8, ROWS, SIDE), BF), ((4, width), F32), ((6, SIDE), F32)],
+        [((6, 8 * SIDE, SIDE), BF), ((8, 2 * SIDE, SIDE), BF), ((64, SIDE, 32), BF), ((8, ROWS, SIDE), F32),
+         ((2, ROWS, SIDE), BF)],
+        "mid_back")
+    rel_half = SIDE // 2
+    rel_fold = rel_part[:64] + rel_part[64:]
+    rel_fold = (rel_fold[:, :rel_half] + rel_fold[:, rel_half:]).reshape(2, 32, rel_half)[:, : rel_pos.shape[1]]
+    normed_sum = lax.psum(part_normed, "mp")
+    rel_sum = lax.psum(rel_fold.astype(BF), "mp").astype(F32)
+
+    def attn_tiles(left_at, right_at, nb_ref, att_ref, gm_ref, gb_ref, wire, lefts, rights):
+        lefts[0:8], lefts[8:10] = nb_ref[...], att_ref[...]
+        rights[0:6], rights[6:14] = gm_ref[...], gb_ref[...]
+        grad_tiles_body(left_at, right_at, 64, lambda i: lefts[i], lambda i: rights[i], wire)
+
+    stack_a, = call(
+        attn_tiles, (xa, ya), (nb, att, gm, gb), [((80, SIDE, 128), BF)],
+        [((10, ROWS, SIDE), BF), ((14, ROWS, SIDE), BF)], "attn_tiles")
+    sum_a = lax.psum_scatter(stack_a, "dp", scatter_dimension=0, tiled=True)
+    tokens_grad, sums_one = call(
+        token_back_body, (), (tok, live[:t], normed_sum, grad_middle, norm_gains),
+        [((t, width), F32), ((2, width), F32)], [], "token_back")
+    gains_grad, biases_grad, outb_grad, rel_grad, qkv_grad, up_grad = lax.psum(
+        (
+            jnp.stack([sums_one[0], sums_two[0]]),
+            jnp.stack([sums_one[1], sums_two[1]]),
+            jnp.stack([sums_two[3], sums_two[2]]),
+            rel_sum,
+            qkv_sums.reshape(-1),
+            up_sums.reshape(-1),
+        ),
+        "dp",
+    )
+
+    def soap(wire, master, left, right, first, second, name):
+        shape = master.shape[1:]
+        outs = call(
+            soap_body, (), (wire, master[0], left[0], right[0], first[0], second[0]),
+            [(shape, F32), (shape, F32), (shape, BF), (shape, F32), (shape, F32)],
+            [((2, 8 * SIDE, 128), F32)] * 4, name)
+        return [value[None] for value in outs]
+
+    mg, mn, mc, mf, ms = soap(sum_m, mlp_master, mlp_left, mlp_right, mlp_first, mlp_second, "soap_mlp")
+    ag, an, ac, af, as_ = soap(sum_a, attn_master, attn_left, attn_right, attn_first, attn_second, "soap_attn")
+    return (block_out[None], tokens_grad[None], gains_grad, biases_grad, outb_grad, qkv_grad, up_grad, rel_grad,
+            ag, mg, an, mn, ac, mc, af, as_, mf, ms)
+
+
+def solution(mesh):
+    return build(mesh)

time: 895 us -> 633 us (0.71); the launches traced: 886 us -> 633 us
  local copies, waits for them, and re-layouts: 271 us -> 6.81 us
  Pallas kernels: 0 us -> 207 us
  matrix products: 85.6 us -> 0 us
  other arithmetic: 65.2 us -> 3.04 us
  waiting for transfers between devices: 396 us -> 350 us
    pallas_call x0 -> x9, Pallas kernels: none -> 207 us  [call(): pl.pallas_call(body, out_shape=[jax.ShapeDtypeStruct(shape, kind) for sha...]
    reshape x22 -> x4, local copies, waits for them, and re-layouts: 144 us -> 1.49 us  [the longest x2 1.34 us: fast_local(): qb, ub = (qkv_bias.reshape(6, SIDE), up_bias.reshape(8, SIDE))]
    dot_general x36 -> x0, matrix products: 85.6 us -> none  [the longest x2 12.9 us: soap_step(): jnp.einsum('mtji,mtjk->mtik', left_square, grad_tiles.reshape(square), pr...]
    gather x4 -> x0, local copies, waits for them, and re-layouts: 56.5 us -> none  [the longest x1 19.2 us: local(): jnp.concatenate([retile(w_up_grad, tile_side), retile(w_down_grad, tile_s...]
    reduce_scatter x2, waiting for transfers between devices: 155 us -> 119 us  [the longest x1 89.9 us: fast_local(): sum_m = lax.psum_scatter(stack_m, 'dp', scatter_dimension=0, tiled=True)]
    another operation x14 -> x4, local copies, waits for them, and re-layouts: 22.7 us -> 0.36 us  [fast_local(): rel_hi, rel_lo = low_parts(jnp.tile(rel, (2, 2)))]
    reduce_sum x10 -> x2, other arithmetic: 19 us -> 1.21 us  [inverse_order(): jnp.sum(jnp.where(owner[:, None] == at[None, :], at[:, None], 0), axis=0)]
    psum x3, waiting for transfers between devices: 81.2 us -> 64.3 us  [the longest x1 34.2 us: fast_local(): down_sum = lax.psum(part_down, 'mp')]
  transfers between devices with their start and end apart: 7 -> 7, of which waited for: 6 -> 6; matrix products, arithmetic and copies ran while one was open for 18% -> 2% of each run, Pallas kernels for 0% -> 10%
where the time goes in v1:
time: 633 us
  waiting for transfers between devices  350 us (55%)
  Pallas kernels  207 us (33%)
  blocking collectives  50.9 us (8%)
  between operations  14.4 us (2%)
  local copies, waits for them, and re-layouts  6.81 us (1%)
    pallas_call x9, Pallas kernels, call(): pl.pallas_call(body, out_shape=[jax.ShapeDtypeStruct(shape, kind) for sha...  207 us
    all_gather x1, waiting for transfers between devices, fast_local(): all_m = lax.all_gather(wire_m, 'dp', axis=0, tiled=True)  105 us
    reduce_scatter x1, waiting for transfers between devices, fast_local(): sum_m = lax.psum_scatter(stack_m, 'dp', scatter_dimension=0, tiled=True)  89.9 us
    all_gather x1, waiting for transfers between devices, fast_local(): all_a = lax.all_gather(wire_a, 'dp', axis=0, tiled=True)  61 us
    psum x1, blocking collectives, fast_local(): lax.psum((jnp.stack([sums_one[0], sums_two[0]]), jnp.stack([sums_one[1],...  40.4 us
    psum x1, waiting for transfers between devices, fast_local(): down_sum = lax.psum(part_down, 'mp')  34.2 us
    psum x1, waiting for transfers between devices, fast_local(): branch = lax.psum(part, 'mp')  30.1 us
    reduce_scatter x1, waiting for transfers between devices, fast_local(): sum_a = lax.psum_scatter(stack_a, 'dp', scatter_dimension=0, tiled=True)  28.7 us
  transfers between devices with their start and end apart: 7, of which 6 were waited for; matrix products, arithmetic and copies ran while one was open for 2% of the time, Pallas kernels for 10%

profile of v1, /device:TPU:0, one launch (start us, length us, event | category | flops | bytes accessed | tf_op | source)
XLA Modules:
  0.0 632.6 jit_solution(3421631089028933101)
XLA Ops:
  7.3 14.3 %pack.1 = (bf16[10,160,128]{2,1,0:T(8,128)(2,1)}, bf16[20,160,128]{2,1,0:T(8,128)(2,1)}) custom-call(f32[8,25600]{1,0:T(8,128)} %bitcast.50, f32[16,25600]{1,0:T(8,128)} %bitcast.48), custom_call_target="tpu_custom_call" | custom-call | tf_op jit(solution)/shard_map/pack/pallas_call | solution.py:802
  21.8 0.1 tile.12
  22.0 0.1 copy.76
  22.1 0.8 copy.80.live
  22.9 0.7 reshape.65.qkv_bias
  23.6 0.1 copy.78.rel_hi
  23.7 0.6 select_reduce_fusion.1.order
  24.3 0.6 subtract_convert_fusion.rel_lo
  24.9 61.0 %all-gather.3.cloned.1.call-done.wire = bf16[80,160,128]{2,1,0:T(8,128)(2,1)} async-done(((bf16[10,160,128]{2,1,0:T(8,128)(2,1)}), bf16[80,160,128]{2,1,0:T(8,128)(2,1)}) %all-gather.3.cloned.1.call-update) | async-done | bytes 3276816 | tf_op jit(solution)/shard_map/all_gather | solution.py:854
  86.0 17.3 %attn_fwd.1 = (bf16[196,1280]{1,0:T(8,128)(2,1)}, bf16[208,1280]{1,0:T(8,128)(2,1)}, bf16[6,208,160]{2,1,0:T(8,128)(2,1)}, f32[4,208,208]{2,1,0:T(8,128)}, bf16[2,208,160]{2,1,0:T(8,128)(2,1)}) custom-call(s32[64]{0:T(128)} %select_reduce_fusion.1.order, bf16[196,1280]{1,0:T(8,128)(2,1)} %bitcast.44, f32[208,1]{1,0:T(8,128)} %copy.80.live, f32[2,1280]{1,0:T(2,128)} %gains.7, ...), custom_call_target="tpu_custom_call" | custom-call | tf_op jit(solution)/shard_map/attn_fwd/pallas_call | solution.py:802
  103.4 0.7 all-gather.5.cloned.1.call-update
  104.1 0.7 reshape.66.up_bias
  104.8 0.6 select_reduce_fusion.order
  105.4 30.1 %all-reduce.8.cloned.1.call-done.branch = bf16[196,1280]{1,0:T(8,128)(2,1)} async-done(((bf16[196,1280]{1,0:T(8,128)(2,1)}), bf16[196,1280]{1,0:T(8,128)(2,1)}) %all-reduce.8.cloned.1.call-update) | async-done | bytes 501776 | tf_op jit(solution)/shard_map/psum | solution.py:863
  135.5 104.9 %all-gather.5.cloned.1.call-done.wire = bf16[160,160,128]{2,1,0:T(8,128)(2,1)} async-done(((bf16[20,160,128]{2,1,0:T(8,128)(2,1)}), bf16[160,160,128]{2,1,0:T(8,128)(2,1)}) %all-gather.5.cloned.1.call-update) | async-done | bytes 6553616 | tf_op jit(solution)/shard_map/all_gather | solution.py:855
  240.4 25.2 %mlp.1 = (bf16[196,1280]{1,0:T(8,128)(2,1)}, bf16[196,1280]{1,0:T(8,128)(2,1)}, bf16[8,208,160]{2,1,0:T(8,128)(2,1)}, bf16[8,208,160]{2,1,0:T(8,128)(2,1)}, bf16...) custom-call(s32[128]{0:T(128)} %select_reduce_fusion.order, bf16[196,1280]{1,0:T(8,128)(2,1)} %bitcast.45, ...), custom_call_target="tpu_custom_call" | custom-call | tf_op jit(solution)/shard_map/mlp/pallas_call | solution.py:802
  265.6 0.2 all-reduce.10.cloned.1.call-start
  265.9 34.2 %all-reduce.12.cloned.1.call-done = (bf16[196,1280]{1,0:T(8,128)(2,1)}, bf16[196,1280]{1,0:T(8,128)(2,1)}) async-done(((bf16[196,1280]{1,0:T(8,128)(2,1)}, bf16[196,1280]{1,0:T(8,128)(2,1)}), (bf16[196,1280]{1,0:T(8,128)(2,1)}, bf16[196,1280]{1,0:T(8,128)(2,1)})) %all-reduce.12.cloned.1.call-update) | async-done | bytes 1003536 | tf_op jit(solution)/shard_map/psum | solution.py:871
  300.1 17.6 %mid_back.1 = (bf16[196,1280]{1,0:T(8,128)(2,1)}, f32[196,1280]{1,0:T(8,128)}, bf16[196,1280]{1,0:T(8,128)(2,1)}, f32[128,160]{1,0:T(8,128)}, bf16[6,208,160]{2,...) custom-call(s32[64]{0:T(128)} %select_reduce_fusion.1.order, ...), custom_call_target="tpu_custom_call" | custom-call | tf_op jit(solution)/shard_map/mid_back/pallas_call | solution.py:802
  317.7 0.5 compare_select_fusion.3
  318.2 9.9 %attn_tiles.1 = bf16[80,160,128]{2,1,0:T(8,128)(2,1)} custom-call(s32[64]{0:T(128)} %get-tuple-element.197.left_at, s32[64]{0:T(128)} %get-tuple-element.196.right_at, bf16[8,208,160]{2,1,0:T(8,128)(2,1)} %get-tuple-element.71.nb_ref, bf16[2,208,160]{2,1,0:T(8,128)(2,1)} %get-tuple-element.61.att.att_ref, bf16[6,208,160]{2,1,0:T(8,128)(2,1)} %get-tuple-element.72.gm_ref, ...), custom_call_target="tpu_custom_call" | custom-call | tf_op jit(solution)/shard_map/attn_tiles/pallas_call | solution.py:802
  328.2 0.5 fusion.1
  328.7 17.4 %mlp_tiles.1 = bf16[160,160,128]{2,1,0:T(8,128)(2,1)} custom-call(s32[128]{0:T(128)} %get-tuple-element.195.left_at, s32[128]{0:T(128)} %get-tuple-element.194.right_at, bf16[8,208,160]{2,1,0:T(8,128)(2,1)} %get-tuple-element.75.sec, bf16[8,208,160]{2,1,0:T(8,128)(2,1)} %get-tuple-element.76.act, bf16[8,208,160]{2,1,0:T(8,128)(2,1)} %get-tuple-element.77.gh_ref, ...), custom_call_target="tpu_custom_call" | custom-call | tf_op jit(solution)/shard_map/mlp_tiles/pallas_call | solution.py:802
  346.2 0.8 copy.82.live
  347.2 10.5 %psum.86 = bf16[2,27,80]{2,0,1:T(2,128)(2,1)S(1)} all-reduce(bf16[2,27,80]{2,0,1:T(2,128)(2,1)S(1)} %copy.85), channel_id=1, replica_groups=mesh['dp'=8,'mp'=4] {'mp'}, use_global_device_ids=true, to_apply=%region_11.12 | all-reduce | flops 4320 | bytes 17280 | tf_op jit(solution)/shard_map/psum | solution.py:896
  357.8 3.4 token_back.1
  361.2 3.2 copy.84
  364.5 40.4 %all-reduce.2 = (f32[2,1280]{1,0:T(2,128)}, f32[2,1280]{1,0:T(2,128)}, f32[2,1280]{1,0:T(2,128)}, f32[960]{0:T(1024)}, f32[1280]{0:T(1024)}, /*index=5*/f32[2,27,80]{2,0,1:T(2,128)}) all-reduce(f32[2,1280]{1,0:T(2,128)S(1)} %get-tuple-element.198, f32[2,1280]{1,0:T(2,128)S(1)} %get-tuple-element.199, ...), channel_id=1, replica_groups=mesh['dp'=8,'mp'=4] {'dp'}, use_global_device_ids=true, to_apply=%region_6.7 | all-reduce | flops 14240 | bytes 105280 | tf_op jit(solution)/shard_map/psum | solution.py:910
  404.9 28.7 %reduce-scatter.3.cloned.1.call-done.wire = bf16[10,160,128]{2,1,0:T(8,128)(2,1)} async-done(((bf16[80,160,128]{2,1,0:T(8,128)(2,1)}), bf16[10,160,128]{2,1,0:T(8,128)(2,1)}) %reduce-scatter.3.cloned.1.call-update) | async-done | bytes 409616 | tf_op jit(solution)/shard_map/reduce_scatter | solution.py:906
  433.6 34.6 %soap_attn.1 = (f32[8,25600]{1,0:T(8,128)}, f32[8,25600]{1,0:T(8,128)}, bf16[8,25600]{1,0:T(8,128)(2,1)}, f32[8,25600]{1,0:T(8,128)}, f32[8,25600]{1,0:T(8,128)}) custom-call(bf16[10,160,128]{2,1,0:T(8,128)(2,1)} %reduce-scatter.3.cloned.1.call-done.wire, f32[8,25600]{1,0:T(8,128)} %bitcast.51, f32[8,25600]{1,0:T(8,128)} %bitcast.59, f32[8,25600]{1,0:T(8,128)} %bitcast.60, ...), custom_call_target="tpu_custom_call" | custom-call | tf_op jit(solution)/shard_map/soap_attn/pallas_call | solution.py:802
  468.2 89.9 %reduce-scatter.5.cloned.1.call-done.wire = bf16[20,160,128]{2,1,0:T(8,128)(2,1)} async-done(((bf16[160,160,128]{2,1,0:T(8,128)(2,1)}), bf16[20,160,128]{2,1,0:T(8,128)(2,1)}) %reduce-scatter.5.cloned.1.call-update) | async-done | bytes 819216 | tf_op jit(solution)/shard_map/reduce_scatter | solution.py:881
  558.1 67.6 %soap_mlp.1 = (f32[16,25600]{1,0:T(8,128)}, f32[16,25600]{1,0:T(8,128)}, bf16[16,25600]{1,0:T(8,128)(2,1)}, f32[16,25600]{1,0:T(8,128)}, f32[16,25600]{1,0:T(8,128)}) custom-call(bf16[20,160,128]{2,1,0:T(8,128)(2,1)} %reduce-scatter.5.cloned.1.call-done.wire, f32[16,25600]{1,0:T(8,128)} %bitcast.49, f32[16,25600]{1,0:T(8,128)} %bitcast.54, ...), custom_call_target="tpu_custom_call" | custom-call | tf_op jit(solution)/shard_map/soap_mlp/pallas_call | solution.py:802
  (53 shorter events, 0.9 us)
Async XLA Ops:
  7.2 14.5 %copy-start.2 = (f32[2,27,80]{2,0,1:T(2,128)S(1)}, f32[2,27,80]{2,0,1:T(2,128)}, u32[]{:S(2)}) copy-start(f32[2,27,80]{2,0,1:T(2,128)} %param.31) | copy-start | bytes 51844
  7.2 78.8 %all-gather.3.cloned.1.call-start = ((), (), s32[]{:S(2)}) async-start(), calls=%async_computation.2 | async-start | bytes 3686400 | tf_op jit(solution)/shard_map/all_gather | solution.py:854
  7.2 14.9 %copy-start.9 = (s32[1,196]{1,0:T(1,128)S(1)}, s32[1,196]{1,0:T(1,128)}, u32[]{:S(2)}) copy-start(s32[1,196]{1,0:T(1,128)} %param.24) | copy-start | bytes 2356
  7.3 15.7 %copy-start.8 = (f32[960]{0:T(1024)S(1)}, f32[960]{0:T(1024)}, u32[]{:S(2)}) copy-start(f32[960]{0:T(1024)} %param.29) | copy-start | bytes 11524
  7.3 16.4 %copy-start.10 = (s32[1,64]{1,0:T(1,128)S(1)}, s32[1,64]{1,0:T(1,128)}, u32[]{:S(2)}) copy-start(s32[1,64]{1,0:T(1,128)} %param.32) | copy-start | bytes 772
  21.6 113.9 %all-reduce.8.cloned.1.call-start = ((), (), s32[]{:S(2)}) async-start(), calls=%async_computation.3 | async-start | bytes 1024000 | tf_op jit(solution)/shard_map/psum | solution.py:863
  23.7 62.3 %copy-start = (bf16[128,160]{1,0:T(8,128)(2,1)}, bf16[128,160]{1,0:T(8,128)(2,1)S(1)}, u32[]{:S(2)}) copy-start(bf16[128,160]{1,0:T(8,128)(2,1)S(1)} %copy.78.rel_hi) | copy-start | bytes 122884
  86.0 18.2 %copy-start.6 = (f32[1280]{0:T(1024)S(1)}, f32[1280]{0:T(1024)}, u32[]{:S(2)}) copy-start(f32[1280]{0:T(1024)} %param.30) | copy-start | bytes 15364
  86.0 18.8 %copy-start.11 = (s32[1,128]{1,0:T(1,128)S(1)}, s32[1,128]{1,0:T(1,128)}, u32[]{:S(2)}) copy-start(s32[1,128]{1,0:T(1,128)} %param.33) | copy-start | bytes 1540
  103.4 137.1 %all-gather.5.cloned.1.call-start = ((), (), s32[]{:S(2)}) async-start(), calls=%async_computation.4 | async-start | bytes 7372800 | tf_op jit(solution)/shard_map/all_gather | solution.py:855
  104.1 196.0 %all-reduce.12.cloned.1.call-start = ((), (), s32[]{:S(2)}) async-start(), calls=%async_computation.8 | async-start | bytes 2048000 | tf_op jit(solution)/shard_map/psum | solution.py:871
  265.6 92.1 %all-reduce.10.cloned.1.call-start = ((), (), s32[]{:S(2)}) async-start(), calls=%async_computation.5 | async-start | bytes 1024000 | tf_op jit(solution)/shard_map/psum | solution.py:895
  317.7 115.9 %reduce-scatter.3.cloned.1.call-start = ((), (), s32[]{:S(2)}) async-start(), calls=%async_computation.6 | async-start | bytes 3686400 | tf_op jit(solution)/shard_map/reduce_scatter | solution.py:906
  328.2 229.9 %reduce-scatter.5.cloned.1.call-start = ((), (), s32[]{:S(2)}) async-start(), calls=%async_computation.7 | async-start | bytes 7372800 | tf_op jit(solution)/shard_map/reduce_scatter | solution.py:881
  346.1 0.8 copy-start.7
  346.1 0.9 copy-start.5
  346.1 1.0 copy-start.1
  346.1 11.6 %copy-start.3 = (f32[4,1280]{1,0:T(4,128)S(1)}, f32[4,1280]{1,0:T(4,128)}, u32[]{:S(2)}) copy-start(f32[4,1280]{1,0:T(4,128)} %get-tuple-element.67) | copy-start | bytes 61444
  361.2 3.2 copy-start.4
Sparse Core Ops, SparseCore 0:
  21.7 64.1 all-gather.2
  103.5 31.9 all-reduce.7
  138.3 102.1 all-gather.4
  265.8 34.2 all-reduce.11
  317.8 33.9 all-reduce.9
  355.3 78.2 reduce-scatter.2
  437.2 120.8 reduce-scatter.4

commit v2 on v1

--- a/solution.py
+++ b/solution.py
@@ -342,11 +342,10 @@
     return high, (value - high.astype(F32)).astype(BF)
 
 
-def flat_to_square(read, square, count):
-    lane = lane_at((count, 128))
-
-    def body(group, carry):
-        base = pl.multiple_of(group * 640, 128)
+def flat_to_square(read, square, count=8):
+    lane = lane_at((8, 128))
+
+    def rows_of(base):
         x = [read(base + 128 * k) for k in range(5)]
         r1 = pltpu.roll(x[1], 96, 1)
         r2 = pltpu.roll(x[2], 96, 1)
@@ -354,58 +353,67 @@
         h3 = pltpu.roll(x[3], 64, 1)
         r3 = pltpu.roll(x[3], 32, 1)
         r4 = pltpu.roll(x[4], 32, 1)
-        pairs = (
+        return (
             (x[0], x[1]),
             (jnp.where(lane < 96, r1, r2), r2),
             (jnp.where(lane < 64, h2, h3), h3),
             (jnp.where(lane < 32, r3, r4), r4),
         )
-        for m, (wide, narrow) in enumerate(pairs):
-            square[0, pl.ds(4 * group + m, count, stride=SIDE), :] = wide
-            square[1, pl.ds(4 * group + m, count, stride=SIDE), :] = narrow
-        return carry
-
-    lax.fori_loop(0, 40, body, 0)
-
-
-def square_to_flat(square, write, count):
-    lane = lane_at((count, 128))
 
     def body(group, carry):
-        base = pl.multiple_of(group * 640, 128)
-        a = [square[0, pl.ds(4 * group + m, count, stride=SIDE), :] for m in range(4)]
-        b = [square[1, pl.ds(4 * group + m, count, stride=SIDE), :] for m in range(4)]
-        a1 = pltpu.roll(a[1], 32, 1)
-        b1 = pltpu.roll(b[1], 32, 1)
-        a2 = pltpu.roll(a[2], 64, 1)
-        b2 = pltpu.roll(b[2], 64, 1)
-        a3 = pltpu.roll(a[3], 96, 1)
-        b3 = pltpu.roll(b[3], 96, 1)
-        write(base, a[0])
-        write(base + 128, jnp.where(lane < 32, b[0], a1))
-        write(base + 256, jnp.where(lane < 32, a1, jnp.where(lane < 64, b1, a2)))
-        write(base + 384, jnp.where(lane < 64, a2, jnp.where(lane < 96, b2, a3)))
-        write(base + 512, jnp.where(lane < 96, a3, b3))
-        return carry
-
-    lax.fori_loop(0, 40, body, 0)
+        base = pl.multiple_of(group * 1280, 128)
+        rows = rows_of(base) + rows_of(base + 640)
+        for part in range(2):
+            stacked = jnp.stack([row[part] for row in rows], axis=0)
+            square[part, :, pl.ds(pl.multiple_of(8 * group, 8), 8), :] = jnp.swapaxes(stacked, 0, 1)
+        return carry
+
+    lax.fori_loop(0, 20, body, 0)
+
+
+def square_to_flat(square, write, count=8):
+    lane = lane_at((8, 128))
+
+    def body(group, carry):
+        at = pl.ds(pl.multiple_of(8 * group, 8), 8)
+        wide = jnp.swapaxes(square[0, :, at, :], 0, 1)
+        narrow = jnp.swapaxes(square[1, :, at, :], 0, 1)
+        for half in range(2):
+            base = pl.multiple_of(group * 1280, 128) + 640 * half
+            a = [wide[4 * half + m] for m in range(4)]
+            b = [narrow[4 * half + m] for m in range(4)]
+            a1 = pltpu.roll(a[1], 32, 1)
+            b1 = pltpu.roll(b[1], 32, 1)
+            a2 = pltpu.roll(a[2], 64, 1)
+            b2 = pltpu.roll(b[2], 64, 1)
+            a3 = pltpu.roll(a[3], 96, 1)
+            b3 = pltpu.roll(b[3], 96, 1)
+            write(base, a[0])
+            write(base + 128, jnp.where(lane < 32, b[0], a1))
+            write(base + 256, jnp.where(lane < 32, a1, jnp.where(lane < 64, b1, a2)))
+            write(base + 384, jnp.where(lane < 64, a2, jnp.where(lane < 96, b2, a3)))
+            write(base + 512, jnp.where(lane < 96, a3, b3))
+        return carry
+
+    lax.fori_loop(0, 20, body, 0)
+
+
+def pack_eight(source, first, wire, base, square):
+    lane = lane_at((SIDE, 128))
+    flat_to_square(lambda at: source[first : first + 8, pl.ds(at, 128)], square)
+    for half in range(2):
+        spare = None
+        for q in range(4):
+            wire[base + 5 * half + q] = square[0, 4 * half + q].astype(BF)
+            piece = square[1, 4 * half + q]
+            spare = piece if q == 0 else jnp.where(lane < 32 * q, spare, pltpu.roll(piece, 32 * q, 1))
+        wire[base + 5 * half + 4] = spare.astype(BF)
 
 
 def pack_body(attn, mlp, wire_attn, wire_mlp, square):
-    lane = lane_at((SIDE, 128))
-    for source, first, target, slot in ((attn, 0, wire_attn, 0), (mlp, 0, wire_mlp, 0), (mlp, 8, wire_mlp, 2)):
-        flat_to_square(lambda at, s=source, f=first: s[f : f + 8, pl.ds(at, 128)], square, 8)
-        for half in range(2):
-            spare = None
-            for q in range(4):
-                row = (4 * half + q) * SIDE
-                target[5 * (slot + half) + q] = square[0, row : row + SIDE, :].astype(BF)
-                piece = square[1, row : row + SIDE, :]
-                if q == 0:
-                    spare = piece
-                else:
-                    spare = jnp.where(lane < 32 * q, spare, pltpu.roll(piece, 32 * q, 1))
-            target[5 * (slot + half) + 4] = spare.astype(BF)
+    pack_eight(attn, 0, wire_attn, 0, square)
+    pack_eight(mlp, 0, wire_mlp, 0, square)
+    pack_eight(mlp, 8, wire_mlp, 10, square)
 
 
 def unpack_narrow(wire, narrow, groups):
@@ -663,14 +671,12 @@
 
 
 def square_tile(square, t):
-    row = pl.multiple_of(t * SIDE, 32)
-    return jnp.concatenate([square[0, pl.ds(row, SIDE), :], square[1, pl.ds(row, SIDE), 0:32]], axis=1)
+    return jnp.concatenate([square[0, t], square[1, t, :, 0:32]], axis=1)
 
 
 def put_tile(square, t, value):
-    row = pl.multiple_of(t * SIDE, 32)
-    square[0, pl.ds(row, SIDE), :] = value[:, 0:128]
-    square[1, pl.ds(row, SIDE), 0:32] = value[:, 128:160]
+    square[0, t] = value[:, 0:128]
+    square[1, t, :, 0:32] = value[:, 128:160]
 
 
 def split_dot(kind, a, b):
@@ -734,9 +740,8 @@
         for half in range(2):
             last = wire[5 * (2 * r + half) + 4].astype(F32)
             for q in range(4):
-                row = (4 * half + q) * SIDE
-                sq_grad[0, row : row + SIDE, :] = wire[5 * (2 * r + half) + q].astype(F32)
-                sq_grad[1, row : row + SIDE, :] = last if q == 0 else pltpu.roll(last, 128 - 32 * q, 1)
+                sq_grad[0, 4 * half + q] = wire[5 * (2 * r + half) + q].astype(F32)
+                sq_grad[1, 4 * half + q] = last if q == 0 else pltpu.roll(last, 128 - 32 * q, 1)
         soap_group(8 * r, sq_grad, master, left, right, first, second,
                    grad_out, new_out, copy_out, first_out, second_out, sq_left, sq_right, sq_work)
 
@@ -850,7 +855,7 @@
 
     wire_a, wire_m = call(
         pack_body, (), (attn_master[0], mlp_master[0]),
-        [((10, SIDE, 128), BF), ((20, SIDE, 128), BF)], [((2, 8 * SIDE, 128), F32)], "pack")
+        [((10, SIDE, 128), BF), ((20, SIDE, 128), BF)], [((2, 8, SIDE, 128), F32)], "pack")
     all_a = lax.all_gather(wire_a, "dp", axis=0, tiled=True)
     all_m = lax.all_gather(wire_m, "dp", axis=0, tiled=True)
 
@@ -924,7 +929,7 @@
         outs = call(
             soap_body, (), (wire, master[0], left[0], right[0], first[0], second[0]),
             [(shape, F32), (shape, F32), (shape, BF), (shape, F32), (shape, F32)],
-            [((2, 8 * SIDE, 128), F32)] * 4, name)
+            [((2, 8, SIDE, 128), F32)] * 4, name)
         return [value[None] for value in outs]
 
     mg, mn, mc, mf, ms = soap(sum_m, mlp_master, mlp_left, mlp_right, mlp_first, mlp_second, "soap_mlp")

time: 633 us -> 605 us (0.956)
  Pallas kernels: 207 us -> 169 us
  waiting for transfers between devices: 350 us -> 361 us
    pallas_call x9, Pallas kernels: 207 us -> 169 us  [call(): pl.pallas_call(body, out_shape=[jax.ShapeDtypeStruct(shape, kind) for sha...]
    reduce_scatter x1, waiting for transfers between devices: 89.9 us -> 101 us  [fast_local(): sum_m = lax.psum_scatter(stack_m, 'dp', scatter_dimension=0, tiled=True)]
  transfers between devices with their start and end apart: 7 -> 7, of which waited for: 6 -> 6; matrix products, arithmetic and copies ran while one was open for 2% -> 2% of each run, Pallas kernels for 10% -> 9%
where the time goes in v2:
time: 605 us
  waiting for transfers between devices  361 us (60%)
  Pallas kernels  169 us (28%)
  blocking collectives  50.8 us (8%)
  between operations  14.4 us (2%)
  local copies, waits for them, and re-layouts  6.81 us (1%)
    pallas_call x9, Pallas kernels, call(): pl.pallas_call(body, out_shape=[jax.ShapeDtypeStruct(shape, kind) for sha...  169 us
    all_gather x1, waiting for transfers between devices, fast_local(): all_m = lax.all_gather(wire_m, 'dp', axis=0, tiled=True)  105 us
    reduce_scatter x1, waiting for transfers between devices, fast_local(): sum_m = lax.psum_scatter(stack_m, 'dp', scatter_dimension=0, tiled=True)  101 us
    all_gather x1, waiting for transfers between devices, fast_local(): all_a = lax.all_gather(wire_a, 'dp', axis=0, tiled=True)  61 us
    psum x1, blocking collectives, fast_local(): lax.psum((jnp.stack([sums_one[0], sums_two[0]]), jnp.stack([sums_one[1],...  40.3 us
    psum x1, waiting for transfers between devices, fast_local(): down_sum = lax.psum(part_down, 'mp')  34.2 us
    psum x1, waiting for transfers between devices, fast_local(): branch = lax.psum(part, 'mp')  30 us
    reduce_scatter x1, waiting for transfers between devices, fast_local(): sum_a = lax.psum_scatter(stack_a, 'dp', scatter_dimension=0, tiled=True)  28.9 us
  transfers between devices with their start and end apart: 7, of which 6 were waited for; matrix products, arithmetic and copies ran while one was open for 2% of the time, Pallas kernels for 9%

profile of v2, /device:TPU:0, one launch (start us, length us, event | category | flops | bytes accessed | tf_op | source)
XLA Modules:
  0.0 604.8 jit_solution(15031193466145897379)
XLA Ops:
  7.3 8.6 %pack.1 = (bf16[10,160,128]{2,1,0:T(8,128)(2,1)}, bf16[20,160,128]{2,1,0:T(8,128)(2,1)}) custom-call(f32[8,25600]{1,0:T(8,128)} %bitcast.50, f32[16,25600]{1,0:T(8,128)} %bitcast.48), custom_call_target="tpu_custom_call" | custom-call | tf_op jit(solution)/shard_map/pack/pallas_call | solution.py:807
  16.1 0.1 tile.12
  16.2 0.1 copy.76
  16.4 0.8 copy.80.live
  17.1 0.7 reshape.65.qkv_bias
  17.8 0.1 copy.78.rel_hi
  17.9 0.6 select_reduce_fusion.1.order
  18.5 0.6 subtract_convert_fusion.rel_lo
  19.2 61.0 %all-gather.3.cloned.1.call-done.wire = bf16[80,160,128]{2,1,0:T(8,128)(2,1)} async-done(((bf16[10,160,128]{2,1,0:T(8,128)(2,1)}), bf16[80,160,128]{2,1,0:T(8,128)(2,1)}) %all-gather.3.cloned.1.call-update) | async-done | bytes 3276816 | tf_op jit(solution)/shard_map/all_gather | solution.py:859
  80.2 17.3 %attn_fwd.1 = (bf16[196,1280]{1,0:T(8,128)(2,1)}, bf16[208,1280]{1,0:T(8,128)(2,1)}, bf16[6,208,160]{2,1,0:T(8,128)(2,1)}, f32[4,208,208]{2,1,0:T(8,128)}, bf16[2,208,160]{2,1,0:T(8,128)(2,1)}) custom-call(s32[64]{0:T(128)} %select_reduce_fusion.1.order, bf16[196,1280]{1,0:T(8,128)(2,1)} %bitcast.44, f32[208,1]{1,0:T(8,128)} %copy.80.live, f32[2,1280]{1,0:T(2,128)} %gains.7, ...), custom_call_target="tpu_custom_call" | custom-call | tf_op jit(solution)/shard_map/attn_fwd/pallas_call | solution.py:807
  97.6 0.7 all-gather.5.cloned.1.call-update
  98.4 0.7 reshape.66.up_bias
  99.1 0.6 select_reduce_fusion.order
  99.7 30.0 %all-reduce.8.cloned.1.call-done.branch = bf16[196,1280]{1,0:T(8,128)(2,1)} async-done(((bf16[196,1280]{1,0:T(8,128)(2,1)}), bf16[196,1280]{1,0:T(8,128)(2,1)}) %all-reduce.8.cloned.1.call-update) | async-done | bytes 501776 | tf_op jit(solution)/shard_map/psum | solution.py:868
  129.7 104.9 %all-gather.5.cloned.1.call-done.wire = bf16[160,160,128]{2,1,0:T(8,128)(2,1)} async-done(((bf16[20,160,128]{2,1,0:T(8,128)(2,1)}), bf16[160,160,128]{2,1,0:T(8,128)(2,1)}) %all-gather.5.cloned.1.call-update) | async-done | bytes 6553616 | tf_op jit(solution)/shard_map/all_gather | solution.py:860
  234.6 25.2 %mlp.1 = (bf16[196,1280]{1,0:T(8,128)(2,1)}, bf16[196,1280]{1,0:T(8,128)(2,1)}, bf16[8,208,160]{2,1,0:T(8,128)(2,1)}, bf16[8,208,160]{2,1,0:T(8,128)(2,1)}, bf16...) custom-call(s32[128]{0:T(128)} %select_reduce_fusion.order, bf16[196,1280]{1,0:T(8,128)(2,1)} %bitcast.45, ...), custom_call_target="tpu_custom_call" | custom-call | tf_op jit(solution)/shard_map/mlp/pallas_call | solution.py:807
  259.9 0.2 all-reduce.10.cloned.1.call-start
  260.1 34.2 %all-reduce.12.cloned.1.call-done = (bf16[196,1280]{1,0:T(8,128)(2,1)}, bf16[196,1280]{1,0:T(8,128)(2,1)}) async-done(((bf16[196,1280]{1,0:T(8,128)(2,1)}, bf16[196,1280]{1,0:T(8,128)(2,1)}), (bf16[196,1280]{1,0:T(8,128)(2,1)}, bf16[196,1280]{1,0:T(8,128)(2,1)})) %all-reduce.12.cloned.1.call-update) | async-done | bytes 1003536 | tf_op jit(solution)/shard_map/psum | solution.py:876
  294.3 17.5 %mid_back.1 = (bf16[196,1280]{1,0:T(8,128)(2,1)}, f32[196,1280]{1,0:T(8,128)}, bf16[196,1280]{1,0:T(8,128)(2,1)}, f32[128,160]{1,0:T(8,128)}, bf16[6,208,160]{2,...) custom-call(s32[64]{0:T(128)} %select_reduce_fusion.1.order, ...), custom_call_target="tpu_custom_call" | custom-call | tf_op jit(solution)/shard_map/mid_back/pallas_call | solution.py:807
  311.9 0.5 compare_select_fusion.3
  312.4 9.9 %attn_tiles.1 = bf16[80,160,128]{2,1,0:T(8,128)(2,1)} custom-call(s32[64]{0:T(128)} %get-tuple-element.197.left_at, s32[64]{0:T(128)} %get-tuple-element.196.right_at, bf16[8,208,160]{2,1,0:T(8,128)(2,1)} %get-tuple-element.71.nb_ref, bf16[2,208,160]{2,1,0:T(8,128)(2,1)} %get-tuple-element.61.att.att_ref, bf16[6,208,160]{2,1,0:T(8,128)(2,1)} %get-tuple-element.72.gm_ref, ...), custom_call_target="tpu_custom_call" | custom-call | tf_op jit(solution)/shard_map/attn_tiles/pallas_call | solution.py:807
  322.4 0.5 fusion.1
  322.9 17.4 %mlp_tiles.1 = bf16[160,160,128]{2,1,0:T(8,128)(2,1)} custom-call(s32[128]{0:T(128)} %get-tuple-element.195.left_at, s32[128]{0:T(128)} %get-tuple-element.194.right_at, bf16[8,208,160]{2,1,0:T(8,128)(2,1)} %get-tuple-element.75.sec, bf16[8,208,160]{2,1,0:T(8,128)(2,1)} %get-tuple-element.76.act, bf16[8,208,160]{2,1,0:T(8,128)(2,1)} %get-tuple-element.77.gh_ref, ...), custom_call_target="tpu_custom_call" | custom-call | tf_op jit(solution)/shard_map/mlp_tiles/pallas_call | solution.py:807
  340.4 0.8 copy.82.live
  341.4 10.5 %psum.86 = bf16[2,27,80]{2,0,1:T(2,128)(2,1)S(1)} all-reduce(bf16[2,27,80]{2,0,1:T(2,128)(2,1)S(1)} %copy.85), channel_id=1, replica_groups=mesh['dp'=8,'mp'=4] {'mp'}, use_global_device_ids=true, to_apply=%region_11.12 | all-reduce | flops 4320 | bytes 17280 | tf_op jit(solution)/shard_map/psum | solution.py:901
  352.0 3.4 token_back.1
  355.4 3.2 copy.84
  358.7 40.3 %all-reduce.2 = (f32[2,1280]{1,0:T(2,128)}, f32[2,1280]{1,0:T(2,128)}, f32[2,1280]{1,0:T(2,128)}, f32[960]{0:T(1024)}, f32[1280]{0:T(1024)}, /*index=5*/f32[2,27,80]{2,0,1:T(2,128)}) all-reduce(f32[2,1280]{1,0:T(2,128)S(1)} %get-tuple-element.198, f32[2,1280]{1,0:T(2,128)S(1)} %get-tuple-element.199, ...), channel_id=1, replica_groups=mesh['dp'=8,'mp'=4] {'dp'}, use_global_device_ids=true, to_apply=%region_6.7 | all-reduce | flops 14240 | bytes 105280 | tf_op jit(solution)/shard_map/psum | solution.py:915
  398.9 28.9 %reduce-scatter.3.cloned.1.call-done.wire = bf16[10,160,128]{2,1,0:T(8,128)(2,1)} async-done(((bf16[80,160,128]{2,1,0:T(8,128)(2,1)}), bf16[10,160,128]{2,1,0:T(8,128)(2,1)}) %reduce-scatter.3.cloned.1.call-update) | async-done | bytes 409616 | tf_op jit(solution)/shard_map/reduce_scatter | solution.py:911
  427.9 23.7 %soap_attn.1 = (f32[8,25600]{1,0:T(8,128)}, f32[8,25600]{1,0:T(8,128)}, bf16[8,25600]{1,0:T(8,128)(2,1)}, f32[8,25600]{1,0:T(8,128)}, f32[8,25600]{1,0:T(8,128)}) custom-call(bf16[10,160,128]{2,1,0:T(8,128)(2,1)} %reduce-scatter.3.cloned.1.call-done.wire, f32[8,25600]{1,0:T(8,128)} %bitcast.51, f32[8,25600]{1,0:T(8,128)} %bitcast.59, f32[8,25600]{1,0:T(8,128)} %bitcast.60, ...), custom_call_target="tpu_custom_call" | custom-call | tf_op jit(solution)/shard_map/soap_attn/pallas_call | solution.py:807
  451.5 100.8 %reduce-scatter.5.cloned.1.call-done.wire = bf16[20,160,128]{2,1,0:T(8,128)(2,1)} async-done(((bf16[160,160,128]{2,1,0:T(8,128)(2,1)}), bf16[20,160,128]{2,1,0:T(8,128)(2,1)}) %reduce-scatter.5.cloned.1.call-update) | async-done | bytes 819216 | tf_op jit(solution)/shard_map/reduce_scatter | solution.py:886
  552.3 45.7 %soap_mlp.1 = (f32[16,25600]{1,0:T(8,128)}, f32[16,25600]{1,0:T(8,128)}, bf16[16,25600]{1,0:T(8,128)(2,1)}, f32[16,25600]{1,0:T(8,128)}, f32[16,25600]{1,0:T(8,128)}) custom-call(bf16[20,160,128]{2,1,0:T(8,128)(2,1)} %reduce-scatter.5.cloned.1.call-done.wire, f32[16,25600]{1,0:T(8,128)} %bitcast.49, f32[16,25600]{1,0:T(8,128)} %bitcast.54, ...), custom_call_target="tpu_custom_call" | custom-call | tf_op jit(solution)/shard_map/soap_mlp/pallas_call | solution.py:807
  (53 shorter events, 0.9 us)
Async XLA Ops:
  7.2 8.7 %copy-start.2 = (f32[2,27,80]{2,0,1:T(2,128)S(1)}, f32[2,27,80]{2,0,1:T(2,128)}, u32[]{:S(2)}) copy-start(f32[2,27,80]{2,0,1:T(2,128)} %param.31) | copy-start | bytes 51844
  7.2 73.0 %all-gather.3.cloned.1.call-start = ((), (), s32[]{:S(2)}) async-start(), calls=%async_computation.2 | async-start | bytes 3686400 | tf_op jit(solution)/shard_map/all_gather | solution.py:859
  7.2 9.1 %copy-start.9 = (s32[1,196]{1,0:T(1,128)S(1)}, s32[1,196]{1,0:T(1,128)}, u32[]{:S(2)}) copy-start(s32[1,196]{1,0:T(1,128)} %param.24) | copy-start | bytes 2356
  7.3 9.9 %copy-start.8 = (f32[960]{0:T(1024)S(1)}, f32[960]{0:T(1024)}, u32[]{:S(2)}) copy-start(f32[960]{0:T(1024)} %param.29) | copy-start | bytes 11524
  7.3 10.7 %copy-start.10 = (s32[1,64]{1,0:T(1,128)S(1)}, s32[1,64]{1,0:T(1,128)}, u32[]{:S(2)}) copy-start(s32[1,64]{1,0:T(1,128)} %param.32) | copy-start | bytes 772
  15.9 113.8 %all-reduce.8.cloned.1.call-start = ((), (), s32[]{:S(2)}) async-start(), calls=%async_computation.3 | async-start | bytes 1024000 | tf_op jit(solution)/shard_map/psum | solution.py:868
  17.9 62.3 %copy-start = (bf16[128,160]{1,0:T(8,128)(2,1)}, bf16[128,160]{1,0:T(8,128)(2,1)S(1)}, u32[]{:S(2)}) copy-start(bf16[128,160]{1,0:T(8,128)(2,1)S(1)} %copy.78.rel_hi) | copy-start | bytes 122884
  80.2 18.2 %copy-start.6 = (f32[1280]{0:T(1024)S(1)}, f32[1280]{0:T(1024)}, u32[]{:S(2)}) copy-start(f32[1280]{0:T(1024)} %param.30) | copy-start | bytes 15364
  80.2 18.8 %copy-start.11 = (s32[1,128]{1,0:T(1,128)S(1)}, s32[1,128]{1,0:T(1,128)}, u32[]{:S(2)}) copy-start(s32[1,128]{1,0:T(1,128)} %param.33) | copy-start | bytes 1540
  97.6 137.0 %all-gather.5.cloned.1.call-start = ((), (), s32[]{:S(2)}) async-start(), calls=%async_computation.4 | async-start | bytes 7372800 | tf_op jit(solution)/shard_map/all_gather | solution.py:860
  98.3 196.0 %all-reduce.12.cloned.1.call-start = ((), (), s32[]{:S(2)}) async-start(), calls=%async_computation.8 | async-start | bytes 2048000 | tf_op jit(solution)/shard_map/psum | solution.py:876
  259.9 92.1 %all-reduce.10.cloned.1.call-start = ((), (), s32[]{:S(2)}) async-start(), calls=%async_computation.5 | async-start | bytes 1024000 | tf_op jit(solution)/shard_map/psum | solution.py:900
  311.9 116.0 %reduce-scatter.3.cloned.1.call-start = ((), (), s32[]{:S(2)}) async-start(), calls=%async_computation.6 | async-start | bytes 3686400 | tf_op jit(solution)/shard_map/reduce_scatter | solution.py:911
  322.4 229.9 %reduce-scatter.5.cloned.1.call-start = ((), (), s32[]{:S(2)}) async-start(), calls=%async_computation.7 | async-start | bytes 7372800 | tf_op jit(solution)/shard_map/reduce_scatter | solution.py:886
  340.3 0.8 copy-start.7
  340.3 0.9 copy-start.5
  340.3 1.0 copy-start.1
  340.3 11.6 %copy-start.3 = (f32[4,1280]{1,0:T(4,128)S(1)}, f32[4,1280]{1,0:T(4,128)}, u32[]{:S(2)}) copy-start(f32[4,1280]{1,0:T(4,128)} %get-tuple-element.67) | copy-start | bytes 61444
  355.4 3.2 copy-start.4
Sparse Core Ops, SparseCore 0:
  16.0 64.1 all-gather.2
  97.7 31.9 all-reduce.7
  132.5 102.1 all-gather.4
  260.0 34.2 all-reduce.11
  312.0 34.1 all-reduce.9
  349.7 78.1 reduce-scatter.2
  431.5 120.7 reduce-scatter.4

commit v3 on v2

--- a/solution.py
+++ b/solution.py
@@ -439,6 +439,94 @@
     lax.fori_loop(0, rows * cols, body, 0)
 
 
+MESH_ID = pl.DeviceIdType.MESH
+PIECE = 5
+
+
+def gather_body(wire, out, send_sem, recv_sem, own_sem):
+    count = wire.shape[0]
+    pieces = count // PIECE
+    me = lax.axis_index("dp")
+    z, x = me // 2, me % 2
+    side = me + 1 - 2 * x
+    up, down = jnp.minimum(me + 2, 6 + x), jnp.maximum(me - 2, x)
+
+    barrier = pltpu.get_barrier_semaphore()
+
+    def greet(target):
+        pl.semaphore_signal(barrier, inc=1, device_id={"dp": target}, device_id_type=MESH_ID)
+
+    greet(side)
+    pl.when(z < 3)(lambda: greet(up))
+    pl.when(z > 0)(lambda: greet(down))
+    inner = (z > 0) & (z < 3)
+    pl.when(inner)(lambda: pl.semaphore_wait(barrier, 3))
+    pl.when(jnp.logical_not(inner))(lambda: pl.semaphore_wait(barrier, 2))
+
+    def copy(way, target, origin, k, own=False):
+        place = out.at[pl.ds(origin * count + PIECE * k, PIECE)]
+        return pltpu.make_async_remote_copy(
+            src_ref=wire.at[pl.ds(PIECE * k, PIECE)] if own else place,
+            dst_ref=place,
+            send_sem=send_sem.at[way, origin // 2, k],
+            recv_sem=recv_sem.at[origin, k],
+            device_id={"dp": target},
+            device_id_type=MESH_ID,
+        )
+
+    for k in range(pieces):
+        copy(0, side, me, k, True).start()
+        pl.when(z < 3)(lambda k=k: copy(1, up, me, k, True).start())
+        pl.when(z > 0)(lambda k=k: copy(2, down, me, k, True).start())
+    keep = pltpu.make_async_copy(wire, out.at[pl.ds(me * count, count)], own_sem)
+    keep.start()
+
+    for d in range(1, 4):
+        for k in range(pieces):
+            def from_below():
+                origin = me - 2 * d
+                copy(1, up, origin, k).wait_recv()
+                copy(0, side, origin, k).start()
+                pl.when(z < 3)(lambda: copy(1, up, origin, k).start())
+
+            def from_above():
+                origin = me + 2 * d
+                copy(2, down, origin, k).wait_recv()
+                copy(0, side, origin, k).start()
+                pl.when(z > 0)(lambda: copy(2, down, origin, k).start())
+
+            pl.when(z >= d)(from_below)
+            pl.when(z + d <= 3)(from_above)
+
+    keep.wait()
+    for k in range(pieces):
+        for line in range(4):
+            origin = 2 * line + x
+            copy(0, side, origin + 1 - 2 * x, k).wait_recv()
+            copy(0, side, origin, k, False).wait_send()
+            pl.when((line <= z) & (z < 3))(lambda: copy(1, up, origin, k).wait_send())
+            pl.when((line >= z) & (z > 0))(lambda: copy(2, down, origin, k).wait_send())
+
+
+def gather(wire, ident, name):
+    count = wire.shape[0]
+    return pl.pallas_call(
+        gather_body,
+        out_shape=jax.ShapeDtypeStruct((8 * count, SIDE, 128), BF),
+        in_specs=[VM],
+        out_specs=pl.BlockSpec(memory_space=pl.ANY),
+        scratch_shapes=[
+            pltpu.SemaphoreType.DMA((3, 4, count // PIECE)),
+            pltpu.SemaphoreType.DMA((8, count // PIECE)),
+            pltpu.SemaphoreType.DMA,
+        ],
+        compiler_params=pltpu.CompilerParams(
+            collective_id=ident, has_side_effects=True, vmem_limit_bytes=LIMIT),
+        cost_estimate=pl.CostEstimate(flops=0, bytes_accessed=count * 12_000_000, transcendentals=0),
+        name=name,
+    )(wire)
+
+
 def norm_parts(x):
     mean = jnp.mean(x, axis=-1, keepdims=True)
     centre = x - mean
@@ -856,8 +944,7 @@
     wire_a, wire_m = call(
         pack_body, (), (attn_master[0], mlp_master[0]),
         [((10, SIDE, 128), BF), ((20, SIDE, 128), BF)], [((2, 8, SIDE, 128), F32)], "pack")
-    all_a = lax.all_gather(wire_a, "dp", axis=0, tiled=True)
-    all_m = lax.all_gather(wire_m, "dp", axis=0, tiled=True)
+    all_a = gather(wire_a, 0, "gather_attn")
 
     part, normed, mixed, probs, att = call(
         attn_fwd_body, (ord_a,),
@@ -866,6 +953,8 @@
         [((6, 8 * SIDE, SIDE), BF), ((8, 2 * SIDE, SIDE), BF), ((64, SIDE, 32), BF), ((8, ROWS, SIDE), F32)],
         "attn_fwd")
     branch = lax.psum(part, "mp")
+    wire_m, mixed = lax.optimization_barrier((wire_m, mixed))
+    all_m = gather(wire_m, 1, "gather_mlp")
     part_down, part_second, sec_blocks, act_blocks, gh, go, up_sums = call(
         mlp_body, (ord_m,),
         (tok, live, cot, branch, norm_gains, norm_biases, out_biases, ub, all_m),
@@ -884,6 +973,7 @@
         mlp_tiles, (xm, ym), (sec_blocks, act_blocks, gh, go), [((160, SIDE, 128), BF)],
         [((16, ROWS, SIDE), BF)] * 2, "mlp_tiles")
     sum_m = lax.psum_scatter(stack_m, "dp", scatter_dimension=0, tiled=True)
+    second_sum, down_sum, stack_m = lax.optimization_barrier((second_sum, down_sum, stack_m))
 
     block_out, grad_middle, part_normed, rel_part, gm, gb, nb, sums_two, qkv_sums = call(
         mid_back_body, (ord_a,),

time: 605 us -> 526 us (0.87)
  waiting for transfers between devices: 361 us -> 165 us
  Pallas kernels: 169 us -> 284 us
    all_gather x2 -> x0, waiting for transfers between devices: 166 us -> none  [the longest x1 105 us: fast_local(): all_m = lax.all_gather(wire_m, 'dp', axis=0, tiled=True)]
    pallas_call x0 -> x2, Pallas kernels: none -> 115 us  [gather(): pl.pallas_call(gather_body, out_shape=jax.ShapeDtypeStruct((8 * count, SI...]
    psum x1, waiting for transfers between devices: 30 us -> 0.01 us  [fast_local(): branch = lax.psum(part, 'mp')]
    psum x1, waiting for transfers between devices: 34.2 us -> 18.3 us  [fast_local(): second_sum = lax.psum(part_second, 'mp')]
    psum x1, waiting for transfers between devices: 0.02 us -> 11.3 us  [fast_local(): normed_sum = lax.psum(part_normed, 'mp')]
  transfers between devices with their start and end apart: 7 -> 5, of which waited for: 6 -> 4; matrix products, arithmetic and copies ran while one was open for 2% -> 1% of each run, Pallas kernels for 9% -> 24%
where the time goes in v3:
time: 526 us
  Pallas kernels  284 us (54%)
  waiting for transfers between devices  165 us (31%)
  blocking collectives  51.1 us (10%)
  between operations  14 us (3%)
  local copies, waits for them, and re-layouts  7.57 us (1%)
    pallas_call x9, Pallas kernels, call(): pl.pallas_call(body, out_shape=[jax.ShapeDtypeStruct(shape, kind) for sha...  169 us
    pallas_call x2, Pallas kernels, gather(): pl.pallas_call(gather_body, out_shape=jax.ShapeDtypeStruct((8 * count, SI...  115 us
    reduce_scatter x1, waiting for transfers between devices, fast_local(): sum_m = lax.psum_scatter(stack_m, 'dp', scatter_dimension=0, tiled=True)  101 us
    psum x1, blocking collectives, fast_local(): lax.psum((jnp.stack([sums_one[0], sums_two[0]]), jnp.stack([sums_one[1],...  40.6 us
    reduce_scatter x1, waiting for transfers between devices, fast_local(): sum_a = lax.psum_scatter(stack_a, 'dp', scatter_dimension=0, tiled=True)  34.6 us
    psum x1, waiting for transfers between devices, fast_local(): second_sum = lax.psum(part_second, 'mp')  18.3 us
    psum x1, waiting for transfers between devices, fast_local(): normed_sum = lax.psum(part_normed, 'mp')  11.3 us
  transfers between devices with their start and end apart: 5, of which 4 were waited for; matrix products, arithmetic and copies ran while one was open for 1% of the time, Pallas kernels for 24%

profile of v3, /device:TPU:0, one launch (start us, length us, event | category | flops | bytes accessed | tf_op | source)
XLA Modules:
  0.0 525.7 jit_solution(10737105012937571789)
XLA Ops:
  7.2 0.7 copy.63
  8.1 0.1 tile.12
  8.4 0.1 copy.68.rel_hi
  8.5 8.6 %pack.1 = (bf16[10,160,128]{2,1,0:T(8,128)(2,1)}, bf16[20,160,128]{2,1,0:T(8,128)(2,1)}) custom-call(f32[8,25600]{1,0:T(8,128)} %bitcast.50, f32[16,25600]{1,0:T(8,128)} %bitcast.48), custom_call_target="tpu_custom_call" | custom-call | tf_op jit(solution)/shard_map/pack/pallas_call | solution.py:895
  17.1 41.6 %gather_attn.1.wire = bf16[80,160,128]{2,1,0:T(8,128)(2,1)} custom-call(bf16[10,160,128]{2,1,0:T(8,128)(2,1)} %get-tuple-element.57.wire), custom_call_target="tpu_custom_call" | custom-call | bytes 120000000 | tf_op jit(solution)/shard_map/gather_attn/pallas_call | solution.py:513
  58.7 0.8 copy.70.live
  59.5 0.6 select_reduce_fusion.1.order
  60.1 0.7 reshape.65.qkv_bias
  60.7 0.6 subtract_convert_fusion.rel_lo
  61.4 17.3 %attn_fwd.1 = (bf16[196,1280]{1,0:T(8,128)(2,1)}, bf16[208,1280]{1,0:T(8,128)(2,1)}, bf16[6,208,160]{2,1,0:T(8,128)(2,1)}, f32[4,208,208]{2,1,0:T(8,128)}, bf16[2,208,160]{2,1,0:T(8,128)(2,1)}) custom-call(s32[64]{0:T(128)} %select_reduce_fusion.1.order, bf16[196,1280]{1,0:T(8,128)(2,1)} %bitcast.44, f32[208,1]{1,0:T(8,128)} %copy.70.live, f32[2,1280]{1,0:T(2,128)} %gains.7, ...), custom_call_target="tpu_custom_call" | custom-call | tf_op jit(solution)/shard_map/attn_fwd/pallas_call | solution.py:895
  78.8 73.9 %gather_mlp.1.wire = bf16[160,160,128]{2,1,0:T(8,128)(2,1)} custom-call(bf16[20,160,128]{2,1,0:T(8,128)(2,1)} %get-tuple-element.61.wire), custom_call_target="tpu_custom_call" | custom-call | bytes 240000000 | tf_op jit(solution)/shard_map/gather_mlp/pallas_call | solution.py:513
  152.7 0.7 reshape.66.up_bias
  153.4 0.6 select_reduce_fusion.order
  154.0 25.2 %mlp.1 = (bf16[196,1280]{1,0:T(8,128)(2,1)}, bf16[196,1280]{1,0:T(8,128)(2,1)}, bf16[8,208,160]{2,1,0:T(8,128)(2,1)}, bf16[8,208,160]{2,1,0:T(8,128)(2,1)}, bf16...) custom-call(s32[128]{0:T(128)} %select_reduce_fusion.order, bf16[196,1280]{1,0:T(8,128)(2,1)} %bitcast.45, ...), custom_call_target="tpu_custom_call" | custom-call | tf_op jit(solution)/shard_map/mlp/pallas_call | solution.py:895
  179.2 0.2 all-reduce.10.cloned.1.call-start
  179.5 0.5 fusion.1
  180.0 17.4 %mlp_tiles.1 = bf16[160,160,128]{2,1,0:T(8,128)(2,1)} custom-call(s32[128]{0:T(128)} %get-tuple-element.187.left_at, s32[128]{0:T(128)} %get-tuple-element.186.right_at, bf16[8,208,160]{2,1,0:T(8,128)(2,1)} %get-tuple-element.64.sec, bf16[8,208,160]{2,1,0:T(8,128)(2,1)} %get-tuple-element.65.act, bf16[8,208,160]{2,1,0:T(8,128)(2,1)} %get-tuple-element.66.gh_ref, ...), custom_call_target="tpu_custom_call" | custom-call | tf_op jit(solution)/shard_map/mlp_tiles/pallas_call | solution.py:895
  197.4 18.3 %all-reduce.12.cloned.1.call-done = (bf16[196,1280]{1,0:T(8,128)(2,1)}, bf16[196,1280]{1,0:T(8,128)(2,1)}) async-done(((bf16[196,1280]{1,0:T(8,128)(2,1)}, bf16[196,1280]{1,0:T(8,128)(2,1)}), (bf16[196,1280]{1,0:T(8,128)(2,1)}, bf16[196,1280]{1,0:T(8,128)(2,1)})) %all-reduce.12.cloned.1.call-update) | async-done | bytes 1003536 | tf_op jit(solution)/shard_map/psum | solution.py:964
  215.6 17.6 %mid_back.1 = (bf16[196,1280]{1,0:T(8,128)(2,1)}, f32[196,1280]{1,0:T(8,128)}, bf16[196,1280]{1,0:T(8,128)(2,1)}, f32[128,160]{1,0:T(8,128)}, bf16[6,208,160]{2,...) custom-call(s32[64]{0:T(128)} %select_reduce_fusion.1.order, ...), custom_call_target="tpu_custom_call" | custom-call | tf_op jit(solution)/shard_map/mid_back/pallas_call | solution.py:895
  233.3 0.5 compare_select_fusion.3
  233.8 10.0 %attn_tiles.1 = bf16[80,160,128]{2,1,0:T(8,128)(2,1)} custom-call(s32[64]{0:T(128)} %get-tuple-element.185.left_at, s32[64]{0:T(128)} %get-tuple-element.184.right_at, bf16[8,208,160]{2,1,0:T(8,128)(2,1)} %get-tuple-element.83.nb_ref, bf16[2,208,160]{2,1,0:T(8,128)(2,1)} %get-tuple-element.73.att.att_ref, bf16[6,208,160]{2,1,0:T(8,128)(2,1)} %get-tuple-element.84.gm_ref, ...), custom_call_target="tpu_custom_call" | custom-call | tf_op jit(solution)/shard_map/attn_tiles/pallas_call | solution.py:895
  243.9 0.5 reduce-scatter.5.cloned.1.call-update
  244.4 0.8 copy.72.live
  245.5 10.5 %psum.86 = bf16[2,27,80]{2,0,1:T(2,128)(2,1)S(1)} all-reduce(bf16[2,27,80]{2,0,1:T(2,128)(2,1)S(1)} %copy.75), channel_id=1, replica_groups=mesh['dp'=8,'mp'=4] {'mp'}, use_global_device_ids=true, to_apply=%region_11.12 | all-reduce | flops 4320 | bytes 17280 | tf_op jit(solution)/shard_map/psum | solution.py:991
  256.0 11.3 %all-reduce.10.cloned.1.call-done.normed_sum = bf16[196,1280]{1,0:T(8,128)(2,1)} async-done(((bf16[196,1280]{1,0:T(8,128)(2,1)}), bf16[196,1280]{1,0:T(8,128)(2,1)}) %all-reduce.10.cloned.1.call-update) | async-done | bytes 501776 | tf_op jit(solution)/shard_map/psum | solution.py:990
  267.4 3.4 token_back.1
  270.8 3.2 copy.74
  274.0 40.6 %all-reduce.2 = (f32[2,1280]{1,0:T(2,128)}, f32[2,1280]{1,0:T(2,128)}, f32[2,1280]{1,0:T(2,128)}, f32[960]{0:T(1024)}, f32[1280]{0:T(1024)}, /*index=5*/f32[2,27,80]{2,0,1:T(2,128)}) all-reduce(f32[2,1280]{1,0:T(2,128)S(1)} %get-tuple-element.188, f32[2,1280]{1,0:T(2,128)S(1)} %get-tuple-element.189, ...), channel_id=1, replica_groups=mesh['dp'=8,'mp'=4] {'dp'}, use_global_device_ids=true, to_apply=%region_6.7 | all-reduce | flops 14240 | bytes 105280 | tf_op jit(solution)/shard_map/psum | solution.py:1005
  314.6 34.6 %reduce-scatter.3.cloned.1.call-done.wire = bf16[10,160,128]{2,1,0:T(8,128)(2,1)} async-done(((bf16[80,160,128]{2,1,0:T(8,128)(2,1)}), bf16[10,160,128]{2,1,0:T(8,128)(2,1)}) %reduce-scatter.3.cloned.1.call-update) | async-done | bytes 409616 | tf_op jit(solution)/shard_map/reduce_scatter | solution.py:1001
  349.2 23.7 %soap_attn.1 = (f32[8,25600]{1,0:T(8,128)}, f32[8,25600]{1,0:T(8,128)}, bf16[8,25600]{1,0:T(8,128)(2,1)}, f32[8,25600]{1,0:T(8,128)}, f32[8,25600]{1,0:T(8,128)}) custom-call(bf16[10,160,128]{2,1,0:T(8,128)(2,1)} %reduce-scatter.3.cloned.1.call-done.wire, f32[8,25600]{1,0:T(8,128)} %bitcast.51, f32[8,25600]{1,0:T(8,128)} %bitcast.59, f32[8,25600]{1,0:T(8,128)} %bitcast.60, ...), custom_call_target="tpu_custom_call" | custom-call | tf_op jit(solution)/shard_map/soap_attn/pallas_call | solution.py:895
  372.8 100.6 %reduce-scatter.5.cloned.1.call-done.wire = bf16[20,160,128]{2,1,0:T(8,128)(2,1)} async-done(((bf16[160,160,128]{2,1,0:T(8,128)(2,1)}), bf16[20,160,128]{2,1,0:T(8,128)(2,1)}) %reduce-scatter.5.cloned.1.call-update) | async-done | bytes 819216 | tf_op jit(solution)/shard_map/reduce_scatter | solution.py:975
  473.4 45.7 %soap_mlp.1 = (f32[16,25600]{1,0:T(8,128)}, f32[16,25600]{1,0:T(8,128)}, bf16[16,25600]{1,0:T(8,128)(2,1)}, f32[16,25600]{1,0:T(8,128)}, f32[16,25600]{1,0:T(8,128)}) custom-call(bf16[20,160,128]{2,1,0:T(8,128)(2,1)} %reduce-scatter.5.cloned.1.call-done.wire, f32[16,25600]{1,0:T(8,128)} %bitcast.49, f32[16,25600]{1,0:T(8,128)} %bitcast.54, ...), custom_call_target="tpu_custom_call" | custom-call | tf_op jit(solution)/shard_map/soap_mlp/pallas_call | solution.py:895
  (47 shorter events, 0.8 us)
Async XLA Ops:
  7.2 146.8 %all-reduce.8.cloned.1.call-start = ((), (), s32[]{:S(2)}) async-start(), calls=%async_computation.2 | async-start | bytes 1024000 | tf_op jit(solution)/shard_map/psum | solution.py:955
  8.5 52.2 %copy-start = (bf16[128,160]{1,0:T(8,128)(2,1)}, bf16[128,160]{1,0:T(8,128)(2,1)S(1)}, u32[]{:S(2)}) copy-start(bf16[128,160]{1,0:T(8,128)(2,1)S(1)} %copy.68.rel_hi) | copy-start | bytes 122884
  17.1 41.6 %copy-start.8 = (s32[1,196]{1,0:T(1,128)S(1)}, s32[1,196]{1,0:T(1,128)}, u32[]{:S(2)}) copy-start(s32[1,196]{1,0:T(1,128)} %param.24) | copy-start | bytes 2356
  17.1 42.4 %copy-start.10 = (s32[1,64]{1,0:T(1,128)S(1)}, s32[1,64]{1,0:T(1,128)}, u32[]{:S(2)}) copy-start(s32[1,64]{1,0:T(1,128)} %param.32) | copy-start | bytes 772
  17.1 43.0 %copy-start.7 = (f32[960]{0:T(1024)S(1)}, f32[960]{0:T(1024)}, u32[]{:S(2)}) copy-start(f32[960]{0:T(1024)} %param.29) | copy-start | bytes 11524
  78.7 136.9 %all-reduce.12.cloned.1.call-start = ((), (), s32[]{:S(2)}) async-start(), calls=%async_computation.6 | async-start | bytes 2048000 | tf_op jit(solution)/shard_map/psum | solution.py:964
  78.8 73.9 %copy-start.5 = (f32[1280]{0:T(1024)S(1)}, f32[1280]{0:T(1024)}, u32[]{:S(2)}) copy-start(f32[1280]{0:T(1024)} %param.30) | copy-start | bytes 15364
  78.8 74.6 %copy-start.9 = (s32[1,128]{1,0:T(1,128)S(1)}, s32[1,128]{1,0:T(1,128)}, u32[]{:S(2)}) copy-start(s32[1,128]{1,0:T(1,128)} %param.33) | copy-start | bytes 1540
  179.2 88.1 %all-reduce.10.cloned.1.call-start = ((), (), s32[]{:S(2)}) async-start(), calls=%async_computation.3 | async-start | bytes 1024000 | tf_op jit(solution)/shard_map/psum | solution.py:990
  233.2 115.9 %reduce-scatter.3.cloned.1.call-start = ((), (), s32[]{:S(2)}) async-start(), calls=%async_computation.4 | async-start | bytes 3686400 | tf_op jit(solution)/shard_map/reduce_scatter | solution.py:1001
  243.8 1.4 copy-start.6
  243.8 1.5 copy-start.1
  243.8 1.6 copy-start.4
  243.8 12.1 %copy-start.2 = (f32[4,1280]{1,0:T(4,128)S(1)}, f32[4,1280]{1,0:T(4,128)}, u32[]{:S(2)}) copy-start(f32[4,1280]{1,0:T(4,128)} %get-tuple-element.79) | copy-start | bytes 61444
  243.8 229.6 %reduce-scatter.5.cloned.1.call-start = ((), (), s32[]{:S(2)}) async-start(), calls=%async_computation.5 | async-start | bytes 7372800 | tf_op jit(solution)/shard_map/reduce_scatter | solution.py:975
  270.8 3.2 copy-start.3
Sparse Core Ops, SparseCore 0:
  78.9 33.4 all-reduce.7
  179.3 36.2 all-reduce.11
  233.3 33.9 all-reduce.9
  270.8 78.3 reduce-scatter.2
  352.6 120.7 reduce-scatter.4

commit v4 on v3

--- a/solution.py
+++ b/solution.py
@@ -1,3 +1,4 @@
+import functools
 import math
 
 import jax
@@ -440,12 +441,11 @@
 
 
 MESH_ID = pl.DeviceIdType.MESH
-PIECE = 5
-
-
-def gather_body(wire, out, send_sem, recv_sem, own_sem):
+
+
+def gather_body(piece, wire, out, send_sem, recv_sem, own_sem):
     count = wire.shape[0]
-    pieces = count // PIECE
+    pieces = count // piece
     me = lax.axis_index("dp")
     z, x = me // 2, me % 2
     side = me + 1 - 2 * x
@@ -464,9 +464,9 @@
     pl.when(jnp.logical_not(inner))(lambda: pl.semaphore_wait(barrier, 2))
 
     def copy(way, target, origin, k, own=False):
-        place = out.at[pl.ds(origin * count + PIECE * k, PIECE)]
+        place = out.at[pl.ds(origin * count + piece * k, piece)]
         return pltpu.make_async_remote_copy(
-            src_ref=wire.at[pl.ds(PIECE * k, PIECE)] if own else place,
+            src_ref=wire.at[pl.ds(piece * k, piece)] if own else place,
             dst_ref=place,
             send_sem=send_sem.at[way, origin // 2, k],
             recv_sem=recv_sem.at[origin, k],
@@ -508,16 +508,16 @@
             pl.when((line >= z) & (z > 0))(lambda: copy(2, down, origin, k).wait_send())
 
 
-def gather(wire, ident, name):
+def gather(wire, ident, name, piece=5):
     count = wire.shape[0]
     return pl.pallas_call(
-        gather_body,
-        out_shape=jax.ShapeDtypeStruct((8 * count, SIDE, 128), BF),
+        functools.partial(gather_body, piece),
+        out_shape=jax.ShapeDtypeStruct((8 * count,) + wire.shape[1:], wire.dtype),
         in_specs=[VM],
         out_specs=pl.BlockSpec(memory_space=pl.ANY),
         scratch_shapes=[
-            pltpu.SemaphoreType.DMA((3, 4, count // PIECE)),
-            pltpu.SemaphoreType.DMA((8, count // PIECE)),
+            pltpu.SemaphoreType.DMA((3, 4, count // piece)),
+            pltpu.SemaphoreType.DMA((8, count // piece)),
             pltpu.SemaphoreType.DMA,
         ],
         compiler_params=pltpu.CompilerParams(
@@ -525,6 +525,104 @@
         cost_estimate=pl.CostEstimate(flops=0, bytes_accessed=count * 12_000_000, transcendentals=0),
         name=name,
     )(wire)
+
+
+CHUNK = 5
+AHEAD = 4
+
+
+def scatter_body(stack_a, stack_m, out_a, out_m, inbox_a, inbox_m, half_a, half_m,
+                 side_send_a, side_recv_a, line_send_a, line_recv_a,
+                 side_send_m, side_recv_m, line_send_m, line_recv_m, own_a, own_m):
+    me = lax.axis_index("dp")
+    z, x = me // 2, me % 2
+    side = me + 1 - 2 * x
+
+    def line_at(j):
+        return lax.rem(z + j, 4)
+
+    barrier = pltpu.get_barrier_semaphore()
+    for target in (side, 2 * line_at(1) + x, 2 * line_at(2) + x, 2 * line_at(3) + x):
+        pl.semaphore_signal(barrier, inc=1, device_id={"dp": target}, device_id_type=MESH_ID)
+    pl.semaphore_wait(barrier, 4)
+
+    sets = (
+        (stack_a, out_a, inbox_a, half_a, side_send_a, side_recv_a, line_send_a, line_recv_a, own_a),
+        (stack_m, out_m, inbox_m, half_m, side_send_m, side_recv_m, line_send_m, line_recv_m, own_m),
+    )
+    steps = [(part, j, k) for part in range(2) for j in (1, 2, 3, 4) for k in range(sets[part][0].shape[0] // 8 // CHUNK)]
+
+    def to_side(part, j, k):
+        stack, _, inbox, _, send, recv, _, _, _ = sets[part]
+        count = stack.shape[0] // 8
+        line = line_at(j)
+        return pltpu.make_async_remote_copy(
+            src_ref=stack.at[pl.ds((2 * line + 1 - x) * count + CHUNK * k, CHUNK)],
+            dst_ref=inbox.at[pl.ds(line * count + CHUNK * k, CHUNK)],
+            send_sem=send.at[j - 1, k], recv_sem=recv.at[j - 1, k],
+            device_id={"dp": side}, device_id_type=MESH_ID)
+
+    def to_line(part, j, k):
+        stack, out, _, half, _, _, send, recv, _ = sets[part]
+        count = stack.shape[0] // 8
+        line = line_at(j)
+        return pltpu.make_async_remote_copy(
+            src_ref=half.at[pl.ds(line * count + CHUNK * k, CHUNK)],
+            dst_ref=out.at[pl.ds(z * count + CHUNK * k, CHUNK)],
+            send_sem=send.at[j - 1, k], recv_sem=recv.at[j - 1, k],
+            device_id={"dp": 2 * line + x}, device_id_type=MESH_ID)
+
+    for step in steps[:AHEAD]:
+        to_side(*step).start()
+    keeps = []
+    for at, (part, j, k) in enumerate(steps):
+        stack, out, inbox, half, _, _, _, _, own = sets[part]
+        count = stack.shape[0] // 8
+        to_side(part, j, k).wait_recv()
+        if at + AHEAD < len(steps):
+            to_side(*steps[at + AHEAD]).start()
+        line = line_at(j)
+
+        def add(i, carry):
+            to = line * count + CHUNK * k + i
+            total = stack[(2 * line + x) * count + CHUNK * k + i].astype(F32) + inbox[to].astype(F32)
+            half[to] = total.astype(BF)
+            return carry
+
+        lax.fori_loop(0, CHUNK, add, 0)
+        if j < 4:
+            to_line(part, j, k).start()
+        else:
+            place = pl.ds(line * count + CHUNK * k, CHUNK)
+            keep = pltpu.make_async_copy(half.at[place], out.at[place], own.at[k])
+            keep.start()
+            keeps.append(keep)
+    for part, j, k in steps:
+        to_side(part, j, k).wait_send()
+        if j < 4:
+            to_line(part, j, k).wait_send()
+            to_line(part, j, k).wait_recv()
+    for keep in keeps:
+        keep.wait()
+
+
+def scatter(stack_a, stack_m, ident, name):
+    shapes = [(4 * (stack.shape[0] // 8),) + stack.shape[1:] for stack in (stack_a, stack_m)]
+    sems = []
+    for stack in (stack_a, stack_m):
+        sems += [pltpu.SemaphoreType.DMA((4, stack.shape[0] // 8 // CHUNK))] * 4
+    sems += [pltpu.SemaphoreType.DMA((stack.shape[0] // 8 // CHUNK,)) for stack in (stack_a, stack_m)]
+    return pl.pallas_call(
+        scatter_body,
+        out_shape=[jax.ShapeDtypeStruct(shape, BF) for shape in shapes],
+        in_specs=[VM, VM],
+        out_specs=[pl.BlockSpec(memory_space=pl.ANY)] * 2,
+        scratch_shapes=[pltpu.VMEM(shape, BF) for shape in shapes + shapes] + sems,
+        compiler_params=pltpu.CompilerParams(
+            collective_id=ident, has_side_effects=True, vmem_limit_bytes=LIMIT),
+        cost_estimate=pl.CostEstimate(flops=0, bytes_accessed=350_000_000, transcendentals=0),
+        name=name,
+    )(stack_a, stack_m)
 
 
 def norm_parts(x):
@@ -824,11 +922,16 @@
 
 def soap_body(wire, master, left, right, first, second,
               grad_out, new_out, copy_out, first_out, second_out, sq_grad, sq_left, sq_right, sq_work):
+    count = wire.shape[0] // 4
     for r in range(master.shape[0] // 8):
         for half in range(2):
-            last = wire[5 * (2 * r + half) + 4].astype(F32)
+            def total(i):
+                w = [wire[p * count + i].astype(F32) for p in range(4)]
+                return (w[0] + w[1]) + (w[2] + w[3])
+
+            last = total(5 * (2 * r + half) + 4)
             for q in range(4):
-                sq_grad[0, 4 * half + q] = wire[5 * (2 * r + half) + q].astype(F32)
+                sq_grad[0, 4 * half + q] = total(5 * (2 * r + half) + q)
                 sq_grad[1, 4 * half + q] = last if q == 0 else pltpu.roll(last, 128 - 32 * q, 1)
         soap_group(8 * r, sq_grad, master, left, right, first, second,
                    grad_out, new_out, copy_out, first_out, second_out, sq_left, sq_right, sq_work)
@@ -972,7 +1075,6 @@
     stack_m, = call(
         mlp_tiles, (xm, ym), (sec_blocks, act_blocks, gh, go), [((160, SIDE, 128), BF)],
         [((16, ROWS, SIDE), BF)] * 2, "mlp_tiles")
-    sum_m = lax.psum_scatter(stack_m, "dp", scatter_dimension=0, tiled=True)
     second_sum, down_sum, stack_m = lax.optimization_barrier((second_sum, down_sum, stack_m))
 
     block_out, grad_middle, part_normed, rel_part, gm, gb, nb, sums_two, qkv_sums = call(
@@ -987,8 +1089,10 @@
     rel_half = SIDE // 2
     rel_fold = rel_part[:64] + rel_part[64:]
     rel_fold = (rel_fold[:, :rel_half] + rel_fold[:, rel_half:]).reshape(2, 32, rel_half)[:, : rel_pos.shape[1]]
-    normed_sum = lax.psum(part_normed, "mp")
-    rel_sum = lax.psum(rel_fold.astype(BF), "mp").astype(F32)
+    rel_size = rel_fold.size
+    rel_rows = -(-rel_size // width)
+    rel_flat = jnp.pad(rel_fold.reshape(-1).astype(BF), (0, rel_rows * width - rel_size)).reshape(rel_rows, width)
+    both_sum = lax.psum(jnp.concatenate([part_normed, rel_flat], axis=0), "mp")
 
     def attn_tiles(left_at, right_at, nb_ref, att_ref, gm_ref, gb_ref, wire, lefts, rights):
         lefts[0:8], lefts[8:10] = nb_ref[...], att_ref[...]
@@ -998,21 +1102,23 @@
     stack_a, = call(
         attn_tiles, (xa, ya), (nb, att, gm, gb), [((80, SIDE, 128), BF)],
         [((10, ROWS, SIDE), BF), ((14, ROWS, SIDE), BF)], "attn_tiles")
-    sum_a = lax.psum_scatter(stack_a, "dp", scatter_dimension=0, tiled=True)
+    sum_a, sum_m = scatter(stack_a, stack_m, 2, "scatter")
+    both_sum, sum_a = lax.optimization_barrier((both_sum, sum_a))
+    normed_sum, rel_sum = both_sum[:t], both_sum[t:].reshape(-1)[:rel_size].astype(F32)
     tokens_grad, sums_one = call(
         token_back_body, (), (tok, live[:t], normed_sum, grad_middle, norm_gains),
         [((t, width), F32), ((2, width), F32)], [], "token_back")
-    gains_grad, biases_grad, outb_grad, rel_grad, qkv_grad, up_grad = lax.psum(
-        (
-            jnp.stack([sums_one[0], sums_two[0]]),
-            jnp.stack([sums_one[1], sums_two[1]]),
-            jnp.stack([sums_two[3], sums_two[2]]),
-            rel_sum,
-            qkv_sums.reshape(-1),
-            up_sums.reshape(-1),
-        ),
-        "dp",
-    )
+    small = [sums_one.reshape(-1), sums_two.reshape(-1), qkv_sums.reshape(-1), up_sums.reshape(-1), rel_sum]
+    edges = np.cumsum([0] + [v.shape[0] for v in small])
+    lines = -(-int(edges[-1]) // 1024) * 8
+    small = jnp.pad(jnp.concatenate(small), (0, lines * 128 - int(edges[-1]))).reshape(1, lines, 128)
+    total = jnp.sum(gather(small, 3, "gather_sums", 1), axis=0).reshape(-1)
+    one, two, qkv_grad, up_grad, rel_grad = [total[edges[i]:edges[i + 1]] for i in range(5)]
+    one, two = one.reshape(2, width), two.reshape(4, width)
+    gains_grad = jnp.stack([one[0], two[0]])
+    biases_grad = jnp.stack([one[1], two[1]])
+    outb_grad = jnp.stack([two[3], two[2]])
+    rel_grad = rel_grad.reshape(rel_pos.shape)
 
     def soap(wire, master, left, right, first, second, name):
         shape = master.shape[1:]

time: 526 us -> 476 us (0.905)
  waiting for transfers between devices: 165 us -> 18.3 us
  Pallas kernels: 284 us -> 423 us
  blocking collectives: 51.1 us -> 0 us
  other arithmetic: 3.04 us -> 8.64 us
    pallas_call x2 -> x4, Pallas kernels: 115 us -> 253 us  [the longest x3 133 us: gather(): pl.pallas_call(functools.partial(gather_body, piece), out_shape=jax.Shape...]
    reduce_scatter x2 -> x0, waiting for transfers between devices: 135 us -> none  [the longest x1 101 us: fast_local(): sum_m = lax.psum_scatter(stack_m, 'dp', scatter_dimension=0, tiled=True)]
    psum x2 -> x0, blocking collectives: 51.1 us -> none  [the longest x1 40.6 us: fast_local(): lax.psum((jnp.stack([sums_one[0], sums_two[0]]), jnp.stack([sums_one[1],...]
    psum x1, waiting for transfers between devices: 11.3 us -> 0.01 us  [fast_local(): both_sum = lax.psum(jnp.concatenate([part_normed, rel_flat], axis=0), 'mp')]
  transfers between devices with their start and end apart: 5 -> 3, of which waited for: 4 -> 1; matrix products, arithmetic and copies ran while one was open for 1% -> 1% of each run, Pallas kernels for 24% -> 56%
where the time goes in v4:
time: 476 us; the launch traced here: 475 us
  Pallas kernels  423 us (89%)
  waiting for transfers between devices  18.3 us (4%)
  between operations  14 us (3%)
  local copies, waits for them, and re-layouts  10.8 us (2%)
  other arithmetic  8.64 us (2%)
    pallas_call x9, Pallas kernels, call(): pl.pallas_call(body, out_shape=[jax.ShapeDtypeStruct(shape, kind) for sha...  170 us
    pallas_call x3, Pallas kernels, gather(): pl.pallas_call(functools.partial(gather_body, piece), out_shape=jax.Shape...  133 us
    pallas_call x1, Pallas kernels, scatter(): pl.pallas_call(scatter_body, out_shape=[jax.ShapeDtypeStruct(shape, BF) f...  120 us
    psum x1, waiting for transfers between devices, fast_local(): second_sum = lax.psum(part_second, 'mp')  18.3 us
  transfers between devices with their start and end apart: 3, of which 1 were waited for; matrix products, arithmetic and copies ran while one was open for 1% of the time, Pallas kernels for 56%

profile of v4, /device:TPU:0, one launch (start us, length us, event | category | flops | bytes accessed | tf_op | source)
XLA Modules:
  0.0 475.0 jit_solution(8227288790269639170)
XLA Ops:
  7.2 0.7 copy.62
  8.5 8.6 %pack.1 = (bf16[10,160,128]{2,1,0:T(8,128)(2,1)}, bf16[20,160,128]{2,1,0:T(8,128)(2,1)}) custom-call(f32[8,25600]{1,0:T(8,128)} %bitcast.84, f32[16,25600]{1,0:T(8,128)} %bitcast.82), custom_call_target="tpu_custom_call" | custom-call | tf_op jit(solution)/shard_map/pack/pallas_call | solution.py:998
  17.1 41.6 %gather_attn.1.wire = bf16[80,160,128]{2,1,0:T(8,128)(2,1)} custom-call(bf16[10,160,128]{2,1,0:T(8,128)(2,1)} %get-tuple-element.62.wire), custom_call_target="tpu_custom_call" | custom-call | bytes 120000000 | tf_op jit(solution)/shard_map/gather_attn/pallas_call | solution.py:513
  58.7 0.8 copy.69.live
  60.1 0.7 reshape.100.qkv_bias
  60.7 0.6 subtract_convert_fusion.rel_lo
  61.4 17.3 %attn_fwd.1 = (bf16[196,1280]{1,0:T(8,128)(2,1)}, bf16[208,1280]{1,0:T(8,128)(2,1)}, bf16[6,208,160]{2,1,0:T(8,128)(2,1)}, f32[4,208,208]{2,1,0:T(8,128)}, bf16[2,208,160]{2,1,0:T(8,128)(2,1)}) custom-call(s32[64]{0:T(128)} %select_reduce_fusion.1.order, bf16[196,1280]{1,0:T(8,128)(2,1)} %bitcast.78, f32[208,1]{1,0:T(8,128)} %copy.69.live, f32[2,1280]{1,0:T(2,128)} %gains.7, ...), custom_call_target="tpu_custom_call" | custom-call | tf_op jit(solution)/shard_map/attn_fwd/pallas_call | solution.py:998
  78.8 73.9 %gather_mlp.1.wire = bf16[160,160,128]{2,1,0:T(8,128)(2,1)} custom-call(bf16[20,160,128]{2,1,0:T(8,128)(2,1)} %get-tuple-element.66.wire), custom_call_target="tpu_custom_call" | custom-call | bytes 240000000 | tf_op jit(solution)/shard_map/gather_mlp/pallas_call | solution.py:513
  152.7 0.7 reshape.101.up_bias
  154.0 25.2 %mlp.1 = (bf16[196,1280]{1,0:T(8,128)(2,1)}, bf16[196,1280]{1,0:T(8,128)(2,1)}, bf16[8,208,160]{2,1,0:T(8,128)(2,1)}, bf16[8,208,160]{2,1,0:T(8,128)(2,1)}, bf16...) custom-call(s32[128]{0:T(128)} %select_reduce_fusion.order, bf16[196,1280]{1,0:T(8,128)(2,1)} %bitcast.79, ...), custom_call_target="tpu_custom_call" | custom-call | tf_op jit(solution)/shard_map/mlp/pallas_call | solution.py:998
  180.0 17.4 %mlp_tiles.1.stack_m = bf16[160,160,128]{2,1,0:T(8,128)(2,1)} custom-call(s32[128]{0:T(128)} %get-tuple-element.191.left_at, s32[128]{0:T(128)} %get-tuple-element.190.right_at, bf16[8,208,160]{2,1,0:T(8,128)(2,1)} %get-tuple-element.69.sec, bf16[8,208,160]{2,1,0:T(8,128)(2,1)} %get-tuple-element.70.act, bf16[8,208,160]{2,1,0:T(8,128)(2,1)} %get-tuple-element.71.gh_ref, ...), custom_call_target="tpu_custom_call" | custom-call | tf_op jit(solution)/shard_map/mlp_tiles/pallas_call | solution.py:998
  197.3 18.3 %all-reduce.13.cloned.1.call-done = (bf16[196,1280]{1,0:T(8,128)(2,1)}, bf16[196,1280]{1,0:T(8,128)(2,1)}) async-done(((bf16[196,1280]{1,0:T(8,128)(2,1)}, bf16[196,1280]{1,0:T(8,128)(2,1)}), (bf16[196,1280]{1,0:T(8,128)(2,1)}, bf16[196,1280]{1,0:T(8,128)(2,1)})) %all-reduce.13.cloned.1.call-update) | async-done | bytes 1003536 | tf_op jit(solution)/shard_map/psum | solution.py:1067
  215.6 17.5 %mid_back.1 = (bf16[196,1280]{1,0:T(8,128)(2,1)}, f32[196,1280]{1,0:T(8,128)}, bf16[196,1280]{1,0:T(8,128)(2,1)}, f32[128,160]{1,0:T(8,128)}, bf16[6,208,160]{2,...) custom-call(s32[64]{0:T(128)} %select_reduce_fusion.1.order, ...), custom_call_target="tpu_custom_call" | custom-call | tf_op jit(solution)/shard_map/mid_back/pallas_call | solution.py:998
  233.2 0.9 slice_add_fusion
  234.3 1.9 pad_maximum_fusion
  236.2 0.8 copy.71.live
  237.7 9.9 %attn_tiles.1.stack_a = bf16[80,160,128]{2,1,0:T(8,128)(2,1)} custom-call(s32[64]{0:T(128)} %get-tuple-element.189.left_at, s32[64]{0:T(128)} %get-tuple-element.188.right_at, bf16[8,208,160]{2,1,0:T(8,128)(2,1)} %get-tuple-element.82.nb_ref, bf16[2,208,160]{2,1,0:T(8,128)(2,1)} %get-tuple-element.78.att.att_ref, ...), custom_call_target="tpu_custom_call" | custom-call | tf_op jit(solution)/shard_map/attn_tiles/pallas_call | solution.py:998
  247.5 119.8 %scatter.1 = (bf16[40,160,128]{2,1,0:T(8,128)(2,1)}, bf16[80,160,128]{2,1,0:T(8,128)(2,1)}) custom-call(bf16[80,160,128]{2,1,0:T(8,128)(2,1)} %attn_tiles.1.stack_a, bf16[160,160,128]{2,1,0:T(8,128)(2,1)} %mlp_tiles.1.stack_m), custom_call_target="tpu_custom_call" | custom-call | bytes 350000000 | tf_op jit(solution)/shard_map/scatter/pallas_call | solution.py:615
  367.3 46.7 %soap_mlp.1 = (f32[16,25600]{1,0:T(8,128)}, f32[16,25600]{1,0:T(8,128)}, bf16[16,25600]{1,0:T(8,128)(2,1)}, f32[16,25600]{1,0:T(8,128)}, f32[16,25600]{1,0:T(8,128)}) custom-call(bf16[80,160,128]{2,1,0:T(8,128)(2,1)} %get-tuple-element.96.wire, f32[16,25600]{1,0:T(8,128)} %bitcast.83, f32[16,25600]{1,0:T(8,128)} %bitcast.88, f32[16,25600]{1,0:T(8,128)} %bitcast.89, ...), custom_call_target="tpu_custom_call" | custom-call | tf_op jit(solution)/shard_map/soap_mlp/pallas_call | solution.py:998
  414.0 0.7 slice.88
  414.8 3.4 token_back.1
  418.2 0.8 reshape.104
  419.1 0.6 pad_bitcast_fusion.wire
  419.7 17.5 %gather_sums.1 = f32[8,112,128]{2,1,0:T(8,128)} custom-call(f32[1,112,128]{2,1,0:T(8,128)} %pad_bitcast_fusion.wire), custom_call_target="tpu_custom_call" | custom-call | bytes 12000000 | tf_op jit(solution)/shard_map/gather_sums/pallas_call | solution.py:513
  437.2 1.1 reduce_sum.29
  438.4 0.7 slice.116
  439.7 0.6 copy.73
  440.4 2.0 copy.72
  442.4 0.6 pad_maximum_fusion.3
  443.0 0.6 pad_maximum_fusion.2
  443.6 0.6 pad_maximum_fusion.1
  444.2 24.2 %soap_attn.1 = (f32[8,25600]{1,0:T(8,128)}, f32[8,25600]{1,0:T(8,128)}, bf16[8,25600]{1,0:T(8,128)(2,1)}, f32[8,25600]{1,0:T(8,128)}, f32[8,25600]{1,0:T(8,128)}) custom-call(bf16[40,160,128]{2,1,0:T(8,128)(2,1)} %get-tuple-element.94.wire, f32[8,25600]{1,0:T(8,128)} %bitcast.85, f32[8,25600]{1,0:T(8,128)} %bitcast.93, f32[8,25600]{1,0:T(8,128)} %bitcast.94, ...), custom_call_target="tpu_custom_call" | custom-call | tf_op jit(solution)/shard_map/soap_attn/pallas_call | solution.py:998
  (58 shorter events, 4.4 us)
Async XLA Ops:
  7.2 146.8 %all-reduce.9.cloned.1.call-start = ((), (), s32[]{:S(2)}) async-start(), calls=%async_computation | async-start | bytes 1024000 | tf_op jit(solution)/shard_map/psum | solution.py:1058
  8.5 52.2 %copy-start = (bf16[128,160]{1,0:T(8,128)(2,1)}, bf16[128,160]{1,0:T(8,128)(2,1)S(1)}, u32[]{:S(2)}) copy-start(bf16[128,160]{1,0:T(8,128)(2,1)S(1)} %copy.67.rel_hi) | copy-start | bytes 122884
  17.1 41.6 %copy-start.7 = (s32[1,196]{1,0:T(1,128)S(1)}, s32[1,196]{1,0:T(1,128)}, u32[]{:S(2)}) copy-start(s32[1,196]{1,0:T(1,128)} %param.24) | copy-start | bytes 2356
  17.1 42.4 %copy-start.9 = (s32[1,64]{1,0:T(1,128)S(1)}, s32[1,64]{1,0:T(1,128)}, u32[]{:S(2)}) copy-start(s32[1,64]{1,0:T(1,128)} %param.32) | copy-start | bytes 772
  17.1 43.0 %copy-start.6 = (f32[960]{0:T(1024)S(1)}, f32[960]{0:T(1024)}, u32[]{:S(2)}) copy-start(f32[960]{0:T(1024)} %param.29) | copy-start | bytes 11524
  78.7 136.9 %all-reduce.13.cloned.1.call-start = ((), (), s32[]{:S(2)}) async-start(), calls=%async_computation.2 | async-start | bytes 2048000 | tf_op jit(solution)/shard_map/psum | solution.py:1067
  78.8 73.9 %copy-start.4 = (f32[1280]{0:T(1024)S(1)}, f32[1280]{0:T(1024)}, u32[]{:S(2)}) copy-start(f32[1280]{0:T(1024)} %param.30) | copy-start | bytes 15364
  78.8 74.6 %copy-start.8 = (s32[1,128]{1,0:T(1,128)S(1)}, s32[1,128]{1,0:T(1,128)}, u32[]{:S(2)}) copy-start(s32[1,128]{1,0:T(1,128)} %param.33) | copy-start | bytes 1540
  179.2 234.8 %all-reduce.11.cloned.1.call-start = ((), (), s32[]{:S(2)}) async-start(), calls=%async_computation.1 | async-start | bytes 1024000 | tf_op jit(solution)/shard_map/psum | solution.py:1095
  233.2 4.3 copy-start.5
  233.2 4.4 copy-start.2
  233.2 4.4 copy-start.3
  418.2 22.2 %copy-start.1 = (f32[196,1280]{1,0:T(8,128)S(1)}, f32[196,1280]{1,0:T(8,128)}, u32[]{:S(2)}) copy-start(f32[196,1280]{1,0:T(8,128)} %get-tuple-element.89) | copy-start | bytes 3010564
Sparse Core Ops, SparseCore 0:
  78.9 33.4 all-reduce.8
  179.3 36.2 all-reduce.12
  236.3 33.9 all-reduce.10

commit v5 on v4

--- a/solution.py
+++ b/solution.py
@@ -531,12 +531,11 @@
 AHEAD = 4
 
 
-def scatter_body(stack_a, stack_m, out_a, out_m, inbox_a, inbox_m, half_a, half_m,
-                 side_send_a, side_recv_a, line_send_a, line_recv_a,
-                 side_send_m, side_recv_m, line_send_m, line_recv_m, own_a, own_m):
+def scatter_steps(stack, out, inbox, half, side_send, side_recv, line_send, line_recv, own, units):
     me = lax.axis_index("dp")
     z, x = me // 2, me % 2
     side = me + 1 - 2 * x
+    count = stack.shape[0] // 8
 
     def line_at(j):
         return lax.rem(z + j, 4)
@@ -545,40 +544,32 @@
     for target in (side, 2 * line_at(1) + x, 2 * line_at(2) + x, 2 * line_at(3) + x):
         pl.semaphore_signal(barrier, inc=1, device_id={"dp": target}, device_id_type=MESH_ID)
     pl.semaphore_wait(barrier, 4)
-
-    sets = (
-        (stack_a, out_a, inbox_a, half_a, side_send_a, side_recv_a, line_send_a, line_recv_a, own_a),
-        (stack_m, out_m, inbox_m, half_m, side_send_m, side_recv_m, line_send_m, line_recv_m, own_m),
-    )
-    steps = [(part, j, k) for part in range(2) for j in (1, 2, 3, 4) for k in range(sets[part][0].shape[0] // 8 // CHUNK)]
-
-    def to_side(part, j, k):
-        stack, _, inbox, _, send, recv, _, _, _ = sets[part]
-        count = stack.shape[0] // 8
+    steps = [(j, k) for j in (1, 2, 3, 4) for k in range(count // CHUNK)]
+
+    def to_side(j, k):
         line = line_at(j)
         return pltpu.make_async_remote_copy(
             src_ref=stack.at[pl.ds((2 * line + 1 - x) * count + CHUNK * k, CHUNK)],
             dst_ref=inbox.at[pl.ds(line * count + CHUNK * k, CHUNK)],
-            send_sem=send.at[j - 1, k], recv_sem=recv.at[j - 1, k],
+            send_sem=side_send.at[j - 1, k], recv_sem=side_recv.at[j - 1, k],
             device_id={"dp": side}, device_id_type=MESH_ID)
 
-    def to_line(part, j, k):
-        stack, out, _, half, _, _, send, recv, _ = sets[part]
-        count = stack.shape[0] // 8
+    def to_line(j, k):
         line = line_at(j)
         return pltpu.make_async_remote_copy(
             src_ref=half.at[pl.ds(line * count + CHUNK * k, CHUNK)],
             dst_ref=out.at[pl.ds(z * count + CHUNK * k, CHUNK)],
-            send_sem=send.at[j - 1, k], recv_sem=recv.at[j - 1, k],
+            send_sem=line_send.at[j - 1, k], recv_sem=line_recv.at[j - 1, k],
             device_id={"dp": 2 * line + x}, device_id_type=MESH_ID)
 
     for step in steps[:AHEAD]:
         to_side(*step).start()
     keeps = []
-    for at, (part, j, k) in enumerate(steps):
-        stack, out, inbox, half, _, _, _, _, own = sets[part]
-        count = stack.shape[0] // 8
-        to_side(part, j, k).wait_recv()
+    units = list(units)
+    for at, (j, k) in enumerate(steps):
+        if units:
+            units.pop(0)()
+        to_side(j, k).wait_recv()
         if at + AHEAD < len(steps):
             to_side(*steps[at + AHEAD]).start()
         line = line_at(j)
@@ -591,38 +582,58 @@
 
         lax.fori_loop(0, CHUNK, add, 0)
         if j < 4:
-            to_line(part, j, k).start()
+            to_line(j, k).start()
         else:
             place = pl.ds(line * count + CHUNK * k, CHUNK)
             keep = pltpu.make_async_copy(half.at[place], out.at[place], own.at[k])
             keep.start()
             keeps.append(keep)
-    for part, j, k in steps:
-        to_side(part, j, k).wait_send()
+    for unit in units:
+        unit()
+    for j, k in steps:
+        to_side(j, k).wait_send()
         if j < 4:
-            to_line(part, j, k).wait_send()
-            to_line(part, j, k).wait_recv()
+            to_line(j, k).wait_send()
+            to_line(j, k).wait_recv()
     for keep in keeps:
         keep.wait()
 
 
-def scatter(stack_a, stack_m, ident, name):
-    shapes = [(4 * (stack.shape[0] // 8),) + stack.shape[1:] for stack in (stack_a, stack_m)]
-    sems = []
-    for stack in (stack_a, stack_m):
-        sems += [pltpu.SemaphoreType.DMA((4, stack.shape[0] // 8 // CHUNK))] * 4
-    sems += [pltpu.SemaphoreType.DMA((stack.shape[0] // 8 // CHUNK,)) for stack in (stack_a, stack_m)]
+def scatter_call(body, stack, args, outs, scratch, ident, cost, name):
+    count = stack.shape[0] // 8
+    shape = (4 * count,) + stack.shape[1:]
+    pieces = count // CHUNK
     return pl.pallas_call(
-        scatter_body,
-        out_shape=[jax.ShapeDtypeStruct(shape, BF) for shape in shapes],
-        in_specs=[VM, VM],
-        out_specs=[pl.BlockSpec(memory_space=pl.ANY)] * 2,
-        scratch_shapes=[pltpu.VMEM(shape, BF) for shape in shapes + shapes] + sems,
+        body,
+        out_shape=[jax.ShapeDtypeStruct(shape, BF)] + [jax.ShapeDtypeStruct(*out) for out in outs],
+        in_specs=[VM] * (1 + len(args)),
+        out_specs=[pl.BlockSpec(memory_space=pl.ANY)] + [VM] * len(outs),
+        scratch_shapes=[pltpu.VMEM(shape, BF)] * 2 + [pltpu.SemaphoreType.DMA((4, pieces))] * 4
+        + [pltpu.SemaphoreType.DMA((pieces,))] + [pltpu.VMEM(*item) for item in scratch],
         compiler_params=pltpu.CompilerParams(
             collective_id=ident, has_side_effects=True, vmem_limit_bytes=LIMIT),
-        cost_estimate=pl.CostEstimate(flops=0, bytes_accessed=350_000_000, transcendentals=0),
+        cost_estimate=pl.CostEstimate(flops=0, bytes_accessed=cost, transcendentals=0),
         name=name,
-    )(stack_a, stack_m)
+    )(stack, *args)
+
+
+def scatter_mlp_body(stack, left_m, right_m, left_a, right_a, out, sq_left_m, sq_right_m, sq_left_a, sq_right_a, *wires):
+    units = []
+    for flat, square in ((left_m, sq_left_m), (right_m, sq_right_m), (left_a, sq_left_a), (right_a, sq_right_a)):
+        for g in range(square.shape[0]):
+            units.append(lambda f=flat, r=8 * g, sq=square, g=g: flat_to_square(
+                lambda at: f[r : r + 8, pl.ds(at, 128)], sq.at[g]))
+    scatter_steps(stack, out, *wires, units)
+
+
+def scatter_attn_body(stack, wire, sq_left, sq_right, master, first, second,
+                      out, grad_out, new_out, copy_out, first_out, second_out, *rest):
+    wires, (sq_grad, sq_work) = rest[:-2], rest[-2:]
+    units = []
+    for g in range(2):
+        units += soap_units(g, g, wire, sq_left, sq_right, master, first, second,
+                            grad_out, new_out, copy_out, first_out, second_out, sq_grad, sq_work)
+    scatter_steps(stack, out, *wires, units)
 
 
 def norm_parts(x):
@@ -871,26 +882,32 @@
     return kind(a_hi, b_hi) + (kind(a_hi, b_lo) + kind(a_lo, b_hi))
 
 
-def soap_group(r0, grad_square, master, left, right, first, second,
-               grad_out, new_out, copy_out, first_out, second_out, sq_left, sq_right, sq_work):
-    rows = slice(r0, r0 + 8)
-
-    def writer(ref):
+def soap_units(r, g, wire, sq_left, sq_right, master, first, second,
+               grad_out, new_out, copy_out, first_out, second_out, sq_grad, sq_work):
+    rows = slice(8 * r, 8 * r + 8)
+    count = wire.shape[0] // 4
+    left, right = sq_left.at[g], sq_right.at[g]
+
+    def total(i):
+        w = [wire[p * count + i].astype(F32) for p in range(4)]
+        return (w[0] + w[1]) + (w[2] + w[3])
+
+    def load():
+        for half in range(2):
+            last = total(5 * (2 * r + half) + 4)
+            for q in range(4):
+                sq_grad[0, 4 * half + q] = total(5 * (2 * r + half) + q)
+                sq_grad[1, 4 * half + q] = last if q == 0 else pltpu.roll(last, 128 - 32 * q, 1)
+
         def write(at, value):
-            ref[rows, pl.ds(at, 128)] = value
-        return write
-
-    flat_to_square(lambda at: left[rows, pl.ds(at, 128)], sq_left, 8)
-    flat_to_square(lambda at: right[rows, pl.ds(at, 128)], sq_right, 8)
-    square_to_flat(grad_square, writer(grad_out), 8)
+            grad_out[rows, pl.ds(at, 128)] = value
+
+        square_to_flat(sq_grad, write)
 
     def rotate(t, carry):
-        l, r = square_tile(sq_left, t), square_tile(sq_right, t)
-        half = split_dot(dot_tn, l, square_tile(grad_square, t))
-        put_tile(sq_work, t, split_dot(dot, half, r))
-        return carry
-
-    lax.fori_loop(0, 8, rotate, 0)
+        half = split_dot(dot_tn, square_tile(left, t), square_tile(sq_grad, t))
+        put_tile(sq_work, t, split_dot(dot, half, square_tile(right, t)))
+        return carry
 
     def moments(at, rotated):
         cols = pl.ds(at, 128)
@@ -900,16 +917,10 @@
         second_out[rows, cols] = s
         new_out[rows, cols] = f / (jnp.sqrt(s) + adam_eps)
 
-    square_to_flat(sq_work, moments, 8)
-    flat_to_square(lambda at: new_out[rows, pl.ds(at, 128)], sq_work, 8)
-
     def turn_back(t, carry):
-        l, r = square_tile(sq_left, t), square_tile(sq_right, t)
-        half = split_dot(dot, l, square_tile(sq_work, t))
-        put_tile(sq_work, t, split_dot(dot_nt, half, r))
-        return carry
-
-    lax.fori_loop(0, 8, turn_back, 0)
+        half = split_dot(dot, square_tile(left, t), square_tile(sq_work, t))
+        put_tile(sq_work, t, split_dot(dot_nt, half, square_tile(right, t)))
+        return carry
 
     def finish(at, update):
         cols = pl.ds(at, 128)
@@ -917,24 +928,24 @@
         new_out[rows, cols] = value
         copy_out[rows, cols] = value.astype(BF)
 
-    square_to_flat(sq_work, finish, 8)
-
-
-def soap_body(wire, master, left, right, first, second,
-              grad_out, new_out, copy_out, first_out, second_out, sq_grad, sq_left, sq_right, sq_work):
-    count = wire.shape[0] // 4
-    for r in range(master.shape[0] // 8):
-        for half in range(2):
-            def total(i):
-                w = [wire[p * count + i].astype(F32) for p in range(4)]
-                return (w[0] + w[1]) + (w[2] + w[3])
-
-            last = total(5 * (2 * r + half) + 4)
-            for q in range(4):
-                sq_grad[0, 4 * half + q] = total(5 * (2 * r + half) + q)
-                sq_grad[1, 4 * half + q] = last if q == 0 else pltpu.roll(last, 128 - 32 * q, 1)
-        soap_group(8 * r, sq_grad, master, left, right, first, second,
-                   grad_out, new_out, copy_out, first_out, second_out, sq_left, sq_right, sq_work)
+    def loop(body):
+        lax.fori_loop(0, 8, body, 0)
+
+    return [
+        load,
+        lambda: loop(rotate),
+        lambda: square_to_flat(sq_work, moments),
+        lambda: flat_to_square(lambda at: new_out[rows, pl.ds(at, 128)], sq_work),
+        lambda: loop(turn_back),
+        lambda: square_to_flat(sq_work, finish),
+    ]
+
+
+def soap_attn_body(wire, sq_left, sq_right, master, first, second,
+                   grad_out, new_out, copy_out, first_out, second_out, sq_grad, sq_work):
+    for unit in soap_units(0, 0, wire, sq_left, sq_right, master, first, second,
+                           grad_out, new_out, copy_out, first_out, second_out, sq_grad, sq_work):
+        unit()
 
 
 def build(mesh):
@@ -1075,7 +1086,10 @@
     stack_m, = call(
         mlp_tiles, (xm, ym), (sec_blocks, act_blocks, gh, go), [((160, SIDE, 128), BF)],
         [((16, ROWS, SIDE), BF)] * 2, "mlp_tiles")
-    second_sum, down_sum, stack_m = lax.optimization_barrier((second_sum, down_sum, stack_m))
+    sum_m, sq_left_m, sq_right_m, sq_left_a, sq_right_a = scatter_call(
+        scatter_mlp_body, stack_m, (mlp_left[0], mlp_right[0], attn_left[0], attn_right[0]),
+        [((2, 2, 8, SIDE, 128), F32)] * 2 + [((1, 2, 8, SIDE, 128), F32)] * 2, [], 2, 250_000_000, "scatter_mlp")
+    second_sum, down_sum, sum_m = lax.optimization_barrier((second_sum, down_sum, sum_m))
 
     block_out, grad_middle, part_normed, rel_part, gm, gb, nb, sums_two, qkv_sums = call(
         mid_back_body, (ord_a,),
@@ -1102,7 +1116,12 @@
     stack_a, = call(
         attn_tiles, (xa, ya), (nb, att, gm, gb), [((80, SIDE, 128), BF)],
         [((10, ROWS, SIDE), BF), ((14, ROWS, SIDE), BF)], "attn_tiles")
-    sum_a, sum_m = scatter(stack_a, stack_m, 2, "scatter")
+    def soap_outs(shape):
+        return [(shape, F32), (shape, F32), (shape, BF), (shape, F32), (shape, F32)]
+
+    sum_a, mg, mn, mc, mf, ms = scatter_call(
+        scatter_attn_body, stack_a, (sum_m, sq_left_m, sq_right_m, mlp_master[0], mlp_first[0], mlp_second[0]),
+        soap_outs(mlp_master.shape[1:]), [((2, 8, SIDE, 128), F32)] * 2, 4, 150_000_000, "scatter_attn")
     both_sum, sum_a = lax.optimization_barrier((both_sum, sum_a))
     normed_sum, rel_sum = both_sum[:t], both_sum[t:].reshape(-1)[:rel_size].astype(F32)
     tokens_grad, sums_one = call(
@@ -1120,18 +1139,11 @@
     outb_grad = jnp.stack([two[3], two[2]])
     rel_grad = rel_grad.reshape(rel_pos.shape)
 
-    def soap(wire, master, left, right, first, second, name):
-        shape = master.shape[1:]
-        outs = call(
-            soap_body, (), (wire, master[0], left[0], right[0], first[0], second[0]),
-            [(shape, F32), (shape, F32), (shape, BF), (shape, F32), (shape, F32)],
-            [((2, 8, SIDE, 128), F32)] * 4, name)
-        return [value[None] for value in outs]
-
-    mg, mn, mc, mf, ms = soap(sum_m, mlp_master, mlp_left, mlp_right, mlp_first, mlp_second, "soap_mlp")
-    ag, an, ac, af, as_ = soap(sum_a, attn_master, attn_left, attn_right, attn_first, attn_second, "soap_attn")
+    ag, an, ac, af, as_ = call(
+        soap_attn_body, (), (sum_a, sq_left_a, sq_right_a, attn_master[0], attn_first[0], attn_second[0]),
+        soap_outs(attn_master.shape[1:]), [((2, 8, SIDE, 128), F32)] * 2, "soap_attn")
     return (block_out[None], tokens_grad[None], gains_grad, biases_grad, outb_grad, qkv_grad, up_grad, rel_grad,
-            ag, mg, an, mn, ac, mc, af, as_, mf, ms)
+            *(value[None] for value in (ag, mg, an, mn, ac, mc, af, as_, mf, ms)))
 
 
 def solution(mesh):

time: 476 us -> 441 us (0.926)
  Pallas kernels: 423 us -> 397 us
  waiting for transfers between devices: 18.3 us -> 0.1 us
  local copies, waits for them, and re-layouts: 10.8 us -> 19.3 us
    pallas_call x9 -> x8, Pallas kernels: 170 us -> 120 us  [call(): pl.pallas_call(body, out_shape=[jax.ShapeDtypeStruct(shape, kind) for sha...]
    pallas_call x1 -> x2, Pallas kernels: 120 us -> 145 us  [scatter_call(): pl.pallas_call(body, out_shape=[jax.ShapeDtypeStruct(shape, BF)] + [jax.S...]
    psum x1, waiting for transfers between devices: 18.3 us -> 0.02 us  [fast_local(): second_sum = lax.psum(part_second, 'mp')]
    unnamed x24 -> x35, local copies, waits for them, and re-layouts: 3.42 us -> 11.2 us
  transfers between devices with their start and end apart: 3 -> 3, of which waited for: 1 -> 0; matrix products, arithmetic and copies ran while one was open for 1% -> 1% of each run, Pallas kernels for 56% -> 56%
where the time goes in v5:
time: 441 us; the launch traced here: 440 us
  Pallas kernels  397 us (90%)
  local copies, waits for them, and re-layouts  19.3 us (4%)
  between operations  14 us (3%)
  other arithmetic  9.97 us (2%)
    pallas_call x2, Pallas kernels, scatter_call(): pl.pallas_call(body, out_shape=[jax.ShapeDtypeStruct(shape, BF)] + [jax.S...  145 us
    pallas_call x3, Pallas kernels, gather(): pl.pallas_call(functools.partial(gather_body, piece), out_shape=jax.Shape...  132 us
    pallas_call x8, Pallas kernels, call(): pl.pallas_call(body, out_shape=[jax.ShapeDtypeStruct(shape, kind) for sha...  120 us
    unnamed x35, local copies, waits for them, and re-layouts  11.2 us
  transfers between devices with their start and end apart: 3, of which 0 were waited for; matrix products, arithmetic and copies ran while one was open for 1% of the time, Pallas kernels for 56%

profile of v5, /device:TPU:0, one launch (start us, length us, event | category | flops | bytes accessed | tf_op | source)
XLA Modules:
  0.0 440.4 jit_solution(11098183405698102610)
XLA Ops:
  7.2 0.7 copy.62
  8.4 1.3 select_reduce_fusion.1.order
  9.6 0.7 convert_bitcast_fusion
  10.3 1.4 reshape.100.qkv_bias
  11.7 0.8 copy.69.live
  12.6 8.6 %pack.1 = (bf16[10,160,128]{2,1,0:T(8,128)(2,1)}, bf16[20,160,128]{2,1,0:T(8,128)(2,1)}) custom-call(f32[8,25600]{1,0:T(8,128)} %bitcast.84, f32[16,25600]{1,0:T(8,128)} %bitcast.82), custom_call_target="tpu_custom_call" | custom-call | tf_op jit(solution)/shard_map/pack/pallas_call | solution.py:1009
  21.1 41.5 %gather_attn.1.wire = bf16[80,160,128]{2,1,0:T(8,128)(2,1)} custom-call(bf16[10,160,128]{2,1,0:T(8,128)(2,1)} %get-tuple-element.66.wire), custom_call_target="tpu_custom_call" | custom-call | bytes 120000000 | tf_op jit(solution)/shard_map/gather_attn/pallas_call | solution.py:513
  63.3 17.3 %attn_fwd.1 = (bf16[196,1280]{1,0:T(8,128)(2,1)}, bf16[208,1280]{1,0:T(8,128)(2,1)}, bf16[6,208,160]{2,1,0:T(8,128)(2,1)}, f32[4,208,208]{2,1,0:T(8,128)}, bf16[2,208,160]{2,1,0:T(8,128)(2,1)}) custom-call(s32[64]{0:T(128)} %select_reduce_fusion.1.order, bf16[196,1280]{1,0:T(8,128)(2,1)} %bitcast.78, f32[208,1]{1,0:T(8,128)} %copy.69.live, f32[2,1280]{1,0:T(2,128)} %gains.7, ...), custom_call_target="tpu_custom_call" | custom-call | tf_op jit(solution)/shard_map/attn_fwd/pallas_call | solution.py:1009
  81.4 73.9 %gather_mlp.1.wire = bf16[160,160,128]{2,1,0:T(8,128)(2,1)} custom-call(bf16[20,160,128]{2,1,0:T(8,128)(2,1)} %get-tuple-element.70.wire), custom_call_target="tpu_custom_call" | custom-call | bytes 240000000 | tf_op jit(solution)/shard_map/gather_mlp/pallas_call | solution.py:513
  155.9 25.2 %mlp.1 = (bf16[196,1280]{1,0:T(8,128)(2,1)}, bf16[196,1280]{1,0:T(8,128)(2,1)}, bf16[8,208,160]{2,1,0:T(8,128)(2,1)}, bf16[8,208,160]{2,1,0:T(8,128)(2,1)}, bf16...) custom-call(s32[128]{0:T(128)} %select_reduce_fusion.order, bf16[196,1280]{1,0:T(8,128)(2,1)} %bitcast.79, ...), custom_call_target="tpu_custom_call" | custom-call | tf_op jit(solution)/shard_map/mlp/pallas_call | solution.py:1009
  181.9 17.4 %mlp_tiles.1.stack = bf16[160,160,128]{2,1,0:T(8,128)(2,1)} custom-call(s32[128]{0:T(128)} %get-tuple-element.199.left_at, s32[128]{0:T(128)} %get-tuple-element.198.right_at, bf16[8,208,160]{2,1,0:T(8,128)(2,1)} %get-tuple-element.73.sec, bf16[8,208,160]{2,1,0:T(8,128)(2,1)} %get-tuple-element.74.act, bf16[8,208,160]{2,1,0:T(8,128)(2,1)} %get-tuple-element.75.gh_ref, ...), custom_call_target="tpu_custom_call" | custom-call | tf_op jit(solution)/shard_map/mlp_tiles/pallas_call | solution.py:1009
  199.3 84.2 %scatter_mlp.1 = (bf16[80,160,128]{2,1,0:T(8,128)(2,1)}, f32[2,2,8,160,128]{4,3,2,1,0:T(8,128)}, f32[2,2,8,160,128]{4,3,2,1,0:T(8,128)}, f32[1,2,8,160,128]{4,3,2,1,0:T(8,128)}, f32[1,2,8,160,128]{4,3,2,1,0:T(8,128)}) custom-call(bf16[160,160,128]{2,1,0:T(8,128)(2,1)} %mlp_tiles.1.stack, f32[16,25600]{1,0:T(8,128)} %bitcast.92, f32[16,25600]{1,0:T(8,128)} %bitcast.93, ...), custom_call_target="tpu_custom_call" | custom-call | bytes 250000000 | tf_op jit(solution)/shard_map/scatter_mlp/pallas_call | solution.py:606
  283.5 17.6 %mid_back.1 = (bf16[196,1280]{1,0:T(8,128)(2,1)}, f32[196,1280]{1,0:T(8,128)}, bf16[196,1280]{1,0:T(8,128)(2,1)}, f32[128,160]{1,0:T(8,128)}, bf16[6,208,160]{2,...) custom-call(s32[64]{0:T(128)} %select_reduce_fusion.1.order, ...), custom_call_target="tpu_custom_call" | custom-call | tf_op jit(solution)/shard_map/mid_back/pallas_call | solution.py:1009
  301.1 0.9 slice_add_fusion
  302.2 1.9 pad_maximum_fusion
  304.1 0.8 copy.71.live
  305.6 9.8 %attn_tiles.1.stack = bf16[80,160,128]{2,1,0:T(8,128)(2,1)} custom-call(s32[64]{0:T(128)} %get-tuple-element.197.left_at, s32[64]{0:T(128)} %get-tuple-element.196.right_at, bf16[8,208,160]{2,1,0:T(8,128)(2,1)} %get-tuple-element.87.nb_ref, bf16[2,208,160]{2,1,0:T(8,128)(2,1)} %get-tuple-element.83.att.att_ref, ...), custom_call_target="tpu_custom_call" | custom-call | tf_op jit(solution)/shard_map/attn_tiles/pallas_call | solution.py:1009
  315.4 60.7 %scatter_attn.1 = (bf16[40,160,128]{2,1,0:T(8,128)(2,1)}, f32[16,25600]{1,0:T(8,128)}, f32[16,25600]{1,0:T(8,128)}, bf16[16,25600]{1,0:T(8,128)(2,1)}, f32[16,25600]{1,0:T(8,128)}, /*index=5*/f32[16,25600]{1,0:T(8,128)}) custom-call(bf16[80,160,128]{2,1,0:T(8,128)(2,1)} %attn_tiles.1.stack, bf16[80,160,128]{2,1,0:T(8,128)(2,1)} %get-tuple-element.90.wire, ...), custom_call_target="tpu_custom_call" | custom-call | bytes 150000000 | tf_op jit(solution)/shard_map/scatter_attn/pallas_call | solution.py:606
  376.1 0.7 slice.88
  376.9 3.4 token_back.1
  380.3 0.8 reshape.104
  381.8 16.3 %gather_sums.1 = f32[8,112,128]{2,1,0:T(8,128)} custom-call(f32[1,112,128]{2,1,0:T(8,128)} %pad_bitcast_fusion.wire), custom_call_target="tpu_custom_call" | custom-call | bytes 12000000 | tf_op jit(solution)/shard_map/gather_sums/pallas_call | solution.py:513
  398.1 1.1 reduce_sum.29
  400.5 2.0 copy.72
  405.1 21.0 %soap_attn.1 = (f32[8,25600]{1,0:T(8,128)}, f32[8,25600]{1,0:T(8,128)}, bf16[8,25600]{1,0:T(8,128)(2,1)}, f32[8,25600]{1,0:T(8,128)}, f32[8,25600]{1,0:T(8,128)}) custom-call(bf16[40,160,128]{2,1,0:T(8,128)(2,1)} %get-tuple-element.101.wire, f32[1,2,8,160,128]{4,3,2,1,0:T(8,128)} %get-tuple-element.102.sq_left, ...), custom_call_target="tpu_custom_call" | custom-call | tf_op jit(solution)/shard_map/soap_attn/pallas_call | solution.py:1009
  426.1 1.2 copy.95
  427.3 0.9 copy-done.2
  428.1 1.2 copy.96
  429.8 0.9 copy.97
  430.7 1.2 copy.98
  431.9 0.9 copy-done
  432.8 1.2 copy.99
  (69 shorter events, 9.5 us)
Async XLA Ops:
  7.2 148.7 %all-reduce.9.cloned.1.call-start = ((), (), s32[]{:S(2)}) async-start(), calls=%async_computation | async-start | bytes 1024000 | tf_op jit(solution)/shard_map/psum | solution.py:1069
  12.6 50.1 %copy-start.4 = (bf16[128,160]{1,0:T(8,128)(2,1)}, bf16[128,160]{1,0:T(8,128)(2,1)S(1)}, u32[]{:S(2)}) copy-start(bf16[128,160]{1,0:T(8,128)(2,1)S(1)} %copy.67.rel_hi) | copy-start | bytes 122884
  63.3 17.4 %copy-start.9 = (f32[1280]{0:T(1024)S(1)}, f32[1280]{0:T(1024)}, u32[]{:S(2)}) copy-start(f32[1280]{0:T(1024)} %param.30) | copy-start | bytes 15364
  80.7 202.8 %all-reduce.13.cloned.1.call-start = ((), (), s32[]{:S(2)}) async-start(), calls=%async_computation.2 | async-start | bytes 2048000 | tf_op jit(solution)/shard_map/psum | solution.py:1078
  81.4 73.9 %copy-start.11 = (s32[1,128]{1,0:T(1,128)S(1)}, s32[1,128]{1,0:T(1,128)}, u32[]{:S(2)}) copy-start(s32[1,128]{1,0:T(1,128)} %param.33) | copy-start | bytes 1540
  181.1 195.0 %all-reduce.11.cloned.1.call-start = ((), (), s32[]{:S(2)}) async-start(), calls=%async_computation.1 | async-start | bytes 1024000 | tf_op jit(solution)/shard_map/psum | solution.py:1109
  301.0 3.8 copy-start.12
  301.1 4.3 copy-start.10
  301.1 4.4 copy-start.8
  301.1 4.5 %copy-start.7 = (f32[4,1280]{1,0:T(4,128)S(1)}, f32[4,1280]{1,0:T(4,128)}, u32[]{:S(2)}) copy-start(f32[4,1280]{1,0:T(4,128)} %get-tuple-element.98) | copy-start | bytes 61444
  380.3 20.2 %copy-start.5 = (f32[196,1280]{1,0:T(8,128)S(1)}, f32[196,1280]{1,0:T(8,128)}, u32[]{:S(2)}) copy-start(f32[196,1280]{1,0:T(8,128)} %get-tuple-element.96) | copy-start | bytes 3010564
  405.1 21.0 %copy-start.3 = (f32[16,25600]{1,0:T(8,128)S(1)}, f32[16,25600]{1,0:T(8,128)}, u32[]{:S(2)}) copy-start(f32[16,25600]{1,0:T(8,128)} %get-tuple-element.105) | copy-start | bytes 4915204
  426.1 2.0 copy-start.2
  428.1 1.7 copy-start.6
  428.1 2.6 copy-start.1
  430.7 2.0 copy-start
Sparse Core Ops, SparseCore 0:
  80.8 33.4 all-reduce.8
  181.3 36.2 all-reduce.12
  304.2 34.7 all-reduce.10

commit v6 on v5

--- a/solution.py
+++ b/solution.py
@@ -531,11 +531,13 @@
 AHEAD = 4
 
 
-def scatter_steps(stack, out, inbox, half, side_send, side_recv, line_send, line_recv, own, units):
+def scatter_steps(count, prepare, source, own_part, out, inbox, half,
+                  side_send, side_recv, line_send, line_recv, own, units, each=1):
     me = lax.axis_index("dp")
     z, x = me // 2, me % 2
     side = me + 1 - 2 * x
-    count = stack.shape[0] // 8
+    pieces = count // CHUNK
+    steps = 4 * pieces
 
     def line_at(j):
         return lax.rem(z + j, 4)
@@ -544,69 +546,75 @@
     for target in (side, 2 * line_at(1) + x, 2 * line_at(2) + x, 2 * line_at(3) + x):
         pl.semaphore_signal(barrier, inc=1, device_id={"dp": target}, device_id_type=MESH_ID)
     pl.semaphore_wait(barrier, 4)
-    steps = [(j, k) for j in (1, 2, 3, 4) for k in range(count // CHUNK)]
-
-    def to_side(j, k):
-        line = line_at(j)
+
+    def place(at):
+        j, k = lax.div(at, pieces), lax.rem(at, pieces)
+        return j, k, line_at(j + 1)
+
+    def to_side(at):
+        j, k, line = place(at)
         return pltpu.make_async_remote_copy(
-            src_ref=stack.at[pl.ds((2 * line + 1 - x) * count + CHUNK * k, CHUNK)],
+            src_ref=source(2 * line + 1 - x, line, k),
             dst_ref=inbox.at[pl.ds(line * count + CHUNK * k, CHUNK)],
-            send_sem=side_send.at[j - 1, k], recv_sem=side_recv.at[j - 1, k],
+            send_sem=side_send.at[j, k], recv_sem=side_recv.at[j, k],
             device_id={"dp": side}, device_id_type=MESH_ID)
 
-    def to_line(j, k):
-        line = line_at(j)
+    def to_line(at):
+        j, k, line = place(at)
         return pltpu.make_async_remote_copy(
             src_ref=half.at[pl.ds(line * count + CHUNK * k, CHUNK)],
             dst_ref=out.at[pl.ds(z * count + CHUNK * k, CHUNK)],
-            send_sem=line_send.at[j - 1, k], recv_sem=line_recv.at[j - 1, k],
+            send_sem=line_send.at[j, k], recv_sem=line_recv.at[j, k],
             device_id={"dp": 2 * line + x}, device_id_type=MESH_ID)
 
-    for step in steps[:AHEAD]:
-        to_side(*step).start()
-    keeps = []
-    units = list(units)
-    for at, (j, k) in enumerate(steps):
-        if units:
-            units.pop(0)()
-        to_side(j, k).wait_recv()
-        if at + AHEAD < len(steps):
-            to_side(*steps[at + AHEAD]).start()
-        line = line_at(j)
-
-        def add(i, carry):
-            to = line * count + CHUNK * k + i
-            total = stack[(2 * line + x) * count + CHUNK * k + i].astype(F32) + inbox[to].astype(F32)
-            half[to] = total.astype(BF)
-            return carry
-
-        lax.fori_loop(0, CHUNK, add, 0)
-        if j < 4:
-            to_line(j, k).start()
-        else:
-            place = pl.ds(line * count + CHUNK * k, CHUNK)
-            keep = pltpu.make_async_copy(half.at[place], out.at[place], own.at[k])
-            keep.start()
-            keeps.append(keep)
-    for unit in units:
-        unit()
-    for j, k in steps:
-        to_side(j, k).wait_send()
-        if j < 4:
-            to_line(j, k).wait_send()
-            to_line(j, k).wait_recv()
-    for keep in keeps:
-        keep.wait()
-
-
-def scatter_call(body, stack, args, outs, scratch, ident, cost, name):
-    count = stack.shape[0] // 8
-    shape = (4 * count,) + stack.shape[1:]
+    def keep(k):
+        return pltpu.make_async_copy(
+            half.at[pl.ds(z * count + CHUNK * k, CHUNK)], out.at[pl.ds(z * count + CHUNK * k, CHUNK)], own.at[k])
+
+    def send(at):
+        _, k, line = place(at)
+        prepare(2 * line + 1 - x, line, k)
+        to_side(at).start()
+
+    def first(at, carry):
+        send(at)
+        return carry
+
+    def step(at, carry):
+        _, k, line = place(at)
+        for i, unit in enumerate(units):
+            turn = i // 2 if i < 2 * each else i - each
+            pl.when(at == min(turn, steps - 1))(unit)
+        to_side(at).wait_recv()
+        pl.when(at + AHEAD < steps)(lambda: send(at + AHEAD))
+        own_part(2 * line + x, line, k)
+        pl.when(at < 3 * pieces)(lambda: to_line(at).start())
+        pl.when(at >= 3 * pieces)(lambda: keep(k).start())
+        return carry
+
+    def last(at, carry):
+        to_side(at).wait_send()
+
+        def lines():
+            to_line(at).wait_send()
+            to_line(at).wait_recv()
+
+        pl.when(at < 3 * pieces)(lines)
+        pl.when(at >= 3 * pieces)(lambda: keep(place(at)[1]).wait())
+        return carry
+
+    lax.fori_loop(0, AHEAD, first, 0)
+    lax.fori_loop(0, steps, step, 0)
+    lax.fori_loop(0, steps, last, 0)
+
+
+def scatter_call(body, count, tables, args, outs, scratch, ident, cost, name):
+    shape = (4 * count, SIDE, 128)
     pieces = count // CHUNK
     return pl.pallas_call(
         body,
         out_shape=[jax.ShapeDtypeStruct(shape, BF)] + [jax.ShapeDtypeStruct(*out) for out in outs],
-        in_specs=[VM] * (1 + len(args)),
+        in_specs=[SM] * len(tables) + [VM] * len(args),
         out_specs=[pl.BlockSpec(memory_space=pl.ANY)] + [VM] * len(outs),
         scratch_shapes=[pltpu.VMEM(shape, BF)] * 2 + [pltpu.SemaphoreType.DMA((4, pieces))] * 4
         + [pltpu.SemaphoreType.DMA((pieces,))] + [pltpu.VMEM(*item) for item in scratch],
@@ -614,26 +622,64 @@
             collective_id=ident, has_side_effects=True, vmem_limit_bytes=LIMIT),
         cost_estimate=pl.CostEstimate(flops=0, bytes_accessed=cost, transcendentals=0),
         name=name,
-    )(stack, *args)
-
-
-def scatter_mlp_body(stack, left_m, right_m, left_a, right_a, out, sq_left_m, sq_right_m, sq_left_a, sq_right_a, *wires):
+    )(*tables, *args)
+
+
+def scatter_mlp_body(left_at, right_at, sec, act, gh, go, left_m, right_m, left_a, right_a,
+                     out, sq_left_m, sq_right_m, sq_left_a, sq_right_a, inbox, half,
+                     side_send, side_recv, line_send, line_recv, own, lefts, rights, sent):
+    lefts[0:8], lefts[8:16] = sec[...], act[...]
+    rights[0:8], rights[8:16] = gh[...], go[...]
+    lane = lane_at((SIDE, 128))
+
+    def tiles(chunk, k, emit):
+        spare = None
+        for q in range(4):
+            s = 16 * chunk + 4 * k + q
+            tile = dot_tn(lefts[left_at[s]], rights[right_at[s]])
+            emit(q, tile[:, 0:128])
+            piece = jnp.concatenate([tile[:, 128:160], jnp.zeros((SIDE, 96), F32)], axis=1)
+            spare = piece if q == 0 else jnp.where(lane < 32 * q, spare, pltpu.roll(piece, 32 * q, 1))
+        emit(4, spare)
+
+    def prepare(chunk, line, k):
+        def emit(q, value):
+            sent[20 * line + CHUNK * k + q] = value.astype(BF)
+        tiles(chunk, k, emit)
+
+    def own_part(chunk, line, k):
+        def emit(q, value):
+            half[20 * line + CHUNK * k + q] = (value + inbox[20 * line + CHUNK * k + q].astype(F32)).astype(BF)
+        tiles(chunk, k, emit)
+
     units = []
     for flat, square in ((left_m, sq_left_m), (right_m, sq_right_m), (left_a, sq_left_a), (right_a, sq_right_a)):
         for g in range(square.shape[0]):
             units.append(lambda f=flat, r=8 * g, sq=square, g=g: flat_to_square(
                 lambda at: f[r : r + 8, pl.ds(at, 128)], sq.at[g]))
-    scatter_steps(stack, out, *wires, units)
+    scatter_steps(20, prepare, lambda chunk, line, k: sent.at[pl.ds(20 * line + CHUNK * k, CHUNK)], own_part,
+                  out, inbox, half, side_send, side_recv, line_send, line_recv, own, units)
 
 
 def scatter_attn_body(stack, wire, sq_left, sq_right, master, first, second,
-                      out, grad_out, new_out, copy_out, first_out, second_out, *rest):
-    wires, (sq_grad, sq_work) = rest[:-2], rest[-2:]
+                      out, grad_out, new_out, copy_out, first_out, second_out, inbox, half,
+                      side_send, side_recv, line_send, line_recv, own, sq_grad, sq_work):
     units = []
     for g in range(2):
         units += soap_units(g, g, wire, sq_left, sq_right, master, first, second,
                             grad_out, new_out, copy_out, first_out, second_out, sq_grad, sq_work)
-    scatter_steps(stack, out, *wires, units)
+
+    def own_part(chunk, line, k):
+        def add(i, carry):
+            to = 10 * line + CHUNK * k + i
+            half[to] = (stack[10 * chunk + CHUNK * k + i].astype(F32) + inbox[to].astype(F32)).astype(BF)
+            return carry
+
+        lax.fori_loop(0, CHUNK, add, 0)
+
+    scatter_steps(10, lambda chunk, line, k: None,
+                  lambda chunk, line, k: stack.at[pl.ds(10 * chunk + CHUNK * k, CHUNK)], own_part,
+                  out, inbox, half, side_send, side_recv, line_send, line_recv, own, units, 4)
 
 
 def norm_parts(x):
@@ -1078,17 +1124,11 @@
     second_sum = lax.psum(part_second, "mp")
     down_sum = lax.psum(part_down, "mp")
 
-    def mlp_tiles(left_at, right_at, sec, act, gh_ref, go_ref, wire, lefts, rights):
-        lefts[0:8], lefts[8:16] = sec[...], act[...]
-        rights[0:8], rights[8:16] = gh_ref[...], go_ref[...]
-        grad_tiles_body(left_at, right_at, 128, lambda i: lefts[i], lambda i: rights[i], wire)
-
-    stack_m, = call(
-        mlp_tiles, (xm, ym), (sec_blocks, act_blocks, gh, go), [((160, SIDE, 128), BF)],
-        [((16, ROWS, SIDE), BF)] * 2, "mlp_tiles")
     sum_m, sq_left_m, sq_right_m, sq_left_a, sq_right_a = scatter_call(
-        scatter_mlp_body, stack_m, (mlp_left[0], mlp_right[0], attn_left[0], attn_right[0]),
-        [((2, 2, 8, SIDE, 128), F32)] * 2 + [((1, 2, 8, SIDE, 128), F32)] * 2, [], 2, 250_000_000, "scatter_mlp")
+        scatter_mlp_body, 20, (xm, ym),
+        (sec_blocks, act_blocks, gh, go, mlp_left[0], mlp_right[0], attn_left[0], attn_right[0]),
+        [((2, 2, 8, SIDE, 128), F32)] * 2 + [((1, 2, 8, SIDE, 128), F32)] * 2,
+        [((16, ROWS, SIDE), BF)] * 2 + [((80, SIDE, 128), BF)], 2, 250_000_000, "scatter_mlp")
     second_sum, down_sum, sum_m = lax.optimization_barrier((second_sum, down_sum, sum_m))
 
     block_out, grad_middle, part_normed, rel_part, gm, gb, nb, sums_two, qkv_sums = call(
@@ -1120,7 +1160,7 @@
         return [(shape, F32), (shape, F32), (shape, BF), (shape, F32), (shape, F32)]
 
     sum_a, mg, mn, mc, mf, ms = scatter_call(
-        scatter_attn_body, stack_a, (sum_m, sq_left_m, sq_right_m, mlp_master[0], mlp_first[0], mlp_second[0]),
+        scatter_attn_body, 10, (), (stack_a, sum_m, sq_left_m, sq_right_m, mlp_master[0], mlp_first[0], mlp_second[0]),
         soap_outs(mlp_master.shape[1:]), [((2, 8, SIDE, 128), F32)] * 2, 4, 150_000_000, "scatter_attn")
     both_sum, sum_a = lax.optimization_barrier((both_sum, sum_a))
     normed_sum, rel_sum = both_sum[:t], both_sum[t:].reshape(-1)[:rel_size].astype(F32)

time: 441 us -> 421 us (0.955)
  Pallas kernels: 397 us -> 376 us
    pallas_call x8 -> x7, Pallas kernels: 120 us -> 103 us  [call(): pl.pallas_call(body, out_shape=[jax.ShapeDtypeStruct(shape, kind) for sha...]
    pallas_call x2, Pallas kernels: 145 us -> 139 us  [scatter_call(): pl.pallas_call(body, out_shape=[jax.ShapeDtypeStruct(shape, BF)] + [jax.S...]
  transfers between devices with their start and end apart: 3 -> 3, of which waited for: 0 -> 0; matrix products, arithmetic and copies ran while one was open for 1% -> 1% of each run, Pallas kernels for 56% -> 53%
where the time goes in v6:
time: 421 us; the launch traced here: 420 us
  Pallas kernels  376 us (89%)
  local copies, waits for them, and re-layouts  19.3 us (5%)
  between operations  14 us (3%)
  other arithmetic  9.98 us (2%)
    pallas_call x2, Pallas kernels, scatter_call(): pl.pallas_call(body, out_shape=[jax.ShapeDtypeStruct(shape, BF)] + [jax.S...  139 us
    pallas_call x3, Pallas kernels, gather(): pl.pallas_call(functools.partial(gather_body, piece), out_shape=jax.Shape...  135 us
    pallas_call x7, Pallas kernels, call(): pl.pallas_call(body, out_shape=[jax.ShapeDtypeStruct(shape, kind) for sha...  103 us
    unnamed x35, local copies, waits for them, and re-layouts  11.2 us
  transfers between devices with their start and end apart: 3, of which 0 were waited for; matrix products, arithmetic and copies ran while one was open for 1% of the time, Pallas kernels for 53%

profile of v6, /device:TPU:0, one launch (start us, length us, event | category | flops | bytes accessed | tf_op | source)
XLA Modules:
  0.0 420.1 jit_solution(13538318011366732797)
XLA Ops:
  7.2 0.7 copy.62
  8.4 1.3 select_reduce_fusion.1.order
  9.6 0.7 convert_bitcast_fusion
  10.3 1.4 reshape.100.qkv_bias
  11.7 0.8 copy.69.live
  12.6 8.6 %pack.1 = (bf16[10,160,128]{2,1,0:T(8,128)(2,1)}, bf16[20,160,128]{2,1,0:T(8,128)(2,1)}) custom-call(f32[8,25600]{1,0:T(8,128)} %bitcast.84, f32[16,25600]{1,0:T(8,128)} %bitcast.82), custom_call_target="tpu_custom_call" | custom-call | tf_op jit(solution)/shard_map/pack/pallas_call | solution.py:1055
  21.1 41.5 %gather_attn.1.wire = bf16[80,160,128]{2,1,0:T(8,128)(2,1)} custom-call(bf16[10,160,128]{2,1,0:T(8,128)(2,1)} %get-tuple-element.66.wire), custom_call_target="tpu_custom_call" | custom-call | bytes 120000000 | tf_op jit(solution)/shard_map/gather_attn/pallas_call | solution.py:513
  63.3 17.3 %attn_fwd.1 = (bf16[196,1280]{1,0:T(8,128)(2,1)}, bf16[208,1280]{1,0:T(8,128)(2,1)}, bf16[6,208,160]{2,1,0:T(8,128)(2,1)}, f32[4,208,208]{2,1,0:T(8,128)}, bf16[2,208,160]{2,1,0:T(8,128)(2,1)}) custom-call(s32[64]{0:T(128)} %select_reduce_fusion.1.order, bf16[196,1280]{1,0:T(8,128)(2,1)} %bitcast.78, f32[208,1]{1,0:T(8,128)} %copy.69.live, f32[2,1280]{1,0:T(2,128)} %gains.7, ...), custom_call_target="tpu_custom_call" | custom-call | tf_op jit(solution)/shard_map/attn_fwd/pallas_call | solution.py:1055
  80.8 0.7 reshape.101.up_bias
  81.4 73.9 %gather_mlp.1.wire = bf16[160,160,128]{2,1,0:T(8,128)(2,1)} custom-call(bf16[20,160,128]{2,1,0:T(8,128)(2,1)} %get-tuple-element.70.wire), custom_call_target="tpu_custom_call" | custom-call | bytes 240000000 | tf_op jit(solution)/shard_map/gather_mlp/pallas_call | solution.py:513
  155.9 25.2 %mlp.1 = (bf16[196,1280]{1,0:T(8,128)(2,1)}, bf16[196,1280]{1,0:T(8,128)(2,1)}, bf16[8,208,160]{2,1,0:T(8,128)(2,1)}, bf16[8,208,160]{2,1,0:T(8,128)(2,1)}, bf16...) custom-call(s32[128]{0:T(128)} %select_reduce_fusion.order, bf16[196,1280]{1,0:T(8,128)(2,1)} %bitcast.79, ...), custom_call_target="tpu_custom_call" | custom-call | tf_op jit(solution)/shard_map/mlp/pallas_call | solution.py:1055
  181.9 84.4 %scatter_mlp.1 = (bf16[80,160,128]{2,1,0:T(8,128)(2,1)}, f32[2,2,8,160,128]{4,3,2,1,0:T(8,128)}, f32[2,2,8,160,128]{4,3,2,1,0:T(8,128)}, f32[1,2,8,160,128]{4,3,2,1,0:T(8,128)}, f32[1,2,8,160,128]{4,3,2,1,0:T(8,128)}) custom-call(s32[128]{0:T(128)} %get-tuple-element.199.left_at, s32[128]{0:T(128)} %get-tuple-element.198.right_at, ...), custom_call_target="tpu_custom_call" | custom-call | bytes 250000000 | tf_op jit(solution)/shard_map/scatter_mlp/pallas_call | solution.py:614
  266.4 17.6 %mid_back.1 = (bf16[196,1280]{1,0:T(8,128)(2,1)}, f32[196,1280]{1,0:T(8,128)}, bf16[196,1280]{1,0:T(8,128)(2,1)}, f32[128,160]{1,0:T(8,128)}, bf16[6,208,160]{2,...) custom-call(s32[64]{0:T(128)} %select_reduce_fusion.1.order, ...), custom_call_target="tpu_custom_call" | custom-call | tf_op jit(solution)/shard_map/mid_back/pallas_call | solution.py:1055
  284.0 0.9 slice_add_fusion
  285.1 1.9 pad_maximum_fusion
  287.0 0.8 copy.71.live
  288.5 9.9 %attn_tiles.1.stack = bf16[80,160,128]{2,1,0:T(8,128)(2,1)} custom-call(s32[64]{0:T(128)} %get-tuple-element.197.left_at, s32[64]{0:T(128)} %get-tuple-element.196.right_at, bf16[8,208,160]{2,1,0:T(8,128)(2,1)} %get-tuple-element.87.nb_ref, bf16[2,208,160]{2,1,0:T(8,128)(2,1)} %get-tuple-element.83.att.att_ref, ...), custom_call_target="tpu_custom_call" | custom-call | tf_op jit(solution)/shard_map/attn_tiles/pallas_call | solution.py:1055
  298.4 54.3 %scatter_attn.1 = (bf16[40,160,128]{2,1,0:T(8,128)(2,1)}, f32[16,25600]{1,0:T(8,128)}, f32[16,25600]{1,0:T(8,128)}, bf16[16,25600]{1,0:T(8,128)(2,1)}, f32[16,25600]{1,0:T(8,128)}, /*index=5*/f32[16,25600]{1,0:T(8,128)}) custom-call(bf16[80,160,128]{2,1,0:T(8,128)(2,1)} %attn_tiles.1.stack, bf16[80,160,128]{2,1,0:T(8,128)(2,1)} %get-tuple-element.90.wire, ...), custom_call_target="tpu_custom_call" | custom-call | bytes 150000000 | tf_op jit(solution)/shard_map/scatter_attn/pallas_call | solution.py:614
  352.7 0.7 slice.88
  353.4 3.4 token_back.1
  356.8 0.8 reshape.104
  358.3 19.4 %gather_sums.1 = f32[8,112,128]{2,1,0:T(8,128)} custom-call(f32[1,112,128]{2,1,0:T(8,128)} %pad_bitcast_fusion.wire), custom_call_target="tpu_custom_call" | custom-call | bytes 12000000 | tf_op jit(solution)/shard_map/gather_sums/pallas_call | solution.py:513
  377.8 1.1 reduce_sum.29
  380.2 2.0 copy.72
  384.8 21.0 %soap_attn.1 = (f32[8,25600]{1,0:T(8,128)}, f32[8,25600]{1,0:T(8,128)}, bf16[8,25600]{1,0:T(8,128)(2,1)}, f32[8,25600]{1,0:T(8,128)}, f32[8,25600]{1,0:T(8,128)}) custom-call(bf16[40,160,128]{2,1,0:T(8,128)(2,1)} %get-tuple-element.101.wire, f32[1,2,8,160,128]{4,3,2,1,0:T(8,128)} %get-tuple-element.102.sq_left, ...), custom_call_target="tpu_custom_call" | custom-call | tf_op jit(solution)/shard_map/soap_attn/pallas_call | solution.py:1055
  405.7 1.2 copy.95
  406.9 0.9 copy-done.2
  407.8 1.2 copy.96
  409.5 0.9 copy.97
  410.4 1.2 copy.98
  411.5 0.9 copy-done
  412.4 1.2 copy.99
  (68 shorter events, 8.8 us)
Async XLA Ops:
  7.2 148.7 %all-reduce.9.cloned.1.call-start = ((), (), s32[]{:S(2)}) async-start(), calls=%async_computation | async-start | bytes 1024000 | tf_op jit(solution)/shard_map/psum | solution.py:1115
  12.6 50.1 %copy-start.4 = (bf16[128,160]{1,0:T(8,128)(2,1)}, bf16[128,160]{1,0:T(8,128)(2,1)S(1)}, u32[]{:S(2)}) copy-start(bf16[128,160]{1,0:T(8,128)(2,1)S(1)} %copy.67.rel_hi) | copy-start | bytes 122884
  63.3 17.4 %copy-start.9 = (f32[1280]{0:T(1024)S(1)}, f32[1280]{0:T(1024)}, u32[]{:S(2)}) copy-start(f32[1280]{0:T(1024)} %param.30) | copy-start | bytes 15364
  80.7 185.7 %all-reduce.13.cloned.1.call-start = ((), (), s32[]{:S(2)}) async-start(), calls=%async_computation.2 | async-start | bytes 2048000 | tf_op jit(solution)/shard_map/psum | solution.py:1124
  81.4 73.9 %copy-start.11 = (s32[1,128]{1,0:T(1,128)S(1)}, s32[1,128]{1,0:T(1,128)}, u32[]{:S(2)}) copy-start(s32[1,128]{1,0:T(1,128)} %param.33) | copy-start | bytes 1540
  181.2 171.5 %all-reduce.11.cloned.1.call-start = ((), (), s32[]{:S(2)}) async-start(), calls=%async_computation.1 | async-start | bytes 1024000 | tf_op jit(solution)/shard_map/psum | solution.py:1149
  284.0 3.8 copy-start.12
  284.0 4.3 %copy-start.10 = (f32[8,160]{1,0:T(8,128)S(1)}, f32[8,160]{1,0:T(8,128)}, u32[]{:S(2)}) copy-start(f32[8,160]{1,0:T(8,128)} %get-tuple-element.100) | copy-start | bytes 15364
  284.0 4.4 %copy-start.8 = (f32[6,160]{1,0:T(8,128)S(1)}, f32[6,160]{1,0:T(8,128)}, u32[]{:S(2)}) copy-start(f32[6,160]{1,0:T(8,128)} %get-tuple-element.99) | copy-start | bytes 11524
  284.0 4.5 %copy-start.7 = (f32[4,1280]{1,0:T(4,128)S(1)}, f32[4,1280]{1,0:T(4,128)}, u32[]{:S(2)}) copy-start(f32[4,1280]{1,0:T(4,128)} %get-tuple-element.98) | copy-start | bytes 61444
  356.8 23.3 %copy-start.5 = (f32[196,1280]{1,0:T(8,128)S(1)}, f32[196,1280]{1,0:T(8,128)}, u32[]{:S(2)}) copy-start(f32[196,1280]{1,0:T(8,128)} %get-tuple-element.96) | copy-start | bytes 3010564
  384.8 21.0 %copy-start.3 = (f32[16,25600]{1,0:T(8,128)S(1)}, f32[16,25600]{1,0:T(8,128)}, u32[]{:S(2)}) copy-start(f32[16,25600]{1,0:T(8,128)} %get-tuple-element.105) | copy-start | bytes 4915204
  405.7 2.0 copy-start.2
  407.8 1.7 copy-start.6
  407.8 2.6 copy-start.1
  410.4 2.0 copy-start
Sparse Core Ops, SparseCore 0:
  80.8 33.4 all-reduce.8
  181.3 36.4 all-reduce.12
  287.1 34.9 all-reduce.10

commit v7 on v6

--- a/solution.py
+++ b/solution.py
@@ -411,10 +411,15 @@
         wire[base + 5 * half + 4] = spare.astype(BF)
 
 
-def pack_body(attn, mlp, wire_attn, wire_mlp, square):
-    pack_eight(attn, 0, wire_attn, 0, square)
-    pack_eight(mlp, 0, wire_mlp, 0, square)
-    pack_eight(mlp, 8, wire_mlp, 10, square)
+def pack_attn_body(attn, wire, square):
+    pack_eight(attn, 0, wire, 0, square)
+
+
+def pack_mlp_units(mlp, wire, square):
+    return [
+        lambda: pack_eight(mlp, 0, wire, 0, square),
+        lambda: pack_eight(mlp, 8, wire, 10, square),
+    ]
 
 
 def unpack_narrow(wire, narrow, groups):
@@ -443,7 +448,11 @@
 MESH_ID = pl.DeviceIdType.MESH
 
 
-def gather_body(piece, wire, out, send_sem, recv_sem, own_sem):
+def gather_body(piece, inputs, outputs, make_units, wire, *refs):
+    args, refs = refs[:inputs], refs[inputs:]
+    out, outs, refs = refs[0], refs[1 : 1 + outputs], refs[1 + outputs :]
+    send_sem, recv_sem, own_sem = refs[:3]
+    units = make_units(*args, *outs, *refs[3:]) if make_units else []
     count = wire.shape[0]
     pieces = count // piece
     me = lax.axis_index("dp")
@@ -480,7 +489,14 @@
         pl.when(z > 0)(lambda k=k: copy(2, down, me, k, True).start())
     keep = pltpu.make_async_copy(wire, out.at[pl.ds(me * count, count)], own_sem)
     keep.start()
-
+    slots = 1 + 3 * pieces
+
+    def work(slot):
+        for i, unit in enumerate(units):
+            if i * slots // len(units) == slot:
+                unit()
+
+    work(0)
     for d in range(1, 4):
         for k in range(pieces):
             def from_below():
@@ -497,6 +513,7 @@
 
             pl.when(z >= d)(from_below)
             pl.when(z + d <= 3)(from_above)
+            work(1 + (d - 1) * pieces + k)
 
     keep.wait()
     for k in range(pieces):
@@ -508,23 +525,25 @@
             pl.when((line >= z) & (z > 0))(lambda: copy(2, down, origin, k).wait_send())
 
 
-def gather(wire, ident, name, piece=5):
+def gather(wire, ident, name, piece=5, make_units=None, args=(), outs=(), scratch=()):
     count = wire.shape[0]
-    return pl.pallas_call(
-        functools.partial(gather_body, piece),
-        out_shape=jax.ShapeDtypeStruct((8 * count,) + wire.shape[1:], wire.dtype),
-        in_specs=[VM],
-        out_specs=pl.BlockSpec(memory_space=pl.ANY),
+    results = pl.pallas_call(
+        functools.partial(gather_body, piece, len(args), len(outs), make_units),
+        out_shape=[jax.ShapeDtypeStruct((8 * count,) + wire.shape[1:], wire.dtype)]
+        + [jax.ShapeDtypeStruct(*out) for out in outs],
+        in_specs=[VM] * (1 + len(args)),
+        out_specs=[pl.BlockSpec(memory_space=pl.ANY)] + [VM] * len(outs),
         scratch_shapes=[
             pltpu.SemaphoreType.DMA((3, 4, count // piece)),
             pltpu.SemaphoreType.DMA((8, count // piece)),
             pltpu.SemaphoreType.DMA,
-        ],
+        ] + [pltpu.VMEM(*item) for item in scratch],
         compiler_params=pltpu.CompilerParams(
             collective_id=ident, has_side_effects=True, vmem_limit_bytes=LIMIT),
         cost_estimate=pl.CostEstimate(flops=0, bytes_accessed=count * 12_000_000, transcendentals=0),
         name=name,
-    )(wire)
+    )(wire, *args)
+    return results if outs else results[0]
 
 
 CHUNK = 5
@@ -625,60 +644,60 @@
     )(*tables, *args)
 
 
+def tile_steps(count, left_at, right_at, lefts, rights, inbox, half, sent):
+    lane = lane_at((SIDE, 128))
+
+    def tiles(chunk, k, emit):
+        spare = None
+        for q in range(4):
+            s = count // 5 * 4 * chunk + 4 * k + q
+            tile = dot_tn(lefts[left_at[s]], rights[right_at[s]])
+            emit(q, tile[:, 0:128])
+            piece = jnp.concatenate([tile[:, 128:160], jnp.zeros((SIDE, 96), F32)], axis=1)
+            spare = piece if q == 0 else jnp.where(lane < 32 * q, spare, pltpu.roll(piece, 32 * q, 1))
+        emit(4, spare)
+
+    def prepare(chunk, line, k):
+        def emit(q, value):
+            sent[count * line + CHUNK * k + q] = value.astype(BF)
+        tiles(chunk, k, emit)
+
+    def source(chunk, line, k):
+        return sent.at[pl.ds(count * line + CHUNK * k, CHUNK)]
+
+    def own_part(chunk, line, k):
+        def emit(q, value):
+            at = count * line + CHUNK * k + q
+            half[at] = (value + inbox[at].astype(F32)).astype(BF)
+        tiles(chunk, k, emit)
+
+    return prepare, source, own_part
+
+
 def scatter_mlp_body(left_at, right_at, sec, act, gh, go, left_m, right_m, left_a, right_a,
                      out, sq_left_m, sq_right_m, sq_left_a, sq_right_a, inbox, half,
                      side_send, side_recv, line_send, line_recv, own, lefts, rights, sent):
     lefts[0:8], lefts[8:16] = sec[...], act[...]
     rights[0:8], rights[8:16] = gh[...], go[...]
-    lane = lane_at((SIDE, 128))
-
-    def tiles(chunk, k, emit):
-        spare = None
-        for q in range(4):
-            s = 16 * chunk + 4 * k + q
-            tile = dot_tn(lefts[left_at[s]], rights[right_at[s]])
-            emit(q, tile[:, 0:128])
-            piece = jnp.concatenate([tile[:, 128:160], jnp.zeros((SIDE, 96), F32)], axis=1)
-            spare = piece if q == 0 else jnp.where(lane < 32 * q, spare, pltpu.roll(piece, 32 * q, 1))
-        emit(4, spare)
-
-    def prepare(chunk, line, k):
-        def emit(q, value):
-            sent[20 * line + CHUNK * k + q] = value.astype(BF)
-        tiles(chunk, k, emit)
-
-    def own_part(chunk, line, k):
-        def emit(q, value):
-            half[20 * line + CHUNK * k + q] = (value + inbox[20 * line + CHUNK * k + q].astype(F32)).astype(BF)
-        tiles(chunk, k, emit)
-
     units = []
     for flat, square in ((left_m, sq_left_m), (right_m, sq_right_m), (left_a, sq_left_a), (right_a, sq_right_a)):
         for g in range(square.shape[0]):
             units.append(lambda f=flat, r=8 * g, sq=square, g=g: flat_to_square(
                 lambda at: f[r : r + 8, pl.ds(at, 128)], sq.at[g]))
-    scatter_steps(20, prepare, lambda chunk, line, k: sent.at[pl.ds(20 * line + CHUNK * k, CHUNK)], own_part,
+    scatter_steps(20, *tile_steps(20, left_at, right_at, lefts, rights, inbox, half, sent),
                   out, inbox, half, side_send, side_recv, line_send, line_recv, own, units)
 
 
-def scatter_attn_body(stack, wire, sq_left, sq_right, master, first, second,
+def scatter_attn_body(left_at, right_at, nb, att, gm, gb, wire, sq_left, sq_right, master, first, second,
                       out, grad_out, new_out, copy_out, first_out, second_out, inbox, half,
-                      side_send, side_recv, line_send, line_recv, own, sq_grad, sq_work):
+                      side_send, side_recv, line_send, line_recv, own, lefts, rights, sent, sq_grad, sq_work):
+    lefts[0:8], lefts[8:10] = nb[...], att[...]
+    rights[0:6], rights[6:14] = gm[...], gb[...]
     units = []
     for g in range(2):
         units += soap_units(g, g, wire, sq_left, sq_right, master, first, second,
                             grad_out, new_out, copy_out, first_out, second_out, sq_grad, sq_work)
-
-    def own_part(chunk, line, k):
-        def add(i, carry):
-            to = 10 * line + CHUNK * k + i
-            half[to] = (stack[10 * chunk + CHUNK * k + i].astype(F32) + inbox[to].astype(F32)).astype(BF)
-            return carry
-
-        lax.fori_loop(0, CHUNK, add, 0)
-
-    scatter_steps(10, lambda chunk, line, k: None,
-                  lambda chunk, line, k: stack.at[pl.ds(10 * chunk + CHUNK * k, CHUNK)], own_part,
+    scatter_steps(10, *tile_steps(10, left_at, right_at, lefts, rights, inbox, half, sent),
                   out, inbox, half, side_send, side_recv, line_send, line_recv, own, units, 4)
 
 
@@ -839,23 +858,6 @@
     lax.fori_loop(0, 8, down, 0)
     for n in range(8):
         part_down[:, SIDE * n : SIDE * n + SIDE] = block[n][0:t, :].astype(BF)
-
-
-def grad_tiles_body(left_at, right_at, count, read_left, read_right, wire):
-    lane = lane_at((SIDE, 128))
-
-    def body(g, carry):
-        spare = None
-        for q in range(4):
-            s = 4 * g + q
-            tile = dot_tn(read_left(left_at[s]), read_right(right_at[s]))
-            wire[5 * g + q] = tile[:, 0:128].astype(BF)
-            piece = jnp.concatenate([tile[:, 128:160], jnp.zeros((SIDE, 96), F32)], axis=1)
-            spare = piece if q == 0 else jnp.where(lane < 32 * q, spare, pltpu.roll(piece, 32 * q, 1))
-        wire[5 * g + 4] = spare.astype(BF)
-        return carry
-
-    lax.fori_loop(0, count // 4, body, 0)
 
 
 def mid_back_body(order, tokens, live, cotangent, branch, down_sum, second_sum, gains, out_biases,
@@ -987,13 +989,6 @@
     ]
 
 
-def soap_attn_body(wire, sq_left, sq_right, master, first, second,
-                   grad_out, new_out, copy_out, first_out, second_out, sq_grad, sq_work):
-    for unit in soap_units(0, 0, wire, sq_left, sq_right, master, first, second,
-                           grad_out, new_out, copy_out, first_out, second_out, sq_grad, sq_work):
-        unit()
-
-
 def build(mesh):
     placed = (
         P("dp", None, None),
@@ -1101,10 +1096,11 @@
     ya = jnp.where(own_a < 48, own_a % 6, 6 + (own_a - 48) % 8)
     xm, ym = own_m // 8, (own_m // 64) * 8 + own_m % 8
 
-    wire_a, wire_m = call(
-        pack_body, (), (attn_master[0], mlp_master[0]),
-        [((10, SIDE, 128), BF), ((20, SIDE, 128), BF)], [((2, 8, SIDE, 128), F32)], "pack")
-    all_a = gather(wire_a, 0, "gather_attn")
+    wire_a, = call(
+        pack_attn_body, (), (attn_master[0],), [((10, SIDE, 128), BF)], [((2, 8, SIDE, 128), F32)], "pack")
+    all_a, wire_m = gather(
+        wire_a, 0, "gather_attn", 5, pack_mlp_units, (mlp_master[0],), [((20, SIDE, 128), BF)],
+        [((2, 8, SIDE, 128), F32)])
 
     part, normed, mixed, probs, att = call(
         attn_fwd_body, (ord_a,),
@@ -1148,20 +1144,13 @@
     rel_flat = jnp.pad(rel_fold.reshape(-1).astype(BF), (0, rel_rows * width - rel_size)).reshape(rel_rows, width)
     both_sum = lax.psum(jnp.concatenate([part_normed, rel_flat], axis=0), "mp")
 
-    def attn_tiles(left_at, right_at, nb_ref, att_ref, gm_ref, gb_ref, wire, lefts, rights):
-        lefts[0:8], lefts[8:10] = nb_ref[...], att_ref[...]
-        rights[0:6], rights[6:14] = gm_ref[...], gb_ref[...]
-        grad_tiles_body(left_at, right_at, 64, lambda i: lefts[i], lambda i: rights[i], wire)
-
-    stack_a, = call(
-        attn_tiles, (xa, ya), (nb, att, gm, gb), [((80, SIDE, 128), BF)],
-        [((10, ROWS, SIDE), BF), ((14, ROWS, SIDE), BF)], "attn_tiles")
     def soap_outs(shape):
         return [(shape, F32), (shape, F32), (shape, BF), (shape, F32), (shape, F32)]
 
     sum_a, mg, mn, mc, mf, ms = scatter_call(
-        scatter_attn_body, 10, (), (stack_a, sum_m, sq_left_m, sq_right_m, mlp_master[0], mlp_first[0], mlp_second[0]),
-        soap_outs(mlp_master.shape[1:]), [((2, 8, SIDE, 128), F32)] * 2, 4, 150_000_000, "scatter_attn")
+        scatter_attn_body, 10, (xa, ya), (nb, att, gm, gb, sum_m, sq_left_m, sq_right_m, mlp_master[0], mlp_first[0], mlp_second[0]),
+        soap_outs(mlp_master.shape[1:]),
+        [((10, ROWS, SIDE), BF), ((14, ROWS, SIDE), BF), ((40, SIDE, 128), BF)] + [((2, 8, SIDE, 128), F32)] * 2, 4, 150_000_000, "scatter_attn")
     both_sum, sum_a = lax.optimization_barrier((both_sum, sum_a))
     normed_sum, rel_sum = both_sum[:t], both_sum[t:].reshape(-1)[:rel_size].astype(F32)
     tokens_grad, sums_one = call(
@@ -1171,7 +1160,11 @@
     edges = np.cumsum([0] + [v.shape[0] for v in small])
     lines = -(-int(edges[-1]) // 1024) * 8
     small = jnp.pad(jnp.concatenate(small), (0, lines * 128 - int(edges[-1]))).reshape(1, lines, 128)
-    total = jnp.sum(gather(small, 3, "gather_sums", 1), axis=0).reshape(-1)
+    gathered, ag, an, ac, af, as_ = gather(
+        small, 3, "gather_sums", 1, functools.partial(soap_units, 0, 0),
+        (sum_a, sq_left_a, sq_right_a, attn_master[0], attn_first[0], attn_second[0]),
+        soap_outs(attn_master.shape[1:]), [((2, 8, SIDE, 128), F32)] * 2)
+    total = jnp.sum(gathered, axis=0).reshape(-1)
     one, two, qkv_grad, up_grad, rel_grad = [total[edges[i]:edges[i + 1]] for i in range(5)]
     one, two = one.reshape(2, width), two.reshape(4, width)
     gains_grad = jnp.stack([one[0], two[0]])
@@ -1179,9 +1172,6 @@
     outb_grad = jnp.stack([two[3], two[2]])
     rel_grad = rel_grad.reshape(rel_pos.shape)
 
-    ag, an, ac, af, as_ = call(
-        soap_attn_body, (), (sum_a, sq_left_a, sq_right_a, attn_master[0], attn_first[0], attn_second[0]),
-        soap_outs(attn_master.shape[1:]), [((2, 8, SIDE, 128), F32)] * 2, "soap_attn")
     return (block_out[None], tokens_grad[None], gains_grad, biases_grad, outb_grad, qkv_grad, up_grad, rel_grad,
             *(value[None] for value in (ag, mg, an, mn, ac, mc, af, as_, mf, ms)))
 

time: 421 us -> 404 us (0.960)
  Pallas kernels: 376 us -> 356 us
    pallas_call x7 -> x5, Pallas kernels: 103 us -> 67.4 us  [call(): pl.pallas_call(body, out_shape=[jax.ShapeDtypeStruct(shape, kind) for sha...]
    pallas_call x3, Pallas kernels: 135 us -> 145 us  [gather(): pl.pallas_call(functools.partial(gather_body, piece, len(args), len(outs)...]
    pallas_call x2, Pallas kernels: 139 us -> 143 us  [scatter_call(): pl.pallas_call(body, out_shape=[jax.ShapeDtypeStruct(shape, BF)] + [jax.S...]
    unnamed x35 -> x50, local copies, waits for them, and re-layouts: 11.2 us -> 14.8 us
  transfers between devices with their start and end apart: 3 -> 3, of which waited for: 0 -> 0; matrix products, arithmetic and copies ran while one was open for 1% -> 1% of each run, Pallas kernels for 53% -> 54%
where the time goes in v7:
time: 404 us; the launch traced here: 403 us
  Pallas kernels  356 us (88%)
  local copies, waits for them, and re-layouts  22.8 us (6%)
  between operations  14 us (3%)
  other arithmetic  10 us (2%)
    pallas_call x3, Pallas kernels, gather(): pl.pallas_call(functools.partial(gather_body, piece, len(args), len(outs)...  145 us
    pallas_call x2, Pallas kernels, scatter_call(): pl.pallas_call(body, out_shape=[jax.ShapeDtypeStruct(shape, BF)] + [jax.S...  143 us
    pallas_call x5, Pallas kernels, call(): pl.pallas_call(body, out_shape=[jax.ShapeDtypeStruct(shape, kind) for sha...  67.4 us
    unnamed x50, local copies, waits for them, and re-layouts  14.8 us
  transfers between devices with their start and end apart: 3, of which 0 were waited for; matrix products, arithmetic and copies ran while one was open for 1% of the time, Pallas kernels for 54%

profile of v7, /device:TPU:0, one launch (start us, length us, event | category | flops | bytes accessed | tf_op | source)
XLA Modules:
  0.0 403.0 jit_solution(6987167569493887133)
XLA Ops:
  7.2 0.7 copy.62
  8.4 1.3 select_reduce_fusion.1.order
  10.3 1.4 reshape.100.qkv_bias
  11.7 0.8 copy.69.live
  12.6 3.9 pack.1.wire
  17.1 43.0 %gather_attn.1 = (bf16[80,160,128]{2,1,0:T(8,128)(2,1)}, bf16[20,160,128]{2,1,0:T(8,128)(2,1)}) custom-call(bf16[10,160,128]{2,1,0:T(8,128)(2,1)} %pack.1.wire, f32[16,25600]{1,0:T(8,128)} %bitcast.82), custom_call_target="tpu_custom_call" | custom-call | bytes 120000000 | tf_op jit(solution)/shard_map/gather_attn/pallas_call | solution.py:530
  60.2 17.3 %attn_fwd.1 = (bf16[196,1280]{1,0:T(8,128)(2,1)}, bf16[208,1280]{1,0:T(8,128)(2,1)}, bf16[6,208,160]{2,1,0:T(8,128)(2,1)}, f32[4,208,208]{2,1,0:T(8,128)}, bf16[2,208,160]{2,1,0:T(8,128)(2,1)}) custom-call(s32[64]{0:T(128)} %select_reduce_fusion.1.order, bf16[196,1280]{1,0:T(8,128)(2,1)} %bitcast.78, f32[208,1]{1,0:T(8,128)} %copy.69.live, f32[2,1280]{1,0:T(2,128)} %gains.7, ...), custom_call_target="tpu_custom_call" | custom-call | tf_op jit(solution)/shard_map/attn_fwd/pallas_call | solution.py:1050
  78.3 73.9 %gather_mlp.1.wire = bf16[160,160,128]{2,1,0:T(8,128)(2,1)} custom-call(bf16[20,160,128]{2,1,0:T(8,128)(2,1)} %get-tuple-element.71.wire), custom_call_target="tpu_custom_call" | custom-call | bytes 240000000 | tf_op jit(solution)/shard_map/gather_mlp/pallas_call | solution.py:530
  152.8 25.2 %mlp.1 = (bf16[196,1280]{1,0:T(8,128)(2,1)}, bf16[196,1280]{1,0:T(8,128)(2,1)}, bf16[8,208,160]{2,1,0:T(8,128)(2,1)}, bf16[8,208,160]{2,1,0:T(8,128)(2,1)}, bf16...) custom-call(s32[128]{0:T(128)} %select_reduce_fusion.order, bf16[196,1280]{1,0:T(8,128)(2,1)} %bitcast.79, ...), custom_call_target="tpu_custom_call" | custom-call | tf_op jit(solution)/shard_map/mlp/pallas_call | solution.py:1050
  178.8 84.7 %scatter_mlp.1 = (bf16[80,160,128]{2,1,0:T(8,128)(2,1)}, f32[2,2,8,160,128]{4,3,2,1,0:T(8,128)}, f32[2,2,8,160,128]{4,3,2,1,0:T(8,128)}, f32[1,2,8,160,128]{4,3,2,1,0:T(8,128)}, f32[1,2,8,160,128]{4,3,2,1,0:T(8,128)}) custom-call(s32[128]{0:T(128)} %get-tuple-element.201.left_at, s32[128]{0:T(128)} %get-tuple-element.200.right_at, ...), custom_call_target="tpu_custom_call" | custom-call | bytes 250000000 | tf_op jit(solution)/shard_map/scatter_mlp/pallas_call | solution.py:633
  263.5 17.6 %mid_back.1 = (bf16[196,1280]{1,0:T(8,128)(2,1)}, f32[196,1280]{1,0:T(8,128)}, bf16[196,1280]{1,0:T(8,128)(2,1)}, f32[128,160]{1,0:T(8,128)}, bf16[6,208,160]{2,...) custom-call(s32[64]{0:T(128)} %select_reduce_fusion.1.order, ...), custom_call_target="tpu_custom_call" | custom-call | tf_op jit(solution)/shard_map/mid_back/pallas_call | solution.py:1050
  281.1 0.9 slice_add_fusion
  282.2 1.9 pad_maximum_fusion
  284.1 0.8 copy.71.live
  285.5 58.6 %scatter_attn.1 = (bf16[40,160,128]{2,1,0:T(8,128)(2,1)}, f32[16,25600]{1,0:T(8,128)}, f32[16,25600]{1,0:T(8,128)}, bf16[16,25600]{1,0:T(8,128)(2,1)}, f32[16,25600]{1,0:T(8,128)}, /*index=5*/f32[16,25600]{1,0:T(8,128)}) custom-call(s32[64]{0:T(128)} %get-tuple-element.199.left_at, s32[64]{0:T(128)} %get-tuple-element.198.right_at, ...), custom_call_target="tpu_custom_call" | custom-call | bytes 150000000 | tf_op jit(solution)/shard_map/scatter_attn/pallas_call | solution.py:633
  344.2 0.7 slice.88
  344.9 3.4 token_back.1
  348.3 0.7 reshape.104
  349.8 28.2 %gather_sums.1 = (f32[8,112,128]{2,1,0:T(8,128)}, f32[8,25600]{1,0:T(8,128)}, f32[8,25600]{1,0:T(8,128)}, bf16[8,25600]{1,0:T(8,128)(2,1)}, f32[8,25600]{1,0:T(8,128)}, /*index=5*/f32[8,25600]{1,0:T(8,128)}) custom-call(f32[1,112,128]{2,1,0:T(8,128)} %pad_bitcast_fusion.wire, bf16[40,160,128]{2,1,0:T(8,128)(2,1)} %get-tuple-element.102.refs_0_, ...), custom_call_target="tpu_custom_call" | custom-call | bytes 12000000 | tf_op jit(solution)/shard_map/gather_sums/pallas_call | solution.py:530
  378.0 1.1 reduce_sum.29
  380.5 2.0 copy.72
  385.1 0.9 copy.100
  386.0 1.2 copy.101
  387.7 0.9 copy.102
  388.6 1.2 copy.103
  389.8 0.8 copy.104
  390.6 0.9 copy.105
  391.5 0.9 copy.106
  392.4 0.9 copy.107
  393.3 1.2 copy.108
  394.4 0.9 copy-done
  395.3 1.2 copy.109
  (81 shorter events, 10.3 us)
Async XLA Ops:
  7.2 145.6 %all-reduce.9.cloned.1.call-start = ((), (), s32[]{:S(2)}) async-start(), calls=%async_computation | async-start | bytes 1024000 | tf_op jit(solution)/shard_map/psum | solution.py:1111
  12.6 47.6 %copy-start.4 = (bf16[128,160]{1,0:T(8,128)(2,1)}, bf16[128,160]{1,0:T(8,128)(2,1)S(1)}, u32[]{:S(2)}) copy-start(bf16[128,160]{1,0:T(8,128)(2,1)S(1)} %copy.67.rel_hi) | copy-start | bytes 122884
  60.2 17.4 %copy-start.14 = (f32[1280]{0:T(1024)S(1)}, f32[1280]{0:T(1024)}, u32[]{:S(2)}) copy-start(f32[1280]{0:T(1024)} %param.30) | copy-start | bytes 15364
  77.5 185.9 %all-reduce.13.cloned.1.call-start = ((), (), s32[]{:S(2)}) async-start(), calls=%async_computation.2 | async-start | bytes 2048000 | tf_op jit(solution)/shard_map/psum | solution.py:1120
  78.3 73.9 %copy-start.16 = (s32[1,128]{1,0:T(1,128)S(1)}, s32[1,128]{1,0:T(1,128)}, u32[]{:S(2)}) copy-start(s32[1,128]{1,0:T(1,128)} %param.33) | copy-start | bytes 1540
  178.0 166.1 %all-reduce.11.cloned.1.call-start = ((), (), s32[]{:S(2)}) async-start(), calls=%async_computation.1 | async-start | bytes 1024000 | tf_op jit(solution)/shard_map/psum | solution.py:1145
  281.0 3.8 copy-start.17
  281.0 4.3 %copy-start.15 = (f32[8,160]{1,0:T(8,128)S(1)}, f32[8,160]{1,0:T(8,128)}, u32[]{:S(2)}) copy-start(f32[8,160]{1,0:T(8,128)} %get-tuple-element.101) | copy-start | bytes 15364
  281.1 4.4 %copy-start.13 = (f32[6,160]{1,0:T(8,128)S(1)}, f32[6,160]{1,0:T(8,128)}, u32[]{:S(2)}) copy-start(f32[6,160]{1,0:T(8,128)} %get-tuple-element.100) | copy-start | bytes 11524
  281.1 4.5 %copy-start.12 = (f32[4,1280]{1,0:T(4,128)S(1)}, f32[4,1280]{1,0:T(4,128)}, u32[]{:S(2)}) copy-start(f32[4,1280]{1,0:T(4,128)} %get-tuple-element.99) | copy-start | bytes 61444
  349.8 30.7 %copy-start.5 = (f32[196,1280]{1,0:T(8,128)S(1)}, f32[196,1280]{1,0:T(8,128)}, u32[]{:S(2)}) copy-start(f32[196,1280]{1,0:T(8,128)} %get-tuple-element.97) | copy-start | bytes 3010564
  378.0 7.1 %copy-start.10 = (f32[8,25600]{1,0:T(8,128)S(1)}, f32[8,25600]{1,0:T(8,128)}, u32[]{:S(2)}) copy-start(f32[8,25600]{1,0:T(8,128)} %get-tuple-element.106) | copy-start | bytes 2457604
  380.5 5.5 %copy-start.3 = (f32[16,25600]{1,0:T(8,128)S(1)}, f32[16,25600]{1,0:T(8,128)}, u32[]{:S(2)}) copy-start(f32[16,25600]{1,0:T(8,128)} %get-tuple-element.107) | copy-start | bytes 4915204
  386.0 1.7 copy-start.9
  386.0 2.6 copy-start.2
  388.6 1.3 copy-start.11
  388.6 2.0 copy-start.6
  389.8 1.7 copy-start.8
  390.6 1.8 copy-start.7
  391.5 1.8 copy-start.1
  393.3 2.0 copy-start
Sparse Core Ops, SparseCore 0:
  77.7 33.4 all-reduce.8
  178.1 36.3 all-reduce.12
  284.2 34.8 all-reduce.10

commit v8 on v7

--- a/solution.py
+++ b/solution.py
@@ -477,7 +477,7 @@
         return pltpu.make_async_remote_copy(
             src_ref=wire.at[pl.ds(piece * k, piece)] if own else place,
             dst_ref=place,
-            send_sem=send_sem.at[way, origin // 2, k],
+            send_sem=send_sem.at[way, origin, k],
             recv_sem=recv_sem.at[origin, k],
             device_id={"dp": target},
             device_id_type=MESH_ID,
@@ -490,6 +490,8 @@
     keep = pltpu.make_async_copy(wire, out.at[pl.ds(me * count, count)], own_sem)
     keep.start()
     slots = 1 + 3 * pieces
+    split = (pieces + 1) // 2
+    lone, high = 1 - x, 7 - x
 
     def work(slot):
         for i, unit in enumerate(units):
@@ -497,32 +499,51 @@
                 unit()
 
     work(0)
-    for d in range(1, 4):
+    for d in range(1, 5):
         for k in range(pieces):
             def from_below():
                 origin = me - 2 * d
                 copy(1, up, origin, k).wait_recv()
-                copy(0, side, origin, k).start()
+                pl.when((z > d) | (k < split))(lambda: copy(0, side, origin, k).start())
                 pl.when(z < 3)(lambda: copy(1, up, origin, k).start())
 
             def from_above():
                 origin = me + 2 * d
                 copy(2, down, origin, k).wait_recv()
-                copy(0, side, origin, k).start()
+                pl.when((z + d < 3) | (k < split))(lambda: copy(0, side, origin, k).start())
                 pl.when(z > 0)(lambda: copy(2, down, origin, k).start())
 
-            pl.when(z >= d)(from_below)
-            pl.when(z + d <= 3)(from_above)
-            work(1 + (d - 1) * pieces + k)
+            def other_low():
+                copy(1, up, lone, k).wait_recv()
+                pl.when(z < 3)(lambda: copy(1, up, lone, k).start())
+
+            def other_high():
+                copy(2, down, high, k).wait_recv()
+                pl.when(z > 0)(lambda: copy(2, down, high, k).start())
+
+            if d < 4:
+                pl.when(z >= d)(from_below)
+                pl.when(z + d <= 3)(from_above)
+                work(1 + (d - 1) * pieces + k)
+            if k >= split:
+                pl.when(z == d - 1)(other_low)
+                pl.when(z == 4 - d)(other_high)
 
     keep.wait()
     for k in range(pieces):
         for line in range(4):
             origin = 2 * line + x
-            copy(0, side, origin + 1 - 2 * x, k).wait_recv()
-            copy(0, side, origin, k, False).wait_send()
+            far = line in (0, 3) and k >= split
+            if far:
+                pl.when(z == line)(lambda: copy(0, side, origin, k).wait_send())
+            else:
+                copy(0, side, origin + 1 - 2 * x, k).wait_recv()
+                copy(0, side, origin, k).wait_send()
             pl.when((line <= z) & (z < 3))(lambda: copy(1, up, origin, k).wait_send())
             pl.when((line >= z) & (z > 0))(lambda: copy(2, down, origin, k).wait_send())
+        if k >= split:
+            pl.when(z < 3)(lambda: copy(1, up, lone, k).wait_send())
+            pl.when(z > 0)(lambda: copy(2, down, high, k).wait_send())
 
 
 def gather(wire, ident, name, piece=5, make_units=None, args=(), outs=(), scratch=()):
@@ -534,7 +555,7 @@
         in_specs=[VM] * (1 + len(args)),
         out_specs=[pl.BlockSpec(memory_space=pl.ANY)] + [VM] * len(outs),
         scratch_shapes=[
-            pltpu.SemaphoreType.DMA((3, 4, count // piece)),
+            pltpu.SemaphoreType.DMA((3, 8, count // piece)),
             pltpu.SemaphoreType.DMA((8, count // piece)),
             pltpu.SemaphoreType.DMA,
         ] + [pltpu.VMEM(*item) for item in scratch],
@@ -551,7 +572,7 @@
 
 
 def scatter_steps(count, prepare, source, own_part, out, inbox, half,
-                  side_send, side_recv, line_send, line_recv, own, units, each=1):
+                  side_send, side_recv, line_send, line_recv, own, units, early=0, early_at=0):
     me = lax.axis_index("dp")
     z, x = me // 2, me % 2
     side = me + 1 - 2 * x
@@ -567,7 +588,7 @@
     pl.semaphore_wait(barrier, 4)
 
     def place(at):
-        j, k = lax.div(at, pieces), lax.rem(at, pieces)
+        j, k = lax.rem(at, 4), lax.div(at, 4)
         return j, k, line_at(j + 1)
 
     def to_side(at):
@@ -599,44 +620,50 @@
         send(at)
         return carry
 
+    def arrived(at, carry):
+        pl.when(lax.rem(at, 4) < 3)(lambda: to_line(at).wait_recv())
+        pl.when(lax.rem(at, 4) == 3)(lambda: keep(lax.div(at, 4)).wait())
+        return carry
+
+    def early_wait():
+        lax.fori_loop(0, 4 * early, arrived, 0)
+
     def step(at, carry):
-        _, k, line = place(at)
-        for i, unit in enumerate(units):
-            turn = i // 2 if i < 2 * each else i - each
-            pl.when(at == min(turn, steps - 1))(unit)
+        j, k, line = place(at)
+        if early:
+            pl.when(at == early_at)(early_wait)
+        for turn, unit in units:
+            pl.when(at == turn)(unit)
         to_side(at).wait_recv()
         pl.when(at + AHEAD < steps)(lambda: send(at + AHEAD))
         own_part(2 * line + x, line, k)
-        pl.when(at < 3 * pieces)(lambda: to_line(at).start())
-        pl.when(at >= 3 * pieces)(lambda: keep(k).start())
+        pl.when(j < 3)(lambda: to_line(at).start())
+        pl.when(j == 3)(lambda: keep(k).start())
         return carry
 
     def last(at, carry):
         to_side(at).wait_send()
-
-        def lines():
-            to_line(at).wait_send()
-            to_line(at).wait_recv()
-
-        pl.when(at < 3 * pieces)(lines)
-        pl.when(at >= 3 * pieces)(lambda: keep(place(at)[1]).wait())
+        pl.when(lax.rem(at, 4) < 3)(lambda: to_line(at).wait_send())
         return carry
 
     lax.fori_loop(0, AHEAD, first, 0)
     lax.fori_loop(0, steps, step, 0)
     lax.fori_loop(0, steps, last, 0)
-
-
-def scatter_call(body, count, tables, args, outs, scratch, ident, cost, name):
+    lax.fori_loop(4 * early, steps, arrived, 0)
+
+
+def scatter_call(body, count, tables, args, outs, scratch, ident, cost, name, given=0):
     shape = (4 * count, SIDE, 128)
+    result = (given or 4 * count, SIDE, 128)
     pieces = count // CHUNK
     return pl.pallas_call(
         body,
-        out_shape=[jax.ShapeDtypeStruct(shape, BF)] + [jax.ShapeDtypeStruct(*out) for out in outs],
+        out_shape=[jax.ShapeDtypeStruct(result, BF)] + [jax.ShapeDtypeStruct(*out) for out in outs],
         in_specs=[SM] * len(tables) + [VM] * len(args),
         out_specs=[pl.BlockSpec(memory_space=pl.ANY)] + [VM] * len(outs),
         scratch_shapes=[pltpu.VMEM(shape, BF)] * 2 + [pltpu.SemaphoreType.DMA((4, pieces))] * 4
-        + [pltpu.SemaphoreType.DMA((pieces,))] + [pltpu.VMEM(*item) for item in scratch],
+        + [pltpu.SemaphoreType.DMA((pieces,))]
+        + [pltpu.VMEM(*item) if item else pltpu.SemaphoreType.DMA((4,)) for item in scratch],
         compiler_params=pltpu.CompilerParams(
             collective_id=ident, has_side_effects=True, vmem_limit_bytes=LIMIT),
         cost_estimate=pl.CostEstimate(flops=0, bytes_accessed=cost, transcendentals=0),
@@ -674,18 +701,30 @@
     return prepare, source, own_part
 
 
-def scatter_mlp_body(left_at, right_at, sec, act, gh, go, left_m, right_m, left_a, right_a,
-                     out, sq_left_m, sq_right_m, sq_left_a, sq_right_a, inbox, half,
-                     side_send, side_recv, line_send, line_recv, own, lefts, rights, sent):
+def scatter_mlp_body(left_at, right_at, sec, act, gh, go, left_m, right_m, left_a, right_a, master, first, second,
+                     out, sq_left_m, sq_right_m, sq_left_a, sq_right_a,
+                     grad_out, new_out, copy_out, first_out, second_out, inbox, half,
+                     side_send, side_recv, line_send, line_recv, own, lefts, rights, sent, landed, moved,
+                     sq_left, sq_right, sq_grad, sq_work):
     lefts[0:8], lefts[8:16] = sec[...], act[...]
     rights[0:8], rights[8:16] = gh[...], go[...]
     units = []
-    for flat, square in ((left_m, sq_left_m), (right_m, sq_right_m), (left_a, sq_left_a), (right_a, sq_right_a)):
-        for g in range(square.shape[0]):
-            units.append(lambda f=flat, r=8 * g, sq=square, g=g: flat_to_square(
-                lambda at: f[r : r + 8, pl.ds(at, 128)], sq.at[g]))
+    for turn, (flat, r, square) in enumerate((
+            (left_m, 0, sq_left), (right_m, 0, sq_right), (left_m, 8, sq_left_m), (right_m, 8, sq_right_m),
+            (left_a, 0, sq_left_a), (right_a, 0, sq_right_a))):
+        units.append((turn, lambda f=flat, r=r, sq=square: flat_to_square(
+            lambda at: f[r : r + 8, pl.ds(at, 128)], sq.at[0])))
+    stages = soap_units(0, 0, landed, sq_left, sq_right, master, first, second,
+                        grad_out, new_out, copy_out, first_out, second_out, sq_grad, sq_work)
+    units += [(10 + i, stage) for i, stage in enumerate(stages)]
     scatter_steps(20, *tile_steps(20, left_at, right_at, lefts, rights, inbox, half, sent),
-                  out, inbox, half, side_send, side_recv, line_send, line_recv, own, units)
+                  landed, inbox, half, side_send, side_recv, line_send, line_recv, own, units, 2, 10)
+    moves = [pltpu.make_async_copy(landed.at[pl.ds(20 * p + 10, 10)], out.at[pl.ds(10 * p, 10)], moved.at[p])
+             for p in range(4)]
+    for move in moves:
+        move.start()
+    for move in moves:
+        move.wait()
 
 
 def scatter_attn_body(left_at, right_at, nb, att, gm, gb, wire, sq_left, sq_right, master, first, second,
@@ -693,12 +732,10 @@
                       side_send, side_recv, line_send, line_recv, own, lefts, rights, sent, sq_grad, sq_work):
     lefts[0:8], lefts[8:10] = nb[...], att[...]
     rights[0:6], rights[6:14] = gm[...], gb[...]
-    units = []
-    for g in range(2):
-        units += soap_units(g, g, wire, sq_left, sq_right, master, first, second,
-                            grad_out, new_out, copy_out, first_out, second_out, sq_grad, sq_work)
+    stages = soap_units(1, 0, wire, sq_left, sq_right, master, first, second,
+                        grad_out, new_out, copy_out, first_out, second_out, sq_grad, sq_work)
     scatter_steps(10, *tile_steps(10, left_at, right_at, lefts, rights, inbox, half, sent),
-                  out, inbox, half, side_send, side_recv, line_send, line_recv, own, units, 4)
+                  out, inbox, half, side_send, side_recv, line_send, line_recv, own, list(enumerate(stages)))
 
 
 def norm_parts(x):
@@ -932,7 +969,7 @@
 
 def soap_units(r, g, wire, sq_left, sq_right, master, first, second,
                grad_out, new_out, copy_out, first_out, second_out, sq_grad, sq_work):
-    rows = slice(8 * r, 8 * r + 8)
+    rows, to = slice(8 * r, 8 * r + 8), slice(0, 8)
     count = wire.shape[0] // 4
     left, right = sq_left.at[g], sq_right.at[g]
 
@@ -942,13 +979,13 @@
 
     def load():
         for half in range(2):
-            last = total(5 * (2 * r + half) + 4)
+            last = total(5 * half + 4)
             for q in range(4):
-                sq_grad[0, 4 * half + q] = total(5 * (2 * r + half) + q)
+                sq_grad[0, 4 * half + q] = total(5 * half + q)
                 sq_grad[1, 4 * half + q] = last if q == 0 else pltpu.roll(last, 128 - 32 * q, 1)
 
         def write(at, value):
-            grad_out[rows, pl.ds(at, 128)] = value
+            grad_out[to, pl.ds(at, 128)] = value
 
         square_to_flat(sq_grad, write)
 
@@ -961,9 +998,9 @@
         cols = pl.ds(at, 128)
         f = beta_one * first[rows, cols] + (1.0 - beta_one) * rotated
         s = beta_two * second[rows, cols] + (1.0 - beta_two) * rotated * rotated
-        first_out[rows, cols] = f
-        second_out[rows, cols] = s
-        new_out[rows, cols] = f / (jnp.sqrt(s) + adam_eps)
+        first_out[to, cols] = f
+        second_out[to, cols] = s
+        new_out[to, cols] = f / (jnp.sqrt(s) + adam_eps)
 
     def turn_back(t, carry):
         half = split_dot(dot, square_tile(left, t), square_tile(sq_work, t))
@@ -973,8 +1010,8 @@
     def finish(at, update):
         cols = pl.ds(at, 128)
         value = master[rows, cols] - learn_rate * update
-        new_out[rows, cols] = value
-        copy_out[rows, cols] = value.astype(BF)
+        new_out[to, cols] = value
+        copy_out[to, cols] = value.astype(BF)
 
     def loop(body):
         lax.fori_loop(0, 8, body, 0)
@@ -983,7 +1020,7 @@
         load,
         lambda: loop(rotate),
         lambda: square_to_flat(sq_work, moments),
-        lambda: flat_to_square(lambda at: new_out[rows, pl.ds(at, 128)], sq_work),
+        lambda: flat_to_square(lambda at: new_out[to, pl.ds(at, 128)], sq_work),
         lambda: loop(turn_back),
         lambda: square_to_flat(sq_work, finish),
     ]
@@ -1120,11 +1157,18 @@
     second_sum = lax.psum(part_second, "mp")
     down_sum = lax.psum(part_down, "mp")
 
-    sum_m, sq_left_m, sq_right_m, sq_left_a, sq_right_a = scatter_call(
+    def soap_outs():
+        shape = (8, SIDE * SIDE)
+        return [(shape, F32), (shape, F32), (shape, BF), (shape, F32), (shape, F32)]
+
+    square = ((1, 2, 8, SIDE, 128), F32)
+    sum_m, sq_left_m, sq_right_m, sq_left_a, sq_right_a, *upper = scatter_call(
         scatter_mlp_body, 20, (xm, ym),
-        (sec_blocks, act_blocks, gh, go, mlp_left[0], mlp_right[0], attn_left[0], attn_right[0]),
-        [((2, 2, 8, SIDE, 128), F32)] * 2 + [((1, 2, 8, SIDE, 128), F32)] * 2,
-        [((16, ROWS, SIDE), BF)] * 2 + [((80, SIDE, 128), BF)], 2, 250_000_000, "scatter_mlp")
+        (sec_blocks, act_blocks, gh, go, mlp_left[0], mlp_right[0], attn_left[0], attn_right[0],
+         mlp_master[0], mlp_first[0], mlp_second[0]),
+        [square] * 4 + soap_outs(),
+        [((16, ROWS, SIDE), BF)] * 2 + [((80, SIDE, 128), BF)] * 2 + [None] + [square] * 2 + [(square[0][1:], F32)] * 2,
+        2, 250_000_000, "scatter_mlp", 40)
     second_sum, down_sum, sum_m = lax.optimization_barrier((second_sum, down_sum, sum_m))
 
     block_out, grad_middle, part_normed, rel_part, gm, gb, nb, sums_two, qkv_sums = call(
@@ -1144,12 +1188,9 @@
     rel_flat = jnp.pad(rel_fold.reshape(-1).astype(BF), (0, rel_rows * width - rel_size)).reshape(rel_rows, width)
     both_sum = lax.psum(jnp.concatenate([part_normed, rel_flat], axis=0), "mp")
 
-    def soap_outs(shape):
-        return [(shape, F32), (shape, F32), (shape, BF), (shape, F32), (shape, F32)]
-
-    sum_a, mg, mn, mc, mf, ms = scatter_call(
+    sum_a, *lower = scatter_call(
         scatter_attn_body, 10, (xa, ya), (nb, att, gm, gb, sum_m, sq_left_m, sq_right_m, mlp_master[0], mlp_first[0], mlp_second[0]),
-        soap_outs(mlp_master.shape[1:]),
+        soap_outs(),
         [((10, ROWS, SIDE), BF), ((14, ROWS, SIDE), BF), ((40, SIDE, 128), BF)] + [((2, 8, SIDE, 128), F32)] * 2, 4, 150_000_000, "scatter_attn")
     both_sum, sum_a = lax.optimization_barrier((both_sum, sum_a))
     normed_sum, rel_sum = both_sum[:t], both_sum[t:].reshape(-1)[:rel_size].astype(F32)
@@ -1160,10 +1201,11 @@
     edges = np.cumsum([0] + [v.shape[0] for v in small])
     lines = -(-int(edges[-1]) // 1024) * 8
     small = jnp.pad(jnp.concatenate(small), (0, lines * 128 - int(edges[-1]))).reshape(1, lines, 128)
+    mg, mn, mc, mf, ms = [jnp.concatenate(pair, axis=0) for pair in zip(upper, lower)]
     gathered, ag, an, ac, af, as_ = gather(
         small, 3, "gather_sums", 1, functools.partial(soap_units, 0, 0),
         (sum_a, sq_left_a, sq_right_a, attn_master[0], attn_first[0], attn_second[0]),
-        soap_outs(attn_master.shape[1:]), [((2, 8, SIDE, 128), F32)] * 2)
+        soap_outs(), [((2, 8, SIDE, 128), F32)] * 2)
     total = jnp.sum(gathered, axis=0).reshape(-1)
     one, two, qkv_grad, up_grad, rel_grad = [total[edges[i]:edges[i + 1]] for i in range(5)]
     one, two = one.reshape(2, width), two.reshape(4, width)

time: 404 us -> 383 us (0.948)
  Pallas kernels: 356 us -> 337 us
  local copies, waits for them, and re-layouts: 22.8 us -> 15.8 us
  other arithmetic: 10 us -> 15 us
    pallas_call x3, Pallas kernels: 145 us -> 132 us  [gather(): pl.pallas_call(functools.partial(gather_body, piece, len(args), len(outs)...]
    unnamed x50 -> x53, local copies, waits for them, and re-layouts: 14.8 us -> 7.78 us
    broadcast_in_dim x0 -> x3, other arithmetic: none -> 6.32 us  [fast_local(): value[None]]
    pallas_call x2, Pallas kernels: 143 us -> 138 us  [scatter_call(): pl.pallas_call(body, out_shape=[jax.ShapeDtypeStruct(result, BF)] + [jax....]
  transfers between devices with their start and end apart: 3 -> 3, of which waited for: 0 -> 0; matrix products, arithmetic and copies ran while one was open for 1% -> 3% of each run, Pallas kernels for 54% -> 53%
where the time goes in v8:
time: 383 us; the launch traced here: 382 us
  Pallas kernels  337 us (88%)
  local copies, waits for them, and re-layouts  15.8 us (4%)
  other arithmetic  15 us (4%)
  between operations  14.1 us (4%)
    pallas_call x2, Pallas kernels, scatter_call(): pl.pallas_call(body, out_shape=[jax.ShapeDtypeStruct(result, BF)] + [jax....  138 us
    pallas_call x3, Pallas kernels, gather(): pl.pallas_call(functools.partial(gather_body, piece, len(args), len(outs)...  132 us
    pallas_call x5, Pallas kernels, call(): pl.pallas_call(body, out_shape=[jax.ShapeDtypeStruct(shape, kind) for sha...  67.4 us
    unnamed x53, local copies, waits for them, and re-layouts  7.78 us
  transfers between devices with their start and end apart: 3, of which 0 were waited for; matrix products, arithmetic and copies ran while one was open for 3% of the time, Pallas kernels for 53%

profile of v8, /device:TPU:0, one launch (start us, length us, event | category | flops | bytes accessed | tf_op | source)
XLA Modules:
  0.0 382.2 jit_solution(17961559621568652315)
XLA Ops:
  7.3 0.7 copy.62
  8.4 3.9 %pack.1.wire = bf16[10,160,128]{2,1,0:T(8,128)(2,1)} custom-call(f32[8,25600]{1,0:T(8,128)} %bitcast.94), custom_call_target="tpu_custom_call" | custom-call | tf_op jit(solution)/shard_map/pack/pallas_call | solution.py:1087
  12.5 0.8 copy.69.live
  13.9 0.7 reshape.100.qkv_bias
  14.5 39.0 %gather_attn.1 = (bf16[80,160,128]{2,1,0:T(8,128)(2,1)}, bf16[20,160,128]{2,1,0:T(8,128)(2,1)}) custom-call(bf16[10,160,128]{2,1,0:T(8,128)(2,1)} %pack.1.wire, f32[16,25600]{1,0:T(8,128)} %bitcast.83), custom_call_target="tpu_custom_call" | custom-call | bytes 120000000 | tf_op jit(solution)/shard_map/gather_attn/pallas_call | solution.py:551
  53.5 0.6 subtract_convert_fusion.rel_lo
  54.1 17.3 %attn_fwd.1 = (bf16[196,1280]{1,0:T(8,128)(2,1)}, bf16[208,1280]{1,0:T(8,128)(2,1)}, bf16[6,208,160]{2,1,0:T(8,128)(2,1)}, f32[4,208,208]{2,1,0:T(8,128)}, bf16[2,208,160]{2,1,0:T(8,128)(2,1)}) custom-call(s32[64]{0:T(128)} %select_reduce_fusion.1.order, bf16[196,1280]{1,0:T(8,128)(2,1)} %bitcast.86, f32[208,1]{1,0:T(8,128)} %copy.69.live, f32[2,1280]{1,0:T(2,128)} %gains.7, ...), custom_call_target="tpu_custom_call" | custom-call | tf_op jit(solution)/shard_map/attn_fwd/pallas_call | solution.py:1087
  71.6 65.5 %gather_mlp.1.wire = bf16[160,160,128]{2,1,0:T(8,128)(2,1)} custom-call(bf16[20,160,128]{2,1,0:T(8,128)(2,1)} %get-tuple-element.76.wire), custom_call_target="tpu_custom_call" | custom-call | bytes 240000000 | tf_op jit(solution)/shard_map/gather_mlp/pallas_call | solution.py:551
  137.1 0.7 reshape.101.up_bias
  138.4 25.2 %mlp.1 = (bf16[196,1280]{1,0:T(8,128)(2,1)}, bf16[196,1280]{1,0:T(8,128)(2,1)}, bf16[8,208,160]{2,1,0:T(8,128)(2,1)}, bf16[8,208,160]{2,1,0:T(8,128)(2,1)}, bf16...) custom-call(s32[128]{0:T(128)} %select_reduce_fusion.order, bf16[196,1280]{1,0:T(8,128)(2,1)} %bitcast.87, ...), custom_call_target="tpu_custom_call" | custom-call | tf_op jit(solution)/shard_map/mlp/pallas_call | solution.py:1087
  163.8 0.8 copy.71.live
  165.7 0.8 reshape.107
  166.4 88.0 %scatter_mlp.1 = (bf16[40,160,128]{2,1,0:T(8,128)(2,1)}, f32[1,2,8,160,128]{4,3,2,1,0:T(8,128)}, f32[1,2,8,160,128]{4,3,2,1,0:T(8,128)}, f32[1,2,8,160,128]{4,3,...) custom-call(s32[128]{0:T(128)} %get-tuple-element.211.left_at, ...), custom_call_target="tpu_custom_call" | custom-call | bytes 250000000 | tf_op jit(solution)/shard_map/scatter_mlp/pallas_call | solution.py:659
  254.4 17.6 %mid_back.1 = (bf16[196,1280]{1,0:T(8,128)(2,1)}, f32[196,1280]{1,0:T(8,128)}, bf16[196,1280]{1,0:T(8,128)(2,1)}, f32[128,160]{1,0:T(8,128)}, bf16[6,208,160]{2,...) custom-call(s32[64]{0:T(128)} %select_reduce_fusion.1.order, ...), custom_call_target="tpu_custom_call" | custom-call | tf_op jit(solution)/shard_map/mid_back/pallas_call | solution.py:1087
  272.0 0.9 slice_add_fusion
  273.1 1.9 pad_maximum_fusion
  275.0 49.8 %scatter_attn.1 = (bf16[40,160,128]{2,1,0:T(8,128)(2,1)}, f32[8,25600]{1,0:T(8,128)}, f32[8,25600]{1,0:T(8,128)}, bf16[8,25600]{1,0:T(8,128)(2,1)}, f32[8,25600]{1,0:T(8,128)}, /*index=5*/f32[8,25600]{1,0:T(8,128)}) custom-call(s32[64]{0:T(128)} %get-tuple-element.209.left_at, s32[64]{0:T(128)} %get-tuple-element.208.right_at, ...), custom_call_target="tpu_custom_call" | custom-call | bytes 150000000 | tf_op jit(solution)/shard_map/scatter_attn/pallas_call | solution.py:659
  324.9 3.5 maximum_bitcast_fusion.2
  328.4 1.9 maximum_bitcast_fusion
  330.3 0.9 maximum_bitcast_fusion.4
  331.3 0.7 slice.88
  332.1 3.4 token_back.1
  335.5 0.7 reshape.104
  336.9 27.3 %gather_sums.1 = (f32[8,112,128]{2,1,0:T(8,128)}, f32[8,25600]{1,0:T(8,128)}, f32[8,25600]{1,0:T(8,128)}, bf16[8,25600]{1,0:T(8,128)(2,1)}, f32[8,25600]{1,0:T(8,128)}, /*index=5*/f32[8,25600]{1,0:T(8,128)}) custom-call(f32[1,112,128]{2,1,0:T(8,128)} %pad_bitcast_fusion.wire, bf16[40,160,128]{2,1,0:T(8,128)(2,1)} %get-tuple-element.107.refs_0_, ...), custom_call_target="tpu_custom_call" | custom-call | bytes 12000000 | tf_op jit(solution)/shard_map/gather_sums/pallas_call | solution.py:551
  364.3 1.1 reduce_sum.29
  365.5 0.7 slice.116
  367.5 2.0 copy.72
  371.4 0.9 copy.95
  372.3 0.9 copy.96
  373.2 0.8 copy.97
  373.9 0.9 copy.98
  374.8 0.9 copy.99
  (87 shorter events, 7.5 us)
Async XLA Ops:
  7.2 5.2 %copy-start.19 = (s32[1,196]{1,0:T(1,128)S(1)}, s32[1,196]{1,0:T(1,128)}, u32[]{:S(2)}) copy-start(s32[1,196]{1,0:T(1,128)} %param.24) | copy-start | bytes 2356
  7.2 6.1 %copy-start.21 = (s32[1,64]{1,0:T(1,128)S(1)}, s32[1,64]{1,0:T(1,128)}, u32[]{:S(2)}) copy-start(s32[1,64]{1,0:T(1,128)} %param.32) | copy-start | bytes 772
  7.2 6.6 %copy-start.18 = (f32[960]{0:T(1024)S(1)}, f32[960]{0:T(1024)}, u32[]{:S(2)}) copy-start(f32[960]{0:T(1024)} %param.29) | copy-start | bytes 11524
  7.2 131.1 %all-reduce.9.cloned.1.call-start = ((), (), s32[]{:S(2)}) async-start(), calls=%async_computation | async-start | bytes 1024000 | tf_op jit(solution)/shard_map/psum | solution.py:1148
  12.4 41.7 %copy-start = (bf16[128,160]{1,0:T(8,128)(2,1)}, bf16[128,160]{1,0:T(8,128)(2,1)S(1)}, u32[]{:S(2)}) copy-start(bf16[128,160]{1,0:T(8,128)(2,1)S(1)} %copy.67.rel_hi) | copy-start | bytes 122884
  71.5 183.0 %all-reduce.13.cloned.1.call-start = ((), (), s32[]{:S(2)}) async-start(), calls=%async_computation.2 | async-start | bytes 2048000 | tf_op jit(solution)/shard_map/psum | solution.py:1157
  71.5 65.5 %copy-start.17 = (f32[1280]{0:T(1024)S(1)}, f32[1280]{0:T(1024)}, u32[]{:S(2)}) copy-start(f32[1280]{0:T(1024)} %param.30) | copy-start | bytes 15364
  71.5 66.2 %copy-start.20 = (s32[1,128]{1,0:T(1,128)S(1)}, s32[1,128]{1,0:T(1,128)}, u32[]{:S(2)}) copy-start(s32[1,128]{1,0:T(1,128)} %param.33) | copy-start | bytes 1540
  163.6 167.7 %all-reduce.11.cloned.1.call-start = ((), (), s32[]{:S(2)}) async-start(), calls=%async_computation.1 | async-start | bytes 1024000 | tf_op jit(solution)/shard_map/psum | solution.py:1189
  275.0 49.8 %copy-start.4 = (f32[8,25600]{1,0:T(8,128)S(1)}, f32[8,25600]{1,0:T(8,128)}, u32[]{:S(2)}) copy-start(f32[8,25600]{1,0:T(8,128)} %get-tuple-element.122) | copy-start | bytes 2457604
  275.0 49.8 %copy-start.5 = (f32[8,25600]{1,0:T(8,128)S(1)}, f32[8,25600]{1,0:T(8,128)}, u32[]{:S(2)}) copy-start(f32[8,25600]{1,0:T(8,128)} %get-tuple-element.124) | copy-start | bytes 2457604
  324.8 3.5 copy-start.2
  324.8 3.5 copy-start.3
  324.8 3.5 copy-start.6
  324.8 3.5 copy-start.7
  328.3 1.9 copy-start.12
  328.3 1.9 copy-start.14
  330.3 1.0 copy-start.15
  330.3 1.0 copy-start.16
  336.9 30.6 %copy-start.1 = (f32[196,1280]{1,0:T(8,128)S(1)}, f32[196,1280]{1,0:T(8,128)}, u32[]{:S(2)}) copy-start(f32[196,1280]{1,0:T(8,128)} %get-tuple-element.102) | copy-start | bytes 3010564
  364.3 7.1 %copy-start.11 = (f32[8,25600]{1,0:T(8,128)S(1)}, f32[8,25600]{1,0:T(8,128)}, u32[]{:S(2)}) copy-start(f32[8,25600]{1,0:T(8,128)} %get-tuple-element.111) | copy-start | bytes 2457604
  367.5 4.8 %copy-start.10 = (f32[8,25600]{1,0:T(8,128)S(1)}, f32[8,25600]{1,0:T(8,128)}, u32[]{:S(2)}) copy-start(f32[8,25600]{1,0:T(8,128)} %get-tuple-element.114) | copy-start | bytes 2457604
  371.4 1.8 copy-start.13
  371.4 2.5 copy-start.9
  372.3 2.5 copy-start.8
Sparse Core Ops, SparseCore 0:
  71.6 33.3 all-reduce.8
  163.7 36.3 all-reduce.12
  275.1 34.2 all-reduce.10

commit v9 on v8

--- a/solution.py
+++ b/solution.py
@@ -585,7 +585,6 @@
     barrier = pltpu.get_barrier_semaphore()
     for target in (side, 2 * line_at(1) + x, 2 * line_at(2) + x, 2 * line_at(3) + x):
         pl.semaphore_signal(barrier, inc=1, device_id={"dp": target}, device_id_type=MESH_ID)
-    pl.semaphore_wait(barrier, 4)
 
     def place(at):
         j, k = lax.rem(at, 4), lax.div(at, 4)
@@ -616,8 +615,13 @@
         prepare(2 * line + 1 - x, line, k)
         to_side(at).start()
 
+    def ready(at, carry):
+        _, k, line = place(at)
+        prepare(2 * line + 1 - x, line, k)
+        return carry
+
     def first(at, carry):
-        send(at)
+        to_side(at).start()
         return carry
 
     def arrived(at, carry):
@@ -646,6 +650,8 @@
         pl.when(lax.rem(at, 4) < 3)(lambda: to_line(at).wait_send())
         return carry
 
+    lax.fori_loop(0, AHEAD, ready, 0)
+    pl.semaphore_wait(barrier, 4)
     lax.fori_loop(0, AHEAD, first, 0)
     lax.fori_loop(0, steps, step, 0)
     lax.fori_loop(0, steps, last, 0)

time: 383 us -> 382 us (level)
  no operation moved by 1% of the time
where the time goes in v9:
time: 382 us; the launch traced here: 381 us
  Pallas kernels  336 us (88%)
  local copies, waits for them, and re-layouts  15.8 us (4%)
  other arithmetic  15 us (4%)
  between operations  14.1 us (4%)
    pallas_call x2, Pallas kernels, scatter_call(): pl.pallas_call(body, out_shape=[jax.ShapeDtypeStruct(result, BF)] + [jax....  137 us
    pallas_call x3, Pallas kernels, gather(): pl.pallas_call(functools.partial(gather_body, piece, len(args), len(outs)...  131 us
    pallas_call x5, Pallas kernels, call(): pl.pallas_call(body, out_shape=[jax.ShapeDtypeStruct(shape, kind) for sha...  67.4 us
    unnamed x53, local copies, waits for them, and re-layouts  7.78 us
  transfers between devices with their start and end apart: 3, of which 0 were waited for; matrix products, arithmetic and copies ran while one was open for 3% of the time, Pallas kernels for 53%

profile of v9, /device:TPU:0, one launch (start us, length us, event | category | flops | bytes accessed | tf_op | source)
XLA Modules:
  0.0 381.4 jit_solution(11658033794426185077)
XLA Ops:
  7.3 0.7 copy.62
  8.4 3.9 %pack.1.wire = bf16[10,160,128]{2,1,0:T(8,128)(2,1)} custom-call(f32[8,25600]{1,0:T(8,128)} %bitcast.94), custom_call_target="tpu_custom_call" | custom-call | tf_op jit(solution)/shard_map/pack/pallas_call | solution.py:1093
  12.5 0.8 copy.69.live
  13.9 0.7 reshape.100.qkv_bias
  14.5 39.0 %gather_attn.1 = (bf16[80,160,128]{2,1,0:T(8,128)(2,1)}, bf16[20,160,128]{2,1,0:T(8,128)(2,1)}) custom-call(bf16[10,160,128]{2,1,0:T(8,128)(2,1)} %pack.1.wire, f32[16,25600]{1,0:T(8,128)} %bitcast.83), custom_call_target="tpu_custom_call" | custom-call | bytes 120000000 | tf_op jit(solution)/shard_map/gather_attn/pallas_call | solution.py:551
  53.5 0.6 subtract_convert_fusion.rel_lo
  54.1 17.3 %attn_fwd.1 = (bf16[196,1280]{1,0:T(8,128)(2,1)}, bf16[208,1280]{1,0:T(8,128)(2,1)}, bf16[6,208,160]{2,1,0:T(8,128)(2,1)}, f32[4,208,208]{2,1,0:T(8,128)}, bf16[2,208,160]{2,1,0:T(8,128)(2,1)}) custom-call(s32[64]{0:T(128)} %select_reduce_fusion.1.order, bf16[196,1280]{1,0:T(8,128)(2,1)} %bitcast.86, f32[208,1]{1,0:T(8,128)} %copy.69.live, f32[2,1280]{1,0:T(2,128)} %gains.7, ...), custom_call_target="tpu_custom_call" | custom-call | tf_op jit(solution)/shard_map/attn_fwd/pallas_call | solution.py:1093
  71.6 65.5 %gather_mlp.1.wire = bf16[160,160,128]{2,1,0:T(8,128)(2,1)} custom-call(bf16[20,160,128]{2,1,0:T(8,128)(2,1)} %get-tuple-element.76.wire), custom_call_target="tpu_custom_call" | custom-call | bytes 240000000 | tf_op jit(solution)/shard_map/gather_mlp/pallas_call | solution.py:551
  137.1 0.7 reshape.101.up_bias
  138.4 25.2 %mlp.1 = (bf16[196,1280]{1,0:T(8,128)(2,1)}, bf16[196,1280]{1,0:T(8,128)(2,1)}, bf16[8,208,160]{2,1,0:T(8,128)(2,1)}, bf16[8,208,160]{2,1,0:T(8,128)(2,1)}, bf16...) custom-call(s32[128]{0:T(128)} %select_reduce_fusion.order, bf16[196,1280]{1,0:T(8,128)(2,1)} %bitcast.87, ...), custom_call_target="tpu_custom_call" | custom-call | tf_op jit(solution)/shard_map/mlp/pallas_call | solution.py:1093
  163.8 0.8 copy.71.live
  165.7 0.8 reshape.107
  166.4 87.6 %scatter_mlp.1 = (bf16[40,160,128]{2,1,0:T(8,128)(2,1)}, f32[1,2,8,160,128]{4,3,2,1,0:T(8,128)}, f32[1,2,8,160,128]{4,3,2,1,0:T(8,128)}, f32[1,2,8,160,128]{4,3,...) custom-call(s32[128]{0:T(128)} %get-tuple-element.211.left_at, ...), custom_call_target="tpu_custom_call" | custom-call | bytes 250000000 | tf_op jit(solution)/shard_map/scatter_mlp/pallas_call | solution.py:665
  254.1 17.6 %mid_back.1 = (bf16[196,1280]{1,0:T(8,128)(2,1)}, f32[196,1280]{1,0:T(8,128)}, bf16[196,1280]{1,0:T(8,128)(2,1)}, f32[128,160]{1,0:T(8,128)}, bf16[6,208,160]{2,...) custom-call(s32[64]{0:T(128)} %select_reduce_fusion.1.order, ...), custom_call_target="tpu_custom_call" | custom-call | tf_op jit(solution)/shard_map/mid_back/pallas_call | solution.py:1093
  271.6 0.9 slice_add_fusion
  272.7 1.9 pad_maximum_fusion
  274.6 49.7 %scatter_attn.1 = (bf16[40,160,128]{2,1,0:T(8,128)(2,1)}, f32[8,25600]{1,0:T(8,128)}, f32[8,25600]{1,0:T(8,128)}, bf16[8,25600]{1,0:T(8,128)(2,1)}, f32[8,25600]{1,0:T(8,128)}, /*index=5*/f32[8,25600]{1,0:T(8,128)}) custom-call(s32[64]{0:T(128)} %get-tuple-element.209.left_at, s32[64]{0:T(128)} %get-tuple-element.208.right_at, ...), custom_call_target="tpu_custom_call" | custom-call | bytes 150000000 | tf_op jit(solution)/shard_map/scatter_attn/pallas_call | solution.py:665
  324.4 3.5 maximum_bitcast_fusion.2
  327.9 1.9 maximum_bitcast_fusion
  329.8 0.9 maximum_bitcast_fusion.4
  330.9 0.7 slice.88
  331.6 3.4 token_back.1
  335.0 0.7 reshape.104
  336.5 27.0 %gather_sums.1 = (f32[8,112,128]{2,1,0:T(8,128)}, f32[8,25600]{1,0:T(8,128)}, f32[8,25600]{1,0:T(8,128)}, bf16[8,25600]{1,0:T(8,128)(2,1)}, f32[8,25600]{1,0:T(8,128)}, /*index=5*/f32[8,25600]{1,0:T(8,128)}) custom-call(f32[1,112,128]{2,1,0:T(8,128)} %pad_bitcast_fusion.wire, bf16[40,160,128]{2,1,0:T(8,128)(2,1)} %get-tuple-element.107.refs_0_, ...), custom_call_target="tpu_custom_call" | custom-call | bytes 12000000 | tf_op jit(solution)/shard_map/gather_sums/pallas_call | solution.py:551
  363.5 1.1 reduce_sum.29
  364.7 0.7 slice.116
  366.7 2.0 copy.72
  370.6 0.9 copy.95
  371.5 0.9 copy.96
  372.4 0.8 copy.97
  373.1 0.9 copy.98
  374.0 0.9 copy.99
  (87 shorter events, 7.5 us)
Async XLA Ops:
  7.2 5.2 %copy-start.19 = (s32[1,196]{1,0:T(1,128)S(1)}, s32[1,196]{1,0:T(1,128)}, u32[]{:S(2)}) copy-start(s32[1,196]{1,0:T(1,128)} %param.24) | copy-start | bytes 2356
  7.2 6.1 %copy-start.21 = (s32[1,64]{1,0:T(1,128)S(1)}, s32[1,64]{1,0:T(1,128)}, u32[]{:S(2)}) copy-start(s32[1,64]{1,0:T(1,128)} %param.32) | copy-start | bytes 772
  7.2 6.6 %copy-start.18 = (f32[960]{0:T(1024)S(1)}, f32[960]{0:T(1024)}, u32[]{:S(2)}) copy-start(f32[960]{0:T(1024)} %param.29) | copy-start | bytes 11524
  7.2 131.1 %all-reduce.9.cloned.1.call-start = ((), (), s32[]{:S(2)}) async-start(), calls=%async_computation | async-start | bytes 1024000 | tf_op jit(solution)/shard_map/psum | solution.py:1154
  12.4 41.7 %copy-start = (bf16[128,160]{1,0:T(8,128)(2,1)}, bf16[128,160]{1,0:T(8,128)(2,1)S(1)}, u32[]{:S(2)}) copy-start(bf16[128,160]{1,0:T(8,128)(2,1)S(1)} %copy.67.rel_hi) | copy-start | bytes 122884
  71.5 182.6 %all-reduce.13.cloned.1.call-start = ((), (), s32[]{:S(2)}) async-start(), calls=%async_computation.2 | async-start | bytes 2048000 | tf_op jit(solution)/shard_map/psum | solution.py:1163
  71.5 65.5 %copy-start.17 = (f32[1280]{0:T(1024)S(1)}, f32[1280]{0:T(1024)}, u32[]{:S(2)}) copy-start(f32[1280]{0:T(1024)} %param.30) | copy-start | bytes 15364
  71.5 66.2 %copy-start.20 = (s32[1,128]{1,0:T(1,128)S(1)}, s32[1,128]{1,0:T(1,128)}, u32[]{:S(2)}) copy-start(s32[1,128]{1,0:T(1,128)} %param.33) | copy-start | bytes 1540
  163.6 167.3 %all-reduce.11.cloned.1.call-start = ((), (), s32[]{:S(2)}) async-start(), calls=%async_computation.1 | async-start | bytes 1024000 | tf_op jit(solution)/shard_map/psum | solution.py:1195
  274.6 49.7 %copy-start.4 = (f32[8,25600]{1,0:T(8,128)S(1)}, f32[8,25600]{1,0:T(8,128)}, u32[]{:S(2)}) copy-start(f32[8,25600]{1,0:T(8,128)} %get-tuple-element.122) | copy-start | bytes 2457604
  274.6 49.7 %copy-start.5 = (f32[8,25600]{1,0:T(8,128)S(1)}, f32[8,25600]{1,0:T(8,128)}, u32[]{:S(2)}) copy-start(f32[8,25600]{1,0:T(8,128)} %get-tuple-element.124) | copy-start | bytes 2457604
  324.4 3.5 copy-start.2
  324.4 3.5 copy-start.3
  324.4 3.5 copy-start.6
  324.4 3.5 copy-start.7
  327.9 1.9 copy-start.12
  327.9 1.9 copy-start.14
  329.8 1.0 copy-start.15
  329.8 1.0 copy-start.16
  336.5 30.2 %copy-start.1 = (f32[196,1280]{1,0:T(8,128)S(1)}, f32[196,1280]{1,0:T(8,128)}, u32[]{:S(2)}) copy-start(f32[196,1280]{1,0:T(8,128)} %get-tuple-element.102) | copy-start | bytes 3010564
  363.5 7.1 %copy-start.11 = (f32[8,25600]{1,0:T(8,128)S(1)}, f32[8,25600]{1,0:T(8,128)}, u32[]{:S(2)}) copy-start(f32[8,25600]{1,0:T(8,128)} %get-tuple-element.111) | copy-start | bytes 2457604
  366.7 4.8 %copy-start.10 = (f32[8,25600]{1,0:T(8,128)S(1)}, f32[8,25600]{1,0:T(8,128)}, u32[]{:S(2)}) copy-start(f32[8,25600]{1,0:T(8,128)} %get-tuple-element.114) | copy-start | bytes 2457604
  370.6 1.8 copy-start.13
  370.6 2.5 copy-start.9
  371.5 2.5 copy-start.8
Sparse Core Ops, SparseCore 0:
  71.6 33.3 all-reduce.8
  163.7 36.3 all-reduce.12
  274.7 34.0 all-reduce.10
